TPU v7x, 32 devices: a whole 2x2x4 slice. The times are simulated.
32 devices in a mesh: shard: 2 (over x), replica: 16 (over z, y, core).
Axes of the slice: x: 2, y: 2, z: 4, core: 2. Of those that a mesh axis runs over, the one named last changes fastest.
Arguments:
- x_in: bfloat16 [32, 128, 2048], P(('shard', 'replica')), may hold values from -6 to 6
- cotangent: bfloat16 [32, 128, 2048], P(('shard', 'replica')), may hold values from -6 to 6
- w_query: bfloat16 [2048, 1024], P('shard'), may hold values from -0.088388348 to 0.088388348
- w_key: bfloat16 [2048, 1024], P('shard'), may hold values from -0.088388348 to 0.088388348
- w_value: bfloat16 [2048, 1024], P('shard'), may hold values from -0.125 to 0.125
- w_out: bfloat16 [1024, 2048], P('shard'), may hold values from -0.1875 to 0.1875
- w_gate: bfloat16 [2048, 4096], P('shard'), may hold values from -0.125 to 0.125
- w_up: bfloat16 [2048, 4096], P('shard'), may hold values from -0.125 to 0.125
- w_down: bfloat16 [4096, 2048], P('shard'), may hold values from -0.09375 to 0.09375
- gain_query: bfloat16 [1024], P('shard'), may hold values from 0.5 to 5
- gain_key: bfloat16 [1024], P('shard'), may hold values from 0.5 to 5
- gain_attn: bfloat16 [2048], P('shard'), may hold values from 0.5 to 1.5
- gain_mlp: bfloat16 [2048], P('shard'), may hold values from 0.5 to 1.5
Outputs:
- output: bfloat16 [32, 128, 2048], P(('shard', 'replica'))
- grad_input: float32 [32, 128, 2048], P(('shard', 'replica'))
- grad_w_query: float32 [2048, 1024], P(('shard', 'replica'))
- grad_w_key: float32 [2048, 1024], P(('shard', 'replica'))
- grad_w_value: float32 [2048, 1024], P(('shard', 'replica'))
- grad_w_out: float32 [1024, 2048], P(('shard', 'replica'))
- grad_w_gate: float32 [2048, 4096], P(('shard', 'replica'))
- grad_w_up: float32 [2048, 4096], P(('shard', 'replica'))
- grad_w_down: float32 [4096, 2048], P(('shard', 'replica'))
- grad_gain_query: float32 [1024], P(('shard', 'replica'))
- grad_gain_key: float32 [1024], P(('shard', 'replica'))
- grad_gain_attn: float32 [2048], P(('shard', 'replica'))
- grad_gain_mlp: float32 [2048], P(('shard', 'replica'))
All inputs are finite; a program needn't handle non-finite values.
Results may differ from a plain program's by a relative error of at most 0.018.
Values may be sent and summed in bfloat16 or wider, within the bound.
A program may use at most 512 MiB of HBM per device.

v0:
```python
import math

import jax
import jax.numpy as jnp
from jax import lax
from jax.sharding import PartitionSpec as P

HD = 128


eps_norm = 1e-06
rope_theta = 500000.0


def rope_tables(length, half):
    position = jnp.arange(length).astype(jnp.float32)[:, None]
    exponent = jnp.arange(half).astype(jnp.float32) * (1.0 / half)
    angle = position * rope_theta ** (-exponent)
    return (jnp.cos(angle), jnp.sin(angle))


def rotate(field, wave_cos, wave_sin):
    half = field.shape[-1] // 2
    first_half = field[..., :half]
    second_half = field[..., half:]
    cos_part = wave_cos[None, :, None, :]
    sin_part = wave_sin[None, :, None, :]
    return jnp.concatenate(
        [
            first_half * cos_part - second_half * sin_part,
            second_half * cos_part + first_half * sin_part,
        ],
        axis=-1,
    )


def unrotate(field, wave_cos, wave_sin):
    half = field.shape[-1] // 2
    first_half = field[..., :half]
    second_half = field[..., half:]
    cos_part = wave_cos[None, :, None, :]
    sin_part = wave_sin[None, :, None, :]
    return jnp.concatenate(
        [
            first_half * cos_part + second_half * sin_part,
            second_half * cos_part - first_half * sin_part,
        ],
        axis=-1,
    )


def rms_scale(field):
    return lax.rsqrt(jnp.mean(field * field, axis=-1, keepdims=True) + eps_norm)


def norm_back(grad_out, field, scale, gain):
    weighted = grad_out * gain
    inner = jnp.mean(weighted * field, axis=-1, keepdims=True)
    grad_field = scale * weighted - field * scale**3 * inner
    grad_gain = jnp.sum(grad_out * field * scale, axis=0)
    return (grad_field, grad_gain)


def matmul(left, right):
    return jnp.dot(left, right, preferred_element_type=jnp.float32)


def attn_scores(query_rot, key_rot, causal):
    scores = jnp.einsum(
        "sqhd,skhd->shqk", query_rot, key_rot, preferred_element_type=jnp.float32
    ) / math.sqrt(HD)
    return jnp.where(causal, scores, -jnp.inf)


def body(
    x_in,
    cotangent,
    w_query,
    w_key,
    w_value,
    w_out,
    w_gate,
    w_up,
    w_down,
    gain_query,
    gain_key,
    gain_attn,
    gain_mlp,
):
    attn_set = (
        lax.all_gather(w_query, "shard", axis=0, tiled=True),
        lax.all_gather(w_key, "shard", axis=0, tiled=True),
        lax.all_gather(w_value, "shard", axis=0, tiled=True),
        lax.all_gather(w_out, "shard", axis=0, tiled=True),
        lax.all_gather(gain_query, "shard", axis=0, tiled=True),
        lax.all_gather(gain_key, "shard", axis=0, tiled=True),
        lax.all_gather(gain_attn, "shard", axis=0, tiled=True),
    )
    mlp_set = (
        lax.all_gather(w_gate, "shard", axis=0, tiled=True),
        lax.all_gather(w_up, "shard", axis=0, tiled=True),
        lax.all_gather(w_down, "shard", axis=0, tiled=True),
        lax.all_gather(gain_mlp, "shard", axis=0, tiled=True),
    )
    seq_count, length, model_width = x_in.shape
    att_width = attn_set[0].shape[1]
    head_count = att_width // HD
    four_shape = (seq_count, length, head_count, HD)
    token_rows = x_in.reshape(seq_count * length, model_width)
    wave_cos, wave_sin = rope_tables(length, HD // 2)
    causal = jnp.arange(length)[:, None] >= jnp.arange(length)[None, :]
    query_proj = matmul(token_rows, attn_set[0])
    query_scale = rms_scale(query_proj)
    query_normed = query_proj * query_scale * attn_set[4].astype(jnp.float32)
    key_proj = matmul(token_rows, attn_set[1])
    key_scale = rms_scale(key_proj)
    key_normed = key_proj * key_scale * attn_set[5].astype(jnp.float32)
    value_four = matmul(token_rows, attn_set[2]).astype(jnp.bfloat16).reshape(four_shape)
    query_rot = rotate(query_normed.reshape(four_shape), wave_cos, wave_sin).astype(jnp.bfloat16)
    key_rot = rotate(key_normed.reshape(four_shape), wave_cos, wave_sin).astype(jnp.bfloat16)
    scores = attn_scores(query_rot, key_rot, causal)
    row_peak = jnp.max(scores, axis=-1, keepdims=True)
    log_total = row_peak + jnp.log(jnp.sum(jnp.exp(scores - row_peak), axis=-1, keepdims=True))
    probs_low = jnp.exp(scores - log_total).astype(jnp.bfloat16)
    attn_mixed = jnp.einsum(
        "shqk,skhd->sqhd", probs_low, value_four, preferred_element_type=jnp.float32
    )
    attn_mixed = attn_mixed.astype(jnp.bfloat16).reshape(-1, att_width)
    attn_proj = matmul(attn_mixed, attn_set[3])
    attn_scale = rms_scale(attn_proj)
    residual = token_rows.astype(jnp.float32) + attn_proj * attn_scale * attn_set[6].astype(
        jnp.float32
    )
    residual_low = residual.astype(jnp.bfloat16)
    gate_proj = matmul(residual_low, mlp_set[0])
    up_proj = matmul(residual_low, mlp_set[1])
    gate_sigmoid = jax.nn.sigmoid(gate_proj)
    gate_silu = gate_proj * gate_sigmoid
    hidden = (gate_silu * up_proj).astype(jnp.bfloat16)
    down_proj = matmul(hidden, mlp_set[2])
    down_scale = rms_scale(down_proj)
    output = residual + down_proj * down_scale * mlp_set[3].astype(jnp.float32)
    mlp_back = (
        lax.all_gather(w_gate, "shard", axis=0, tiled=True),
        lax.all_gather(w_up, "shard", axis=0, tiled=True),
        lax.all_gather(w_down, "shard", axis=0, tiled=True),
        lax.all_gather(gain_mlp, "shard", axis=0, tiled=True),
    )
    grad_output = cotangent.reshape(-1, model_width).astype(jnp.float32)
    grad_down, grad_gain_mlp = norm_back(
        grad_output, down_proj, down_scale, mlp_back[3].astype(jnp.float32)
    )
    grad_down = grad_down.astype(jnp.bfloat16)
    grad_w_down = matmul(hidden.T, grad_down)
    grad_hidden = matmul(grad_down, mlp_back[2].T)
    grad_gate = (
        grad_hidden * up_proj * gate_sigmoid * (1.0 + gate_proj * (1.0 - gate_sigmoid))
    ).astype(jnp.bfloat16)
    grad_up = (grad_hidden * gate_silu).astype(jnp.bfloat16)
    grad_w_gate = matmul(residual_low.T, grad_gate)
    grad_w_up = matmul(residual_low.T, grad_up)
    grad_residual = grad_output + matmul(grad_gate, mlp_back[0].T) + matmul(grad_up, mlp_back[1].T)
    mlp_grads = (grad_w_gate, grad_w_up, grad_w_down, grad_gain_mlp)
    mlp_half = (
        lax.psum_scatter(
            mlp_grads[0].astype(jnp.bfloat16), "shard", scatter_dimension=0, tiled=True
        ).astype(jnp.float32),
        lax.psum_scatter(
            mlp_grads[1].astype(jnp.bfloat16), "shard", scatter_dimension=0, tiled=True
        ).astype(jnp.float32),
        lax.psum_scatter(
            mlp_grads[2].astype(jnp.bfloat16), "shard", scatter_dimension=0, tiled=True
        ).astype(jnp.float32),
        lax.psum_scatter(
            mlp_grads[3].astype(jnp.bfloat16), "shard", scatter_dimension=0, tiled=True
        ).astype(jnp.float32),
    )
    mlp_owned = (
        lax.psum_scatter(mlp_half[0], "replica", scatter_dimension=0, tiled=True),
        lax.psum_scatter(mlp_half[1], "replica", scatter_dimension=0, tiled=True),
        lax.psum_scatter(mlp_half[2], "replica", scatter_dimension=0, tiled=True),
        lax.psum_scatter(mlp_half[3], "replica", scatter_dimension=0, tiled=True),
    )
    attn_back = (
        lax.all_gather(w_query, "shard", axis=0, tiled=True),
        lax.all_gather(w_key, "shard", axis=0, tiled=True),
        lax.all_gather(w_value, "shard", axis=0, tiled=True),
        lax.all_gather(w_out, "shard", axis=0, tiled=True),
        lax.all_gather(gain_query, "shard", axis=0, tiled=True),
        lax.all_gather(gain_key, "shard", axis=0, tiled=True),
        lax.all_gather(gain_attn, "shard", axis=0, tiled=True),
    )
    grad_attn, grad_gain_attn = norm_back(
        grad_residual, attn_proj, attn_scale, attn_back[6].astype(jnp.float32)
    )
    grad_attn = grad_attn.astype(jnp.bfloat16)
    grad_w_out = matmul(attn_mixed.T, grad_attn)
    grad_mixed = matmul(grad_attn, attn_back[3].T).astype(jnp.bfloat16).reshape(four_shape)
    probs_again = jnp.exp(attn_scores(query_rot, key_rot, causal) - log_total)
    grad_value = jnp.einsum(
        "shqk,sqhd->skhd",
        probs_again.astype(jnp.bfloat16),
        grad_mixed,
        preferred_element_type=jnp.float32,
    ).astype(jnp.bfloat16)
    grad_probs = jnp.einsum(
        "sqhd,skhd->shqk", grad_mixed, value_four, preferred_element_type=jnp.float32
    )
    grad_scores = probs_again * (
        grad_probs - jnp.sum(probs_again * grad_probs, axis=-1, keepdims=True)
    )
    grad_scores = (grad_scores / math.sqrt(HD)).astype(jnp.bfloat16)
    grad_qrot = jnp.einsum(
        "shqk,skhd->sqhd", grad_scores, key_rot, preferred_element_type=jnp.float32
    )
    grad_krot = jnp.einsum(
        "shqk,sqhd->skhd", grad_scores, query_rot, preferred_element_type=jnp.float32
    )
    grad_qnormed = unrotate(grad_qrot, wave_cos, wave_sin).reshape(-1, att_width)
    grad_knormed = unrotate(grad_krot, wave_cos, wave_sin).reshape(-1, att_width)
    grad_query, grad_gain_query = norm_back(
        grad_qnormed, query_proj, query_scale, attn_back[4].astype(jnp.float32)
    )
    grad_key, grad_gain_key = norm_back(
        grad_knormed, key_proj, key_scale, attn_back[5].astype(jnp.float32)
    )
    grad_query = grad_query.astype(jnp.bfloat16)
    grad_key = grad_key.astype(jnp.bfloat16)
    grad_value = grad_value.reshape(-1, att_width)
    grad_w_query = matmul(token_rows.T, grad_query)
    grad_w_key = matmul(token_rows.T, grad_key)
    grad_w_value = matmul(token_rows.T, grad_value)
    grad_input = (
        grad_residual
        + matmul(grad_query, attn_back[0].T)
        + matmul(grad_key, attn_back[1].T)
        + matmul(grad_value, attn_back[2].T)
    )
    attn_grads = (
        grad_w_query,
        grad_w_key,
        grad_w_value,
        grad_w_out,
        grad_gain_query,
        grad_gain_key,
        grad_gain_attn,
    )
    attn_half = (
        lax.psum_scatter(
            attn_grads[0].astype(jnp.bfloat16), "shard", scatter_dimension=0, tiled=True
        ).astype(jnp.float32),
        lax.psum_scatter(
            attn_grads[1].astype(jnp.bfloat16), "shard", scatter_dimension=0, tiled=True
        ).astype(jnp.float32),
        lax.psum_scatter(
            attn_grads[2].astype(jnp.bfloat16), "shard", scatter_dimension=0, tiled=True
        ).astype(jnp.float32),
        lax.psum_scatter(
            attn_grads[3].astype(jnp.bfloat16), "shard", scatter_dimension=0, tiled=True
        ).astype(jnp.float32),
        lax.psum_scatter(
            attn_grads[4].astype(jnp.bfloat16), "shard", scatter_dimension=0, tiled=True
        ).astype(jnp.float32),
        lax.psum_scatter(
            attn_grads[5].astype(jnp.bfloat16), "shard", scatter_dimension=0, tiled=True
        ).astype(jnp.float32),
        lax.psum_scatter(
            attn_grads[6].astype(jnp.bfloat16), "shard", scatter_dimension=0, tiled=True
        ).astype(jnp.float32),
    )
    attn_owned = (
        lax.psum_scatter(attn_half[0], "replica", scatter_dimension=0, tiled=True),
        lax.psum_scatter(attn_half[1], "replica", scatter_dimension=0, tiled=True),
        lax.psum_scatter(attn_half[2], "replica", scatter_dimension=0, tiled=True),
        lax.psum_scatter(attn_half[3], "replica", scatter_dimension=0, tiled=True),
        lax.psum_scatter(attn_half[4], "replica", scatter_dimension=0, tiled=True),
        lax.psum_scatter(attn_half[5], "replica", scatter_dimension=0, tiled=True),
        lax.psum_scatter(attn_half[6], "replica", scatter_dimension=0, tiled=True),
    )
    return (
        output.astype(jnp.bfloat16).reshape(x_in.shape),
        grad_input.reshape(x_in.shape),
        attn_owned[0],
        attn_owned[1],
        attn_owned[2],
        attn_owned[3],
        mlp_owned[0],
        mlp_owned[1],
        mlp_owned[2],
        attn_owned[4],
        attn_owned[5],
        attn_owned[6],
        mlp_owned[3],
    )


def solution(mesh):
    return jax.shard_map(
        body,
        mesh=mesh,
        in_specs=(
            P(("shard", "replica"), None, None),
            P(("shard", "replica"), None, None),
            P("shard", None),
            P("shard", None),
            P("shard", None),
            P("shard", None),
            P("shard", None),
            P("shard", None),
            P("shard", None),
            P("shard"),
            P("shard"),
            P("shard"),
            P("shard"),
        ),
        out_specs=(
            P(("shard", "replica"), None, None),
            P(("shard", "replica"), None, None),
            P(("shard", "replica"), None),
            P(("shard", "replica"), None),
            P(("shard", "replica"), None),
            P(("shard", "replica"), None),
            P(("shard", "replica"), None),
            P(("shard", "replica"), None),
            P(("shard", "replica"), None),
            P(("shard", "replica")),
            P(("shard", "replica")),
            P(("shard", "replica")),
            P(("shard", "replica")),
        ),
        check_vma=False,
    )
```

profile of v0, /device:TPU:0, one launch (start us, length us, event | category | flops | bytes accessed | tf_op | source)
XLA Modules:
  0.0 2560.4 jit_solution(11630051221962567769)
XLA Ops:
  31.1 37.9 %all-gather.14.cloned.1.call-done = bf16[2048,1024]{1,0:T(8,128)(2,1)} async-done(((bf16[1024,1024]{1,0:T(8,128)(2,1)}), bf16[2048,1024]{1,0:T(8,128)(2,1)}) %all-gather.14.cloned.1.call-update) | async-done | bytes 4194320 | tf_op jit(solution)/shard_map/all_gather | solution.py:92
  73.1 54.3 %all-gather.12.cloned.1.call-done = bf16[2048,1024]{1,0:T(8,128)(2,1)} async-done(((bf16[1024,1024]{1,0:T(8,128)(2,1)}), bf16[2048,1024]{1,0:T(8,128)(2,1)}) %all-gather.12.cloned.1.call-update) | async-done | bytes 4194320 | tf_op jit(solution)/shard_map/all_gather | solution.py:91
  133.5 52.2 %all-gather.10.cloned.1.call-done = bf16[2048,1024]{1,0:T(8,128)(2,1)} async-done(((bf16[1024,1024]{1,0:T(8,128)(2,1)}), bf16[2048,1024]{1,0:T(8,128)(2,1)}) %all-gather.10.cloned.1.call-update) | async-done | bytes 4194320 | tf_op jit(solution)/shard_map/all_gather | solution.py:93
  188.9 54.9 %all-gather.16.cloned.1.call-done = bf16[1024,2048]{1,0:T(8,128)(2,1)} async-done(((bf16[512,2048]{1,0:T(8,128)(2,1)}), bf16[1024,2048]{1,0:T(8,128)(2,1)}) %all-gather.16.cloned.1.call-update) | async-done | bytes 4194320 | tf_op jit(solution)/shard_map/all_gather | solution.py:94
  247.1 197.0 %all-gather.18.cloned.1.call-done = bf16[2048,4096]{1,0:T(8,128)(2,1)} async-done(((bf16[1024,4096]{1,0:T(8,128)(2,1)}), bf16[2048,4096]{1,0:T(8,128)(2,1)}) %all-gather.18.cloned.1.call-update) | async-done | bytes 16777232 | tf_op jit(solution)/shard_map/all_gather | solution.py:100
  444.1 9.4 fusion.64
  453.5 190.8 %all-gather.20.cloned.1.call-done = bf16[2048,4096]{1,0:T(8,128)(2,1)} async-done(((bf16[1024,4096]{1,0:T(8,128)(2,1)}), bf16[2048,4096]{1,0:T(8,128)(2,1)}) %all-gather.20.cloned.1.call-update) | async-done | bytes 16777232 | tf_op jit(solution)/shard_map/all_gather | solution.py:101
  644.4 11.3 multiply_convert_fusion.2
  655.6 189.2 %all-gather.22.cloned.1.call-done = bf16[4096,2048]{1,0:T(8,128)(2,1)} async-done(((bf16[2048,2048]{1,0:T(8,128)(2,1)}), bf16[4096,2048]{1,0:T(8,128)(2,1)}) %all-gather.22.cloned.1.call-update) | async-done | bytes 16777232 | tf_op jit(solution)/shard_map/all_gather | solution.py:102
  844.8 8.9 multiply_reduce_fusion.2
  854.7 14.4 multiply_convert_fusion
  869.1 12.7 convolution_add_fusion.4
  881.8 13.7 multiply_reduce_fusion
  930.7 8.5 convolution_convert_fusion
  940.5 8.1 convolution_convert_fusion.2
  949.8 8.1 convolution_convert_fusion.1
  963.8 52.5 %reduce-scatter.23.cloned.1.call-done = bf16[1024,1024]{0,1:T(8,128)(2,1)} async-done(((bf16[2048,1024]{0,1:T(8,128)(2,1)}), bf16[1024,1024]{0,1:T(8,128)(2,1)}) %reduce-scatter.23.cloned.1.call-update) | async-done | bytes 2097168 | tf_op jit(solution)/shard_map/reduce_scatter | solution.py:252
  1020.5 52.3 %reduce-scatter.27.cloned.1.call-done = bf16[512,2048]{1,0:T(8,128)(2,1)} async-done(((bf16[1024,2048]{1,0:T(8,128)(2,1)}), bf16[512,2048]{1,0:T(8,128)(2,1)}) %reduce-scatter.27.cloned.1.call-update) | async-done | bytes 2097168 | tf_op jit(solution)/shard_map/reduce_scatter | solution.py:258
  1077.0 52.5 %reduce-scatter.21.cloned.1.call-done = bf16[1024,1024]{0,1:T(8,128)(2,1)} async-done(((bf16[2048,1024]{0,1:T(8,128)(2,1)}), bf16[1024,1024]{0,1:T(8,128)(2,1)}) %reduce-scatter.21.cloned.1.call-update) | async-done | bytes 2097168 | tf_op jit(solution)/shard_map/reduce_scatter | solution.py:249
  1133.7 187.2 %reduce-scatter.39.cloned.1.call-done = bf16[2048,2048]{1,0:T(8,128)(2,1)} async-done(((bf16[4096,2048]{1,0:T(8,128)(2,1)}), bf16[2048,2048]{1,0:T(8,128)(2,1)}) %reduce-scatter.39.cloned.1.call-update) | async-done | bytes 8388624 | tf_op jit(solution)/shard_map/reduce_scatter | solution.py:171
  1320.9 11.8 convert_element_type.288
  1332.7 179.7 %reduce-scatter.31.cloned.1.call-done = bf16[1024,4096]{1,0:T(8,128)(2,1)} async-done(((bf16[2048,4096]{1,0:T(8,128)(2,1)}), bf16[1024,4096]{1,0:T(8,128)(2,1)}) %reduce-scatter.31.cloned.1.call-update) | async-done | bytes 8388624 | tf_op jit(solution)/shard_map/reduce_scatter | solution.py:165
  1512.4 11.9 convert_element_type.284
  1524.6 179.2 %reduce-scatter.35.cloned.1.call-done = bf16[1024,4096]{1,0:T(8,128)(2,1)} async-done(((bf16[2048,4096]{1,0:T(8,128)(2,1)}), bf16[1024,4096]{1,0:T(8,128)(2,1)}) %reduce-scatter.35.cloned.1.call-update) | async-done | bytes 8388624 | tf_op jit(solution)/shard_map/reduce_scatter | solution.py:168
  1703.8 11.6 convert_element_type.286
  1726.8 59.8 %all-reduce.8 = (f32[512]{0:T(512)S(1)}, f32[512]{0:T(512)S(1)}, f32[1024]{0:T(1024)S(1)}, f32[1024]{0:T(1024)S(1)}) all-reduce(f32[512]{0:T(512)S(1)} %dynamic-slice_convert_fusion.3, f32[512]{0:T(512)S(1)} %dynamic-slice_convert_fusion.2, ...), channel_id=17, replica_groups=mesh['shard'=2,'replica'=16] {'replica'}, use_global_device_ids=true, to_apply=%region_27.28.clone | all-reduce | flops 3072 | bytes 24576
  1797.7 59.8 %reduce-scatter.45.cloned.1.call-done = f32[64,1024]{1,0:T(8,128)} async-done(((f32[1024,1024]{1,0:T(8,128)}), f32[64,1024]{1,0:T(8,128)}) %reduce-scatter.45.cloned.1.call-update) | async-done | bytes 262160
  1857.6 76.2 %reduce-scatter.29.cloned.1.call-done = f32[32,2048]{1,0:T(8,128)} async-done(((f32[512,2048]{1,0:T(8,128)}), f32[32,2048]{1,0:T(8,128)}) %reduce-scatter.29.cloned.1.call-update) | async-done | bytes 262160 | tf_op jit(solution)/shard_map/reduce_scatter | solution.py:275
  1933.7 76.1 %reduce-scatter.43.cloned.1.call-done = f32[64,1024]{1,0:T(8,128)} async-done(((f32[1024,1024]{1,0:T(8,128)}), f32[64,1024]{1,0:T(8,128)}) %reduce-scatter.43.cloned.1.call-update) | async-done | bytes 262160
  2009.9 181.1 %reduce-scatter.41.cloned.1.call-done = f32[128,2048]{1,0:T(8,128)} async-done(((f32[2048,2048]{1,0:T(8,128)}), f32[128,2048]{1,0:T(8,128)}) %reduce-scatter.41.cloned.1.call-update) | async-done | bytes 1048592 | tf_op jit(solution)/shard_map/reduce_scatter | solution.py:181
  2191.0 181.0 %reduce-scatter.33.cloned.1.call-done = f32[64,4096]{1,0:T(8,128)} async-done(((f32[1024,4096]{1,0:T(8,128)}), f32[64,4096]{1,0:T(8,128)}) %reduce-scatter.33.cloned.1.call-update) | async-done | bytes 1048592 | tf_op jit(solution)/shard_map/reduce_scatter | solution.py:179
  2372.0 181.1 %reduce-scatter.37.cloned.1.call-done = f32[64,4096]{1,0:T(8,128)} async-done(((f32[1024,4096]{1,0:T(8,128)}), f32[64,4096]{1,0:T(8,128)}) %reduce-scatter.37.cloned.1.call-update) | async-done | bytes 1048592 | tf_op jit(solution)/shard_map/reduce_scatter | solution.py:180
  (224 shorter events, 117.0 us)
Async XLA Ops:
  7.2 61.9 %all-gather.14.cloned.1.call-start = ((), (), s32[]{:S(2)}) async-start(), calls=%async_computation.16 | async-start | bytes 6291456 | tf_op jit(solution)/shard_map/all_gather | solution.py:92
  7.9 119.5 %all-gather.12.cloned.1.call-start = ((), (), s32[]{:S(2)}) async-start(), calls=%async_computation.15 | async-start | bytes 6291456 | tf_op jit(solution)/shard_map/all_gather | solution.py:91
  8.7 177.0 %all-gather.10.cloned.1.call-start = ((), (), s32[]{:S(2)}) async-start(), calls=%async_computation.14 | async-start | bytes 6291456 | tf_op jit(solution)/shard_map/all_gather | solution.py:93
  9.4 234.5 %all-gather.16.cloned.1.call-start = ((), (), s32[]{:S(2)}) async-start(), calls=%async_computation.17 | async-start | bytes 6291456 | tf_op jit(solution)/shard_map/all_gather | solution.py:94
  10.0 434.1 %all-gather.18.cloned.1.call-start = ((), (), s32[]{:S(2)}) async-start(), calls=%async_computation.18 | async-start | bytes 25165824 | tf_op jit(solution)/shard_map/all_gather | solution.py:100
  10.6 633.8 %all-gather.20.cloned.1.call-start = ((), (), s32[]{:S(2)}) async-start(), calls=%async_computation.19 | async-start | bytes 25165824 | tf_op jit(solution)/shard_map/all_gather | solution.py:101
  11.2 57.9 %copy-start = (bf16[1,128,2048]{2,1,0:T(8,128)(2,1)S(1)}, bf16[1,128,2048]{2,1,0:T(8,128)(2,1)}, u32[]{:S(2)}) copy-start(bf16[1,128,2048]{2,1,0:T(8,128)(2,1)} %param.13) | copy-start | bytes 1572868
  11.2 833.6 %all-gather.22.cloned.1.call-start = ((), (), s32[]{:S(2)}) async-start(), calls=%async_computation.20 | async-start | bytes 25165824 | tf_op jit(solution)/shard_map/all_gather | solution.py:102
  11.9 947.6 %reduce-scatter.25.cloned.1.call-start = ((), (), s32[]{:S(2)}) async-start(), calls=%async_computation.23 | async-start | bytes 6291456 | tf_op jit(solution)/shard_map/reduce_scatter | solution.py:255
  72.6 57.7 %copy-start.36 = (f32[128]{0:T(128)}, f32[128]{0:T(128)S(1)}, u32[]{:S(2)}) copy-start(f32[128]{0:T(128)S(1)} %get-tuple-element.78) | copy-start | bytes 1540
  133.4 110.5 %copy-start.5 = (f32[8,128,128]{1,2,0:T(8,128)}, f32[8,128,128]{1,2,0:T(8,128)S(1)}, u32[]{:S(2)}) copy-start(f32[8,128,128]{1,2,0:T(8,128)S(1)} %get-tuple-element.90) | copy-start | bytes 1572868
  133.5 113.4 %copy-start.31 = (f32[8,128]{1,0:T(8,128)}, f32[8,128]{1,0:T(8,128)S(1)}, u32[]{:S(2)}) copy-start(f32[8,128]{1,0:T(8,128)S(1)} %log_add_fusion) | copy-start | bytes 12292
  188.6 55.2 %copy-start.24 = (bf16[16,8,8,128]{3,2,1,0:T(8,128)(2,1)}, bf16[16,8,8,128]{3,2,1,0:T(8,128)(2,1)S(1)}, u32[]{:S(2)}) copy-start(bf16[16,8,8,128]{3,2,1,0:T(8,128)(2,1)S(1)} %fusion.10) | copy-start | bytes 786436
  188.9 264.6 %copy-start.22 = (bf16[8,128,128]{2,1,0:T(8,128)(2,1)}, bf16[8,128,128]{2,1,0:T(8,128)(2,1)S(1)}, u32[]{:S(2)}) copy-start(bf16[8,128,128]{2,1,0:T(8,128)(2,1)S(1)} %convolution_convert_fusion.5) | copy-start | bytes 786436
  853.8 15.3 copy-start.46
  853.8 41.8 %copy-start.38 = (f32[128]{0:T(128)}, f32[128]{0:T(128)S(1)}, u32[]{:S(2)}) copy-start(f32[128]{0:T(128)S(1)} %get-tuple-element.84) | copy-start | bytes 1540
  905.0 111.2 %reduce-scatter.23.cloned.1.call-start = ((), (), s32[]{:S(2)}) async-start(), calls=%async_computation.22 | async-start | bytes 6291456 | tf_op jit(solution)/shard_map/reduce_scatter | solution.py:252
  919.4 153.4 %reduce-scatter.27.cloned.1.call-start = ((), (), s32[]{:S(2)}) async-start(), calls=%async_computation.24 | async-start | bytes 6291456 | tf_op jit(solution)/shard_map/reduce_scatter | solution.py:258
  922.8 206.8 %reduce-scatter.21.cloned.1.call-start = ((), (), s32[]{:S(2)}) async-start(), calls=%async_computation.21 | async-start | bytes 6291456 | tf_op jit(solution)/shard_map/reduce_scatter | solution.py:249
  929.7 391.2 %reduce-scatter.39.cloned.1.call-start = ((), (), s32[]{:S(2)}) async-start(), calls=%async_computation.30 | async-start | bytes 25165824 | tf_op jit(solution)/shard_map/reduce_scatter | solution.py:171
  939.3 573.1 %reduce-scatter.31.cloned.1.call-start = ((), (), s32[]{:S(2)}) async-start(), calls=%async_computation.26 | async-start | bytes 25165824 | tf_op jit(solution)/shard_map/reduce_scatter | solution.py:165
  948.6 755.1 %reduce-scatter.35.cloned.1.call-start = ((), (), s32[]{:S(2)}) async-start(), calls=%async_computation.28 | async-start | bytes 25165824 | tf_op jit(solution)/shard_map/reduce_scatter | solution.py:168
  958.0 839.8 %reduce-scatter.47.cloned.1.call-start = ((), (), s32[]{:S(2)}) async-start(), calls=%async_computation.34 | async-start | bytes 4456448
  963.7 893.8 %reduce-scatter.45.cloned.1.call-start = ((), (), s32[]{:S(2)}) async-start(), calls=%async_computation.33 | async-start | bytes 4456448
  1020.4 913.3 %reduce-scatter.29.cloned.1.call-start = ((), (), s32[]{:S(2)}) async-start(), calls=%async_computation.25 | async-start | bytes 4456448 | tf_op jit(solution)/shard_map/reduce_scatter | solution.py:275
  1076.9 932.9 %reduce-scatter.43.cloned.1.call-start = ((), (), s32[]{:S(2)}) async-start(), calls=%async_computation.32 | async-start | bytes 4456448
  1133.7 1057.3 %reduce-scatter.41.cloned.1.call-start = ((), (), s32[]{:S(2)}) async-start(), calls=%async_computation.31 | async-start | bytes 17825792 | tf_op jit(solution)/shard_map/reduce_scatter | solution.py:181
  1332.7 1039.3 %reduce-scatter.33.cloned.1.call-start = ((), (), s32[]{:S(2)}) async-start(), calls=%async_computation.27 | async-start | bytes 17825792 | tf_op jit(solution)/shard_map/reduce_scatter | solution.py:179
  1524.3 1028.8 %reduce-scatter.37.cloned.1.call-start = ((), (), s32[]{:S(2)}) async-start(), calls=%async_computation.29 | async-start | bytes 17825792 | tf_op jit(solution)/shard_map/reduce_scatter | solution.py:180
  1715.4 73.5 %copy-start.4 = (f32[128,2048]{1,0:T(8,128)S(1)}, f32[128,2048]{1,0:T(8,128)}, u32[]{:S(2)}) copy-start(f32[128,2048]{1,0:T(8,128)} %get-tuple-element.97) | copy-start | bytes 3145732
  1715.4 73.5 %copy-start.21 = (bf16[128,1024]{1,0:T(8,128)(2,1)S(1)}, bf16[128,1024]{1,0:T(8,128)(2,1)}, u32[]{:S(2)}) copy-start(bf16[128,1024]{1,0:T(8,128)(2,1)} %copy-done.20) | copy-start | bytes 786436
  1715.4 77.3 %copy-start.19 = (bf16[128,1024]{1,0:T(8,128)(2,1)S(1)}, bf16[128,1024]{1,0:T(8,128)(2,1)}, u32[]{:S(2)}) copy-start(bf16[128,1024]{1,0:T(8,128)(2,1)} %copy-done.18) | copy-start | bytes 786436
  (41 other events, 142.2 us)
Sparse Core Ops, SparseCore 0:
  9.5 59.4 all-gather.13
  70.6 56.7 all-gather.11
  128.9 56.7 all-gather.9
  187.1 56.7 all-gather.15
  245.2 198.8 all-gather.17
  445.5 198.8 all-gather.19
  645.9 198.8 all-gather.21
  905.1 54.3 reduce-scatter.24
  961.8 54.3 reduce-scatter.22
  1018.4 54.3 reduce-scatter.26
  1075.1 54.3 reduce-scatter.20
  1131.7 189.2 reduce-scatter.38
  1323.2 189.1 reduce-scatter.30
  1514.6 189.1 reduce-scatter.34
  1708.1 73.2 reduce-scatter.46
  1785.7 71.8 reduce-scatter.44
  1861.8 71.8 reduce-scatter.28
  1938.0 71.8 reduce-scatter.42
  2014.5 176.4 reduce-scatter.40
  2195.5 176.4 reduce-scatter.32
  2376.7 176.4 reduce-scatter.36
where the time goes:
time: 2570 us; the launch traced here: 2560 us
  waiting for transfers between devices  2240 us (87%)
  matrix products  138 us (5%)
  blocking collectives  85.3 us (3%)
  other arithmetic  50.8 us (2%)
  local copies, waits for them, and re-layouts  26.2 us (1%)
    all_gather x1, waiting for transfers between devices, body(): lax.all_gather(w_gate, 'shard', axis=0, tiled=True)  197 us
    all_gather x1, waiting for transfers between devices, body(): lax.all_gather(w_up, 'shard', axis=0, tiled=True)  191 us
    all_gather x1, waiting for transfers between devices, body(): lax.all_gather(w_down, 'shard', axis=0, tiled=True)  189 us
    reduce_scatter x1, waiting for transfers between devices, body(): lax.psum_scatter(mlp_grads[2].astype(jnp.bfloat16), 'shard', scatter_dime...  187 us
    reduce_scatter x1, waiting for transfers between devices, body(): lax.psum_scatter(mlp_half[1], 'replica', scatter_dimension=0, tiled=True)  181 us
    reduce_scatter x1, waiting for transfers between devices, body(): lax.psum_scatter(mlp_half[2], 'replica', scatter_dimension=0, tiled=True)  181 us
    reduce_scatter x1, waiting for transfers between devices, body(): lax.psum_scatter(mlp_half[0], 'replica', scatter_dimension=0, tiled=True)  181 us
    reduce_scatter x1, waiting for transfers between devices, body(): lax.psum_scatter(mlp_grads[0].astype(jnp.bfloat16), 'shard', scatter_dime...  180 us
  transfers between devices with their start and end apart: 21, of which 20 were waited for; matrix products, arithmetic and copies ran while one was open for 6% of the time, Pallas kernels for 0%

commit v1 on v0

v1 whole, which is shorter than its diff:
```python
import math

import jax
import jax.numpy as jnp
from jax import lax
from jax.sharding import Mesh
from jax.sharding import PartitionSpec as P

HD = 128
TP = 4
CORES = 2

eps_norm = 1e-06
rope_theta = 500000.0

DATA = ("shard", "hi", "core")
ALL = ("shard", "hi", "t", "core")


def rope_tables(length, half):
    position = jnp.arange(length).astype(jnp.float32)[:, None]
    exponent = jnp.arange(half).astype(jnp.float32) * (1.0 / half)
    angle = position * rope_theta ** (-exponent)
    return (jnp.cos(angle), jnp.sin(angle))


def rotate(field, cos_part, sin_part):
    half = field.shape[-1] // 2
    a = field[..., :half]
    b = field[..., half:]
    return jnp.concatenate([a * cos_part - b * sin_part, b * cos_part + a * sin_part], axis=-1)


def matmul(left, right):
    return jnp.dot(left, right, preferred_element_type=jnp.float32)


def matmul_nt(left, right):
    return lax.dot_general(left, right, (((1,), (1,)), ((), ())), preferred_element_type=jnp.float32)


def matmul_tn(left, right):
    return lax.dot_general(left, right, (((0,), (0,)), ((), ())), preferred_element_type=jnp.float32)


def body(x_in, cotangent, w_query, w_key, w_value, w_out, w_gate, w_up, w_down,
         gain_query, gain_key, gain_attn, gain_mlp):
    bf16, f32 = jnp.bfloat16, jnp.float32
    t = lax.axis_index("t")
    core = lax.axis_index("core")
    shards = lax.axis_size("shard")
    his = lax.axis_size("hi")
    seqs, length, width = x_in.shape
    tokens = seqs * length
    att = w_query.shape[1]
    ff = w_gate.shape[1]
    heads_here = att // HD // TP

    def at(array, axis, index):
        return lax.dynamic_index_in_dim(array, index, axis, keepdims=False)

    def head_cols(w):
        return at(w.reshape(w.shape[0], heads_here, TP, HD), 2, t).reshape(w.shape[0], heads_here * HD)

    def hidden_cols(w):
        return at(w.reshape(w.shape[0], shards, his, TP, -1), 3, t).reshape(w.shape[0], ff // TP)

    def whole(block):
        rows = block.shape[0] // CORES
        piece = lax.dynamic_slice_in_dim(block, core * rows, rows, 0)
        return lax.all_gather(piece, ("shard", "core"), axis=0, tiled=True)

    gains = lax.all_gather(jnp.concatenate([gain_query, gain_key, gain_attn, gain_mlp]), "shard", axis=0)
    na, nd = gain_query.shape[0], gain_attn.shape[0]
    g_query = gains[:, :na].reshape(-1).astype(f32)
    g_key = gains[:, na:2 * na].reshape(-1).astype(f32)
    g_attn = gains[:, 2 * na:2 * na + nd].reshape(-1).astype(f32)
    g_mlp = gains[:, 2 * na + nd:].reshape(-1).astype(f32)
    g_query = at(g_query.reshape(heads_here, TP, HD), 1, t).reshape(-1)
    g_key = at(g_key.reshape(heads_here, TP, HD), 1, t).reshape(-1)

    rows = x_in.reshape(tokens, width)
    x_all = lax.all_gather(rows, "t", axis=0, tiled=True)
    w_qkv = whole(jnp.concatenate([head_cols(w_query), head_cols(w_key), head_cols(w_value)], axis=1))
    w_o = whole(at(w_out.reshape(heads_here // shards, TP, HD, width), 1, t).reshape(-1, width))
    w_gu = whole(jnp.concatenate([hidden_cols(w_gate), hidden_cols(w_up)], axis=1))
    w_d = whole(at(w_down.reshape(his, TP, -1, width), 1, t).reshape(-1, width))

    ha = heads_here * HD
    four = (TP * seqs, length, heads_here, HD)
    wave_cos, wave_sin = rope_tables(length, HD // 2)
    wave_cos = wave_cos[None, :, None, :]
    wave_sin = wave_sin[None, :, None, :]
    causal = jnp.arange(length)[:, None] >= jnp.arange(length)[None, :]

    qkv = matmul(x_all, w_qkv)
    q_proj, k_proj = qkv[:, :ha], qkv[:, ha:2 * ha]
    value = qkv[:, 2 * ha:].astype(bf16).reshape(four)
    squares = jnp.stack([jnp.sum(q_proj * q_proj, -1), jnp.sum(k_proj * k_proj, -1)])
    squares = lax.psum(squares, "t")
    scales = lax.rsqrt(squares / att + eps_norm)
    q_scale, k_scale = scales[0][:, None], scales[1][:, None]
    q_rot = rotate((q_proj * q_scale * g_query).reshape(four), wave_cos, wave_sin).astype(bf16)
    k_rot = rotate((k_proj * k_scale * g_key).reshape(four), wave_cos, wave_sin).astype(bf16)
    scores = jnp.einsum("sqhd,skhd->shqk", q_rot, k_rot, preferred_element_type=f32) / math.sqrt(HD)
    scores = jnp.where(causal, scores, -jnp.inf)
    peak = jnp.max(scores, axis=-1, keepdims=True)
    log_total = peak + jnp.log(jnp.sum(jnp.exp(scores - peak), axis=-1, keepdims=True))
    probs = jnp.exp(scores - log_total)
    probs_low = probs.astype(bf16)
    mixed = jnp.einsum("shqk,skhd->sqhd", probs_low, value, preferred_element_type=f32)
    mixed = mixed.astype(bf16).reshape(-1, ha)

    def scatter(partial):
        return lax.psum_scatter(partial.astype(bf16), "t", scatter_dimension=0, tiled=True).astype(f32)

    def rms_scale(field):
        return lax.rsqrt(jnp.mean(field * field, axis=-1, keepdims=True) + eps_norm)

    def norm_back(grad_out, field, scale, gain):
        weighted = grad_out * gain
        inner = jnp.mean(weighted * field, axis=-1, keepdims=True)
        return scale * weighted - field * scale**3 * inner, jnp.sum(grad_out * field * scale, axis=0)

    attn_proj = scatter(matmul(mixed, w_o))
    attn_scale = rms_scale(attn_proj)
    residual = rows.astype(f32) + attn_proj * attn_scale * g_attn
    res_all = lax.all_gather(residual.astype(bf16), "t", axis=0, tiled=True)
    gu = matmul(res_all, w_gu)
    fh = ff // TP
    gate, up = gu[:, :fh], gu[:, fh:]
    sig = jax.nn.sigmoid(gate)
    silu = gate * sig
    hidden = (silu * up).astype(bf16)
    down = scatter(matmul(hidden, w_d))
    down_scale = rms_scale(down)
    output = residual + down * down_scale * g_mlp

    cot = cotangent.reshape(tokens, width).astype(f32)
    grad_down, gg_mlp = norm_back(cot, down, down_scale, g_mlp)
    gd_all = lax.all_gather(grad_down.astype(bf16), "t", axis=0, tiled=True)
    gw_down = matmul_tn(hidden, gd_all)
    grad_hidden = matmul_nt(gd_all, w_d)
    grad_gate = (grad_hidden * up * sig * (1.0 + gate * (1.0 - sig))).astype(bf16)
    grad_up = (grad_hidden * silu).astype(bf16)
    grad_gu = jnp.concatenate([grad_gate, grad_up], axis=1)
    gw_gu = matmul_tn(res_all, grad_gu)
    grad_res = cot + scatter(matmul_nt(grad_gu, w_gu))

    grad_attn, gg_attn = norm_back(grad_res, attn_proj, attn_scale, g_attn)
    ga_all = lax.all_gather(grad_attn.astype(bf16), "t", axis=0, tiled=True)
    gw_out = matmul_tn(mixed, ga_all)
    grad_mixed = matmul_nt(ga_all, w_o).astype(bf16).reshape(four)
    grad_value = jnp.einsum("shqk,sqhd->skhd", probs_low, grad_mixed, preferred_element_type=f32).astype(bf16)
    grad_probs = jnp.einsum("sqhd,skhd->shqk", grad_mixed, value, preferred_element_type=f32)
    grad_scores = probs * (grad_probs - jnp.sum(probs * grad_probs, axis=-1, keepdims=True))
    grad_scores = (grad_scores / math.sqrt(HD)).astype(bf16)
    grad_q = jnp.einsum("shqk,skhd->sqhd", grad_scores, k_rot, preferred_element_type=f32)
    grad_k = jnp.einsum("shqk,sqhd->skhd", grad_scores, q_rot, preferred_element_type=f32)
    grad_q = rotate(grad_q, wave_cos, -wave_sin).reshape(-1, ha)
    grad_k = rotate(grad_k, wave_cos, -wave_sin).reshape(-1, ha)
    gg_query = jnp.sum(grad_q * q_proj * q_scale, axis=0)
    gg_key = jnp.sum(grad_k * k_proj * k_scale, axis=0)
    wq_, wk_ = grad_q * g_query, grad_k * g_key
    inner = lax.psum(jnp.stack([jnp.sum(wq_ * q_proj, -1), jnp.sum(wk_ * k_proj, -1)]), "t") / att
    gq = (q_scale * wq_ - q_proj * q_scale**3 * inner[0][:, None]).astype(bf16)
    gk = (k_scale * wk_ - k_proj * k_scale**3 * inner[1][:, None]).astype(bf16)
    grad_qkv = jnp.concatenate([gq, gk, grad_value.reshape(-1, ha)], axis=1)
    gw_qkv = matmul_tn(x_all, grad_qkv)
    grad_input = grad_res + scatter(matmul_nt(grad_qkv, w_qkv))

    def reduce_rows(grad):
        own = grad.shape[0] // (shards * his * TP * CORES)
        pieces = grad.astype(bf16).reshape(shards, his, TP, CORES, own, -1).transpose(0, 1, 3, 2, 4, 5)
        pieces = pieces.reshape(shards * his * CORES * TP * own, -1)
        mine = lax.psum_scatter(pieces, DATA, scatter_dimension=0, tiled=True)
        mine = lax.all_to_all(mine.reshape(TP, own, -1), "t", 0, 0)
        return mine.astype(f32)

    r_gu = reduce_rows(gw_gu)
    own = r_gu.shape[1]

    def hidden_out(block):
        return block.reshape(TP, own, shards, his, -1).transpose(1, 2, 3, 0, 4).reshape(own, ff)

    r_gate, r_up = hidden_out(r_gu[..., :fh]), hidden_out(r_gu[..., fh:])
    r_qkv = reduce_rows(gw_qkv)

    def head_out(block):
        return block.reshape(TP, own, heads_here, HD).transpose(1, 2, 0, 3).reshape(own, att)

    r_down = lax.psum_scatter(gw_down.astype(bf16), DATA, scatter_dimension=0, tiled=True).astype(f32)
    padded = jnp.zeros((shards, heads_here // shards, TP, HD, width), bf16)
    padded = lax.dynamic_update_index_in_dim(
        padded, gw_out.astype(bf16).reshape(shards, heads_here // shards, HD, width), t, 2)
    r_out = lax.psum_scatter(padded.reshape(att, width), ALL, scatter_dimension=0, tiled=True).astype(f32)

    def spread(vec):
        wide = jnp.zeros((heads_here, TP, HD), f32)
        return lax.dynamic_update_index_in_dim(wide, vec.reshape(heads_here, HD), t, 1).reshape(-1)

    devices = shards * his * TP * CORES
    small = jnp.concatenate([v.reshape(devices, -1) for v in (spread(gg_query), spread(gg_key), gg_attn, gg_mlp)], axis=1)
    small = lax.psum_scatter(small, ALL, scatter_dimension=0, tiled=True)[0]
    na, nd = att // devices, width // devices
    return (
        output.astype(bf16).reshape(x_in.shape),
        grad_input.reshape(x_in.shape),
        head_out(r_qkv[..., :ha]),
        head_out(r_qkv[..., ha:2 * ha]),
        head_out(r_qkv[..., 2 * ha:]),
        r_out,
        r_gate,
        r_up,
        r_down,
        small[:na],
        small[na:2 * na],
        small[2 * na:2 * na + nd],
        small[2 * na + nd:],
    )


def solution(mesh):
    shards, replicas = mesh.shape["shard"], mesh.shape["replica"]
    inner = Mesh(mesh.devices.reshape(shards, replicas // (TP * CORES), TP, CORES), ALL)
    token = P(ALL, None, None)
    weight = P("shard", None)
    return jax.shard_map(
        body,
        mesh=inner,
        in_specs=(token, token) + (weight,) * 7 + (P("shard"),) * 4,
        out_specs=(token, token) + (P(ALL, None),) * 7 + (P(ALL),) * 4,
        check_vma=False,
    )
```

time: 2570 us -> 1000 us (0.39)
  waiting for transfers between devices: 2240 us -> 685 us
  local copies, waits for them, and re-layouts: 26.2 us -> 107 us
  matrix products: 138 us -> 73.1 us
    reduce_scatter x11 -> x8, waiting for transfers between devices: 1320 us -> 444 us  [the longest x4 127 us: scatter(): lax.psum_scatter(partial.astype(bf16), 't', scatter_dimension=0, tiled=True)]
    all_gather x7 -> x8, waiting for transfers between devices: 776 us -> 241 us  [the longest x4 115 us: whole(): return lax.all_gather(piece, ('shard', 'core'), axis=0, tiled=True)]
    unnamed x24 -> x16, waiting for transfers between devices: 141 us -> 0.93 us
    dot_general x21 -> x4, matrix products: 129 us -> 21.5 us  [matmul(): return jnp.dot(left, right, preferred_element_type=jnp.float32)]
    dot_general x6 -> x14, matrix products: 8.09 us -> 51.6 us  [the longest x4 23.8 us: matmul_nt(): lax.dot_general(left, right, (((1,), (1,)), ((), ())), preferred_element_...]
    convert_element_type x16 -> x8, other arithmetic: 42.8 us -> 12.9 us  [the longest x1 2.96 us: body(): ga_all = lax.all_gather(grad_attn.astype(bf16), 't', axis=0, tiled=True)]
    unnamed x117 -> x102, local copies, waits for them, and re-layouts: 25 us -> 51.8 us
    unnamed x2 -> x1, blocking collectives: 66.5 us -> 46.3 us
  transfers between devices with their start and end apart: 21 -> 18, of which waited for: 20 -> 14; matrix products, arithmetic and copies ran while one was open for 6% -> 13% of each run, Pallas kernels for 0% -> 0%
where the time goes in v1:
time: 1000 us; the launch traced here: 994 us
  waiting for transfers between devices  685 us (68%)
  local copies, waits for them, and re-layouts  107 us (11%)
  matrix products  73.1 us (7%)
  blocking collectives  70.1 us (7%)
  other arithmetic  35 us (4%)
  between operations  15.2 us (2%)
    reduce_scatter x4, waiting for transfers between devices, scatter(): lax.psum_scatter(partial.astype(bf16), 't', scatter_dimension=0, tiled=True)  127 us
    reduce_scatter x2, waiting for transfers between devices, reduce_rows(): mine = lax.psum_scatter(pieces, DATA, scatter_dimension=0, tiled=True)  126 us
    reduce_scatter x1, waiting for transfers between devices, body(): lax.psum_scatter(padded.reshape(att, width), ALL, scatter_dimension=0, ti...  124 us
    all_gather x4, waiting for transfers between devices, whole(): return lax.all_gather(piece, ('shard', 'core'), axis=0, tiled=True)  115 us
    reduce_scatter x1, waiting for transfers between devices, body(): lax.psum_scatter(gw_down.astype(bf16), DATA, scatter_dimension=0, tiled=T...  67.4 us
    unnamed x102, local copies, waits for them, and re-layouts  51.8 us
    unnamed x1, blocking collectives  46.3 us
    all_gather x1, waiting for transfers between devices, body(): gd_all = lax.all_gather(grad_down.astype(bf16), 't', axis=0, tiled=True)  44.2 us
  transfers between devices with their start and end apart: 18, of which 14 were waited for; matrix products, arithmetic and copies ran while one was open for 13% of the time, Pallas kernels for 0%

profile of v1, /device:TPU:0, one launch (start us, length us, event | category | flops | bytes accessed | tf_op | source)
XLA Modules:
  0.0 993.6 jit_solution(16554085987702400809)
XLA Ops:
  8.0 3.9 copy.105
  15.9 4.0 copy.104
  24.3 5.3 all-gather.1
  30.7 25.8 %all-gather.24.cloned.1.call-done = bf16[1,512,2048]{2,1,0:T(8,128)(2,1)} async-done(((bf16[1,128,2048]{2,1,0:T(8,128)(2,1)}), bf16[1,512,2048]{2,1,0:T(8,128)(2,1)}) %all-gather.24.cloned.1.call-update) | async-done | bytes 2097168 | tf_op jit(solution)/shard_map/all_gather | solution.py:83
  56.5 30.4 %all-gather.12.cloned.1.call-done = bf16[2048,768]{0,1:T(8,128)(2,1)} async-done(((bf16[512,768]{0,1:T(8,128)(2,1)}), bf16[2048,768]{0,1:T(8,128)(2,1)}) %all-gather.12.cloned.1.call-update) | async-done | bytes 3145744 | tf_op jit(solution)/shard_map/all_gather | solution.py:71
  86.8 4.4 fusion.7
  91.4 9.8 psum.14
  120.2 41.1 %reduce-scatter.9.cloned.1.call-done = bf16[128,2048]{1,0:T(8,128)(2,1)} async-done(((bf16[512,2048]{1,0:T(8,128)(2,1)}), bf16[128,2048]{1,0:T(8,128)(2,1)}) %reduce-scatter.9.cloned.1.call-update) | async-done | bytes 524304 | tf_op jit(solution)/shard_map/reduce_scatter | solution.py:115
  165.2 12.0 %copy.114 = bf16[1024,4096]{0,1:T(8,128)(2,1)} copy(bf16[1024,4096]{1,0:T(8,128)(2,1)} %param.19) | data formatting | bytes 16777216 | tf_op args[6]
  177.2 12.0 %copy.115 = bf16[1024,4096]{0,1:T(8,128)(2,1)} copy(bf16[1024,4096]{1,0:T(8,128)(2,1)} %param.20) | data formatting | bytes 16777216 | tf_op args[7]
  196.6 12.8 %all-gather.14.cloned.1.call-done = bf16[512,2048]{1,0:T(8,128)(2,1)} async-done(((bf16[128,2048]{1,0:T(8,128)(2,1)}), bf16[512,2048]{1,0:T(8,128)(2,1)}) %all-gather.14.cloned.1.call-update) | async-done | bytes 2097168 | tf_op jit(solution)/shard_map/all_gather | solution.py:128
  209.4 59.4 %all-gather.16.cloned.1.call-done = bf16[2048,2048]{0,1:T(8,128)(2,1)} async-done(((bf16[512,2048]{0,1:T(8,128)(2,1)}), bf16[2048,2048]{0,1:T(8,128)(2,1)}) %all-gather.16.cloned.1.call-update) | async-done | bytes 8388624 | tf_op jit(solution)/shard_map/all_gather | solution.py:71
  268.8 7.6 fusion.83
  280.0 25.4 %all-gather.18.cloned.1.call-done = bf16[1024,2048]{1,0:T(8,128)(2,1)} async-done(((bf16[256,2048]{1,0:T(8,128)(2,1)}), bf16[1024,2048]{1,0:T(8,128)(2,1)}) %all-gather.18.cloned.1.call-update) | async-done | bytes 4194320 | tf_op jit(solution)/shard_map/all_gather | solution.py:71
  305.4 6.2 convolution_convert_fusion.3
  311.7 42.9 %reduce-scatter.11.cloned.1.call-done = bf16[128,2048]{1,0:T(8,128)(2,1)} async-done(((bf16[512,2048]{1,0:T(8,128)(2,1)}), bf16[128,2048]{1,0:T(8,128)(2,1)}) %reduce-scatter.11.cloned.1.call-update) | async-done | bytes 524304 | tf_op jit(solution)/shard_map/reduce_scatter | solution.py:115
  360.2 44.2 %all-gather.20.cloned.1.call-done = bf16[512,2048]{1,0:T(8,128)(2,1)} async-done(((bf16[128,2048]{1,0:T(8,128)(2,1)}), bf16[512,2048]{1,0:T(8,128)(2,1)}) %all-gather.20.cloned.1.call-update) | async-done | bytes 2097168 | tf_op jit(solution)/shard_map/all_gather | solution.py:141
  404.4 7.0 multiply_convert_fusion.1
  412.7 9.1 convolution_convert_fusion.6
  421.9 42.6 %reduce-scatter.13.cloned.1.call-done = bf16[128,2048]{1,0:T(8,128)(2,1)} async-done(((bf16[512,2048]{1,0:T(8,128)(2,1)}), bf16[128,2048]{1,0:T(8,128)(2,1)}) %reduce-scatter.13.cloned.1.call-update) | async-done | bytes 524304 | tf_op jit(solution)/shard_map/reduce_scatter | solution.py:115
  471.3 42.7 %all-gather.22.cloned.1.call-done = bf16[512,2048]{1,0:T(8,128)(2,1)} async-done(((bf16[128,2048]{1,0:T(8,128)(2,1)}), bf16[512,2048]{1,0:T(8,128)(2,1)}) %all-gather.22.cloned.1.call-update) | async-done | bytes 2097168 | tf_op jit(solution)/shard_map/all_gather | solution.py:151
  533.9 8.6 psum.15
  547.8 4.7 copy.129
  557.9 8.5 convolution_convert_fusion
  566.4 8.8 copy.135
  576.4 6.0 convolution_convert_fusion.1
  583.5 5.1 convolution_convert_fusion.5
  595.5 20.6 %reduce-scatter.17.cloned.1.call-done = bf16[256,768]{1,0:T(8,128)(2,1)} async-done(((bf16[2048,768]{1,0:T(8,128)(2,1)}), bf16[256,768]{1,0:T(8,128)(2,1)}) %reduce-scatter.17.cloned.1.call-update) | async-done | bytes 393232 | tf_op jit(solution)/shard_map/reduce_scatter | solution.py:176
  619.5 105.1 %reduce-scatter.21.cloned.1.call-done = bf16[256,2048]{1,0:T(8,128)(2,1)} async-done(((bf16[2048,2048]{1,0:T(8,128)(2,1)}), bf16[256,2048]{1,0:T(8,128)(2,1)}) %reduce-scatter.21.cloned.1.call-update) | async-done | bytes 1048592 | tf_op jit(solution)/shard_map/reduce_scatter | solution.py:176
  728.3 67.4 %reduce-scatter.23.cloned.1.call-done = bf16[128,2048]{1,0:T(8,128)(2,1)} async-done(((bf16[1024,2048]{1,0:T(8,128)(2,1)}), bf16[128,2048]{1,0:T(8,128)(2,1)}) %reduce-scatter.23.cloned.1.call-update) | async-done | bytes 524304 | tf_op jit(solution)/shard_map/reduce_scatter | solution.py:192
  798.2 46.3 %all-reduce = f32[32,192]{1,0:T(8,128)S(1)} all-reduce(f32[32,192]{1,0:T(8,128)S(1)} %pad_maximum_fusion.14), channel_id=13, replica_groups=mesh['shard'=2,'hi'=2,'t'=4,'core'=2] {'shard','hi','t','core'}, use_global_device_ids=true, to_apply=%region_25.26.clone | all-reduce | flops 6144 | bytes 49152
  861.0 124.0 %reduce-scatter.19.cloned.1.call-done = bf16[32,2048]{1,0:T(8,128)(2,1)} async-done(((bf16[1024,2048]{1,0:T(8,128)(2,1)}), bf16[32,2048]{1,0:T(8,128)(2,1)}) %reduce-scatter.19.cloned.1.call-update) | async-done | bytes 131088 | tf_op jit(solution)/shard_map/reduce_scatter | solution.py:196
  (242 shorter events, 124.7 us)
Async XLA Ops:
  7.2 16.2 %copy-start = (bf16[512,2048]{1,0:T(8,128)(2,1)S(1)}, bf16[512,2048]{1,0:T(8,128)(2,1)}, u32[]{:S(2)}) copy-start(bf16[512,2048]{1,0:T(8,128)(2,1)} %param.18) | copy-start | bytes 6291460
  7.2 49.3 %all-gather.24.cloned.1.call-start = ((), (), s32[]{:S(2)}) async-start(), calls=%async_computation.24 | async-start | bytes 2621440 | tf_op jit(solution)/shard_map/all_gather | solution.py:83
  7.9 78.9 %all-gather.12.cloned.1.call-start = ((), (), s32[]{:S(2)}) async-start(), calls=%async_computation.10 | async-start | bytes 3932160 | tf_op jit(solution)/shard_map/all_gather | solution.py:71
  23.3 92.8 %all-gather.26.cloned.1.call-start = ((), (), s32[]{:S(2)}) async-start(), calls=%async_computation.25 | async-start | bytes 1310720 | tf_op jit(solution)/shard_map/all_gather | solution.py:71
  24.1 137.1 %reduce-scatter.9.cloned.1.call-start = ((), (), s32[]{:S(2)}) async-start(), calls=%async_computation.11 | async-start | bytes 2621440 | tf_op jit(solution)/shard_map/reduce_scatter | solution.py:115
  29.6 61.6 %copy-start.24 = (bf16[2,3072]{1,0:T(2,128)(2,1)}, bf16[2,3072]{1,0:T(2,128)(2,1)S(1)}, u32[]{:S(2)}) copy-start(bf16[2,3072]{1,0:T(2,128)(2,1)S(1)} %reshape.425) | copy-start | bytes 36868
  29.7 71.6 %copy-start.30 = (f32[2,1,128]{2,1,0:T(1,128)}, f32[2,1,128]{2,1,0:T(1,128)S(1)}, u32[]{:S(2)}) copy-start(f32[2,1,128]{2,1,0:T(1,128)S(1)} %get-tuple-element.77) | copy-start | bytes 3076
  29.7 71.6 %copy-start.32 = (f32[2,1,128]{2,1,0:T(1,128)}, f32[2,1,128]{2,1,0:T(1,128)S(1)}, u32[]{:S(2)}) copy-start(f32[2,1,128]{2,1,0:T(1,128)S(1)} %get-tuple-element.78) | copy-start | bytes 3076
  120.1 42.9 %copy-start.4 = (bf16[1,128,2048]{2,1,0:T(8,128)(2,1)S(1)}, bf16[1,128,2048]{2,1,0:T(8,128)(2,1)}, u32[]{:S(2)}) copy-start(bf16[1,128,2048]{2,1,0:T(8,128)(2,1)} %param.13) | copy-start | bytes 1572868
  120.1 89.3 %all-gather.14.cloned.1.call-start = ((), (), s32[]{:S(2)}) async-start(), calls=%async_computation.12 | async-start | bytes 2621440 | tf_op jit(solution)/shard_map/all_gather | solution.py:128
  163.0 14.2 %copy-start.35 = (f32[128]{0:T(128)}, f32[128]{0:T(128)S(1)}, u32[]{:S(2)}) copy-start(f32[128]{0:T(128)S(1)} %get-tuple-element.70) | copy-start | bytes 1540
  165.1 103.7 %all-gather.16.cloned.1.call-start = ((), (), s32[]{:S(2)}) async-start(), calls=%async_computation.13 | async-start | bytes 10485760 | tf_op jit(solution)/shard_map/all_gather | solution.py:71
  193.5 111.9 %all-gather.18.cloned.1.call-start = ((), (), s32[]{:S(2)}) async-start(), calls=%async_computation.14 | async-start | bytes 5242880 | tf_op jit(solution)/shard_map/all_gather | solution.py:71
  196.4 158.2 %reduce-scatter.11.cloned.1.call-start = ((), (), s32[]{:S(2)}) async-start(), calls=%async_computation.15 | async-start | bytes 2621440 | tf_op jit(solution)/shard_map/reduce_scatter | solution.py:115
  311.6 44.2 %copy-start.2 = (bf16[1,128,2048]{2,1,0:T(8,128)(2,1)S(1)}, bf16[1,128,2048]{2,1,0:T(8,128)(2,1)}, u32[]{:S(2)}) copy-start(bf16[1,128,2048]{2,1,0:T(8,128)(2,1)} %param.14) | copy-start | bytes 1572868
  311.6 92.8 %all-gather.20.cloned.1.call-start = ((), (), s32[]{:S(2)}) async-start(), calls=%async_computation.16 | async-start | bytes 2621440 | tf_op jit(solution)/shard_map/all_gather | solution.py:141
  360.1 104.3 %reduce-scatter.13.cloned.1.call-start = ((), (), s32[]{:S(2)}) async-start(), calls=%async_computation.17 | async-start | bytes 2621440 | tf_op jit(solution)/shard_map/reduce_scatter | solution.py:115
  421.8 44.9 %copy-start.3 = (bf16[128,2048]{1,0:T(8,128)(2,1)S(1)}, bf16[128,2048]{1,0:T(8,128)(2,1)}, u32[]{:S(2)}) copy-start(bf16[128,2048]{1,0:T(8,128)(2,1)} %reduce-scatter.11.cloned.1.call-done) | copy-start | bytes 1572868
  421.8 92.1 %all-gather.22.cloned.1.call-start = ((), (), s32[]{:S(2)}) async-start(), calls=%async_computation.18 | async-start | bytes 2621440 | tf_op jit(solution)/shard_map/all_gather | solution.py:151
  469.6 146.4 %reduce-scatter.17.cloned.1.call-start = ((), (), s32[]{:S(2)}) async-start(), calls=%async_computation.20 | async-start | bytes 3538944 | tf_op jit(solution)/shard_map/reduce_scatter | solution.py:176
  471.3 48.2 %copy-start.27 = (f32[1,8,128]{2,1,0:T(8,128)S(1)}, f32[1,8,128]{2,1,0:T(8,128)}, u32[]{:S(2)}) copy-start(f32[1,8,128]{2,1,0:T(8,128)} %copy-done.26) | copy-start | bytes 12292
  516.5 5.6 copy-start.12
  556.4 168.2 %reduce-scatter.21.cloned.1.call-start = ((), (), s32[]{:S(2)}) async-start(), calls=%async_computation.22 | async-start | bytes 9437184 | tf_op jit(solution)/shard_map/reduce_scatter | solution.py:176
  575.2 220.5 %reduce-scatter.23.cloned.1.call-start = ((), (), s32[]{:S(2)}) async-start(), calls=%async_computation.23 | async-start | bytes 4718592 | tf_op jit(solution)/shard_map/reduce_scatter | solution.py:192
  582.5 263.2 %reduce-scatter.15.cloned.1.call-start = ((), (), s32[]{:S(2)}) async-start(), calls=%async_computation.19 | async-start | bytes 2621440 | tf_op jit(solution)/shard_map/reduce_scatter | solution.py:115
  588.6 396.3 %reduce-scatter.19.cloned.1.call-start = ((), (), s32[]{:S(2)}) async-start(), calls=%async_computation.21 | async-start | bytes 4325376 | tf_op jit(solution)/shard_map/reduce_scatter | solution.py:196
  595.4 132.7 %copy-start.28 = (f32[2048]{0:T(1024)S(1)}, f32[2048]{0:T(1024)}, u32[]{:S(2)}) copy-start(f32[2048]{0:T(1024)} %get-tuple-element.23) | copy-start | bytes 24580
  595.5 132.7 %copy-start.29 = (f32[2048]{0:T(1024)S(1)}, f32[2048]{0:T(1024)}, u32[]{:S(2)}) copy-start(f32[2048]{0:T(1024)} %get-tuple-element.19) | copy-start | bytes 24580
  616.0 108.6 %all-to-all-start = ((bf16[4,64,768]{2,1,0:T(8,128)(2,1)}), bf16[4,64,768]{2,1,0:T(8,128)(2,1)S(1)}, u32[]{:S(2)}, u32[]{:S(2)}) async-start(bf16[4,64,768]{2,1,0:T(8,128)(2,1)} %bitcast.207), calls=%async_computation.5 | async-start | bytes 786432 | tf_op jit(solution)/shard_map/all_to_all | solution.py:177
  619.5 226.2 %copy-start.5 = (bf16[128,2048]{1,0:T(8,128)(2,1)S(1)}, bf16[128,2048]{1,0:T(8,128)(2,1)}, u32[]{:S(2)}) copy-start(bf16[128,2048]{1,0:T(8,128)(2,1)} %reduce-scatter.13.cloned.1.call-done) | copy-start | bytes 1572868
  724.6 126.8 %all-to-all-start.1 = ((bf16[4,64,2048]{2,1,0:T(8,128)(2,1)}), bf16[4,64,2048]{2,1,0:T(8,128)(2,1)S(1)}, u32[]{:S(2)}, u32[]{:S(2)}) async-start(bf16[4,64,2048]{2,1,0:T(8,128)(2,1)} %bitcast.201), calls=%async_computation.8 | async-start | bytes 2097152 | tf_op jit(solution)/shard_map/all_to_all | solution.py:177
  856.6 130.0 %copy-start.1 = (bf16[512,2048]{1,0:T(8,128)(2,1)S(1)}, bf16[512,2048]{1,0:T(8,128)(2,1)}, u32[]{:S(2)}) copy-start(bf16[512,2048]{1,0:T(8,128)(2,1)} %param.18) | copy-start | bytes 6291460
  (31 other events, 53.4 us)
Sparse Core Ops, SparseCore 0:
  9.6 46.8 all-gather.23
  58.6 28.1 all-gather.11
  89.0 16.6 all-gather.25
  120.2 40.9 reduce-scatter.8
  165.2 44.1 all-gather.13
  210.8 57.9 all-gather.15
  270.9 34.4 all-gather.17
  311.8 42.7 reduce-scatter.10
  360.2 44.1 all-gather.19
  421.9 42.4 reduce-scatter.12
  469.7 44.1 all-gather.21
  556.5 59.4 reduce-scatter.16
  619.5 105.0 reduce-scatter.20
  727.8 67.8 reduce-scatter.22
  797.9 42.1 reduce-scatter.14
  842.1 142.7 reduce-scatter.18

commit v2 on v1

v2 whole, which is shorter than its diff:
```python
import functools
import math

import jax
import jax.numpy as jnp
from jax import lax
from jax.experimental import pallas as pl
from jax.experimental.pallas import tpu as pltpu
from jax.sharding import PartitionSpec as P

HD = 128
TP = 4
CORES = 2
CHUNKS = 4

eps_norm = 1e-06
rope_theta = 500000.0

bf16 = jnp.bfloat16
f32 = jnp.float32


def rope_tables(length, half):
    position = jnp.arange(length).astype(f32)[:, None]
    exponent = jnp.arange(half).astype(f32) * (1.0 / half)
    angle = position * rope_theta ** (-exponent)
    return (jnp.cos(angle), jnp.sin(angle))


def dot_nn(left, right):
    return lax.dot_general(left, right, (((1,), (0,)), ((), ())), preferred_element_type=f32)


def dot_nt(left, right, precision=None):
    return lax.dot_general(
        left, right, (((1,), (1,)), ((), ())), preferred_element_type=f32, precision=precision)


def dot_tn(left, right):
    return lax.dot_general(left, right, (((0,), (0,)), ((), ())), preferred_element_type=f32)


def mul_of(index, step):
    return pl.ds(pl.multiple_of(index * step, step), step)


def loop(count, step):
    lax.fori_loop(0, count, lambda i, c: (step(i), c)[1], 0)


class Dims:
    def __init__(self, length, width, att, ff, shards, replicas):
        self.L, self.D, self.att, self.ff = length, width, att, ff
        self.S, self.R = shards, replicas
        self.his = replicas // (TP * CORES)
        self.T = TP * length
        self.ha = att // TP
        self.fh = ff // TP
        self.unit = ff // (shards * replicas)
        self.own = width // (shards * replicas)
        self.own_o = att // (shards * replicas)
        self.pieces = HD // self.own_o
        self.levels = self.his.bit_length() - 1
        self.gains = 2 * HD + width
        self.ggs = 2 * width + 2 * att
        assert shards == 2 and self.his == 1 << self.levels and self.ha == shards * HD


def kernel(
    d,
    x_h, cot_h, wqkv_h, wo_h, wgu_h, wd_h, gain_v, cos_v, sin_v,
    out_h, gin_h, gu_h, qkv_h, down_h, o_h, gg_o,
    wqkv, wo, wgu, wd, gbuf, gat, gml,
    xall, rall, gdall, gaall, cot,
    qk, vb, qkrot, probs, mixed, gqkv, stat, statr,
    gu, hid, gg2,
    abuf, bbuf, cbuf, outb,
    acc, s1, s2, r1, r2, k2,
    stage, rc_gu, rc_d, rc_q, rc_o, rx_gu, rx_d, rx_q, rx_o, rh_gu, rh_d, rh_q, o_pc,
    gsum, grecv,
    ag_s, ag_r, rs_s, rs_r, w_s, w_r, wf_s, wf_r, loc, st_s, st_r,
    stg_s, c_s, c_r, x_s, x_r, h_s, h_r, a_s, a_r, o_s, o_r, gn_s, gn_r,
):
    L, D, T, ha, fh = d.L, d.D, d.T, d.ha, d.fh
    CW = D // CHUNKS
    HW = CW // 2
    s = lax.axis_index("shard")
    r = lax.axis_index("replica")
    hi, t, core = r // (TP * CORES), (r // CORES) % TP, r % CORES
    tz, ty = t // 2, t % 2
    t_y, t_z, t_d = tz * 2 + 1 - ty, (1 - tz) * 2 + ty, (1 - tz) * 2 + 1 - ty

    def rep(hi_, t_, core_):
        return hi_ * (TP * CORES) + t_ * CORES + core_

    dev_y, dev_z, dev_d = ((s, rep(hi, q, core)) for q in (t_y, t_z, t_d))
    dev_x = (1 - s, r)
    dev_c = (s, rep(hi, t, 1 - core))

    def send(src, dst, ssem, rsem, dev):
        return pltpu.make_async_remote_copy(
            src_ref=src, dst_ref=dst, send_sem=ssem, recv_sem=rsem, device_id=dev,
            device_id_type=pl.DeviceIdType.MESH)

    def blk(q):
        return mul_of(q, L)

    barrier = pltpu.get_barrier_semaphore()

    def greet(q):
        @pl.when(q != r)
        def _():
            pl.semaphore_signal(barrier, inc=1, device_id=(s, q), device_id_type=pl.DeviceIdType.MESH)

    loop(d.R, greet)
    pl.semaphore_signal(barrier, inc=1, device_id=dev_x, device_id_type=pl.DeviceIdType.MESH)
    pl.semaphore_wait(barrier, d.R)

    def ag_copies(buf, inst, i, src=None):
        own = buf.at[blk(t), pl.ds(i * CW, CW)]
        first = own if src is None else src.at[:, pl.ds(i * CW, CW)]
        ca, cb = pl.ds(i * CW, HW), pl.ds(i * CW + HW, HW)
        fy, fz = buf.at[blk(t_y), ca], buf.at[blk(t_z), cb]
        ends = ((first, own, dev_y), (first, own, dev_z), (fy, fy, dev_z), (fz, fz, dev_y))

        def copy(j):
            return send(ends[j][0], ends[j][1], ag_s.at[inst, i, j], ag_r.at[inst, i, j], ends[j][2])

        return copy

    def ag_start(buf, inst, i, src=None):
        c = ag_copies(buf, inst, i, src)
        c(0).start()
        c(1).start()

    def ag_fwd(buf, inst, i):
        c = ag_copies(buf, inst, i)
        c(0).wait_recv()
        c(2).start()
        c(1).wait_recv()
        c(3).start()

    def ag_done(buf, inst, i):
        c = ag_copies(buf, inst, i)
        c(2).wait_recv()
        c(3).wait_recv()

    def ag_drain(buf, inst):
        for i in range(CHUNKS):
            c = ag_copies(buf, inst, i)
            for j in range(4):
                c(j).wait_send()

    def ag(buf, inst, src=None, between=lambda i: None):
        ag_start(buf, inst, 0, src)
        ag_start(buf, inst, 1, src)
        for i in range(CHUNKS):
            ag_fwd(buf, inst, i)
            if i + 2 < CHUNKS:
                ag_start(buf, inst, i + 2, src)
            between(i)
        for i in range(CHUNKS):
            ag_done(buf, inst, i)
        ag_drain(buf, inst)

    def rs_copies(inst, i):
        ends = ((s1.at[i, 0:2], r1.at[i, 0:2], dev_y), (s1.at[i, 2:4], r1.at[i, 2:4], dev_z),
                (s2.at[i, 0], r2.at[i, 0], dev_z), (s2.at[i, 1], r2.at[i, 1], dev_y))

        def copy(j):
            return send(ends[j][0], ends[j][1], rs_s.at[inst, i, j], rs_r.at[inst, i, j], ends[j][2])

        return copy

    def rs_send(inst, i, dest):
        c = rs_copies(inst, i)
        step = L // 4

        def part(j):
            def rows(q):
                return pl.ds(pl.multiple_of(q * L + j * step, step), step)

            here = mul_of(j, step)
            s1[i, 0, here] = acc[rows(t_y), 0:HW].astype(bf16)
            s1[i, 1, here] = acc[rows(t_d), 0:HW].astype(bf16)
            s1[i, 2, here] = acc[rows(t_z), HW:CW].astype(bf16)
            s1[i, 3, here] = acc[rows(t_d), HW:CW].astype(bf16)
            k2[i, 0, here] = acc[rows(t_z), 0:HW]
            k2[i, 1, here] = acc[rows(t_y), HW:CW]
            dest[here, i * CW:(i + 1) * CW] = acc[rows(t), :]

        loop(4, part)
        c(0).start()
        c(1).start()

    def rs_fwd(inst, i, dest):
        c = rs_copies(inst, i)
        c(0).wait_recv()
        s2[i, 0] = (k2[i, 0] + r1[i, 1].astype(f32)).astype(bf16)
        c(2).start()
        c(1).wait_recv()
        s2[i, 1] = (k2[i, 1] + r1[i, 3].astype(f32)).astype(bf16)
        c(3).start()
        dest[:, i * CW:i * CW + HW] += r1[i, 0].astype(f32)
        dest[:, i * CW + HW:(i + 1) * CW] += r1[i, 2].astype(f32)

    def rs_done(inst, i, dest):
        c = rs_copies(inst, i)
        c(2).wait_recv()
        c(3).wait_recv()
        dest[:, i * CW:i * CW + HW] += r2[i, 0].astype(f32)
        dest[:, i * CW + HW:(i + 1) * CW] += r2[i, 1].astype(f32)

    def rs_drain(inst):
        for i in range(CHUNKS):
            c = rs_copies(inst, i)
            for j in range(4):
                c(j).wait_send()

    def rs(inst, dest, compute, between=lambda i: None):
        for i in range(CHUNKS):
            compute(i)
            rs_send(inst, i, dest)
        for i in range(CHUNKS):
            between(i)
            rs_fwd(inst, i, dest)
        between(CHUNKS)
        for i in range(CHUNKS):
            rs_done(inst, i, dest)
        rs_drain(inst)

    def split_place(half):
        return lambda s_, piece: s_ * half + piece * (half // 2)

    def down_place(s_, piece):
        return (piece * 2 + s_) * (d.his * d.unit)

    tables = (
        (wqkv_h, wqkv, split_place(D // 2), D // 4),
        (wo_h, wo, split_place(HD), HD // 2),
        (wgu_h, wgu, split_place(D // 2), D // 4),
        (wd_h, wd, down_place, d.his * d.unit),
    )

    def w_local(k, piece):
        src, buf, place, n = tables[k]
        return pltpu.make_async_copy(
            src.at[pl.ds(piece * n, n)], buf.at[pl.ds(pl.multiple_of(place(s, piece), n), n)], loc.at[k, piece])

    def w_cross(k):
        src, buf, place, n = tables[k]
        return send(src.at[mul_of(core, n)], buf.at[pl.ds(pl.multiple_of(place(s, core), n), n)],
                    w_s.at[k], w_r.at[k], dev_x)

    def w_share(k):
        _, buf, place, n = tables[k]
        here = buf.at[pl.ds(pl.multiple_of(place(1 - s, core), n), n)]
        return send(here, here, wf_s.at[k], wf_r.at[k], dev_c)

    own_x = pltpu.make_async_copy(x_h, xall.at[blk(t)], loc.at[4, 0])
    own_cot = pltpu.make_async_copy(cot_h, cot, loc.at[4, 1])
    own_gain = pltpu.make_async_copy(gain_v, gbuf.at[s], loc.at[5, 0])
    far_gain = send(gain_v, gbuf.at[s], w_s.at[4], w_r.at[4], dev_x)
    own_x.start()
    far_gain.start()
    w_cross(0).start()
    ag_start(xall, 0, 0, x_h)
    ag_start(xall, 0, 1, x_h)
    own_gain.start()
    for k in range(4):
        if k:
            w_cross(k).start()
        w_local(k, 0).start()
        w_local(k, 1).start()
    own_cot.start()

    def w_forward(k):
        w_cross(k).wait_recv()
        w_share(k).start()

    def w_ready(k):
        w_local(k, 0).wait()
        w_local(k, 1).wait()
        w_share(k).wait_recv()

    for i in range(CHUNKS):
        ag_fwd(xall, 0, i)
        if i + 2 < CHUNKS:
            ag_start(xall, 0, i + 2, x_h)
    w_forward(0)
    own_x.wait()
    own_gain.wait()
    far_gain.wait_recv()
    for q in range(2):
        gat[:, q * (D // 2):(q + 1) * (D // 2)] = gbuf[q, :, 2 * HD:2 * HD + D // 2]
        gml[:, q * (D // 2):(q + 1) * (D // 2)] = gbuf[q, :, 2 * HD + D // 2:]
    gsum[...] = jnp.zeros_like(gsum)
    for i in range(CHUNKS):
        ag_done(xall, 0, i)
    ag_drain(xall, 0)
    w_ready(0)
    w_forward(1)

    qk[:, 0:ha] = dot_nn(xall[...], wqkv[:, 0:ha])
    qk[:, ha:2 * ha] = dot_nn(xall[...], wqkv[:, ha:2 * ha])
    vb[...] = dot_nn(xall[...], wqkv[:, 2 * ha:]).astype(bf16)

    row8 = lax.broadcasted_iota(jnp.int32, (8, 2 * ha), 0)
    col8 = lax.broadcasted_iota(jnp.int32, (8, 2 * ha), 1)
    pick = jnp.where((row8 < 4) == (col8 < ha), 1.0, 0.0).astype(f32)
    HIGH = lax.Precision.HIGHEST

    def stat_sum(k, values):
        def part(b):
            stat[k, :, blk(b)] = dot_nt(pick, values(blk(b)), HIGH)

        loop(TP, part)
        copies = [send(stat.at[k], statr.at[k, j], st_s.at[k, j], st_r.at[k, j], dev)
                  for j, dev in enumerate((dev_y, dev_z, dev_d))]
        for c in copies:
            c.start()
        for c in copies:
            c.wait_recv()
        for c in copies:
            c.wait_send()
        return stat[k] + statr[k, 0] + statr[k, 1] + statr[k, 2]

    def squares(rows):
        v = qk[rows, :]
        return v * v

    stat[2] = lax.rsqrt(stat_sum(0, squares) / d.att + eps_norm)

    def columns(k, b):
        flat = stat[k, :, blk(b)]
        wide = jnp.concatenate([flat] * (L // 8), axis=0).T
        return wide[:, 0:1], wide[:, 4:5]

    def gain_of(which, h):
        return gbuf[h, :, which * HD:(which + 1) * HD]

    inv = 1.0 / math.sqrt(HD)
    heads = ha // HD

    def attend(b):
        rows = blk(b)
        scale = columns(2, b)
        cos, sin = cos_v[...], sin_v[...]
        above = lax.broadcasted_iota(jnp.int32, (L, L), 0) < lax.broadcasted_iota(jnp.int32, (L, L), 1)
        for h in range(heads):
            rot = []
            for which in range(2):
                at = pl.ds(which * ha + h * HD, HD)
                normed = qk[rows, at] * scale[which] * gain_of(which, h)
                turned = (normed * cos + pltpu.roll(normed, HD // 2, 1) * sin).astype(bf16)
                qkrot[rows, at] = turned
                rot.append(turned)
            scores = jnp.where(above, -jnp.inf, dot_nt(rot[0], rot[1]) * inv)
            peak = jnp.max(scores, axis=-1, keepdims=True)
            log_total = peak + jnp.log(jnp.sum(jnp.exp(scores - peak), axis=-1, keepdims=True))
            p = jnp.exp(scores - log_total)
            probs[b * heads + h] = p
            head = pl.ds(h * HD, HD)
            mixed[rows, head] = dot_nn(p.astype(bf16), vb[rows, head]).astype(bf16)

    loop(TP, attend)
    w_ready(1)

    def attn_chunk(i):
        acc[...] = dot_nn(mixed[...], wo[:, i * CW:(i + 1) * CW])

    rs(0, abuf, attn_chunk)

    BL = 16

    def residual_rows(j):
        rows = mul_of(j, BL)
        a = abuf[rows, :]
        scale = lax.rsqrt(jnp.mean(a * a, axis=-1, keepdims=True) + eps_norm)
        xr = xall[pl.ds(pl.multiple_of(t * L + j * BL, BL), BL), :].astype(f32)
        res = xr + a * scale * gat[...]
        cbuf[rows, :] = res
        rall[pl.ds(pl.multiple_of(t * L + j * BL, BL), BL), :] = res.astype(bf16)

    loop(L // BL, residual_rows)
    ag(rall, 1)
    w_forward(2)
    w_ready(2)

    NT = 256

    def gate_up(n):
        g_at, u_at = mul_of(n, NT), pl.ds(pl.multiple_of(fh + n * NT, NT), NT)
        gu[:, g_at] = dot_nn(rall[...], wgu[:, g_at])
        gu[:, u_at] = dot_nn(rall[...], wgu[:, u_at])

        def rows_of(j):
            rows = mul_of(j, 64)
            g, u = gu[rows, g_at], gu[rows, u_at]
            hid[rows, g_at] = (g * jax.nn.sigmoid(g) * u).astype(bf16)

        loop(T // 64, rows_of)

    loop(fh // NT, gate_up)
    w_forward(3)
    w_ready(3)

    def down_chunk(i):
        acc[...] = dot_nn(hid[...], wd[:, i * CW:(i + 1) * CW])

    rs(1, bbuf, down_chunk)
    own_cot.wait()

    def output_rows(j):
        rows = mul_of(j, BL)
        dn = bbuf[rows, :]
        scale = lax.rsqrt(jnp.mean(dn * dn, axis=-1, keepdims=True) + eps_norm)
        outb[rows, :] = (cbuf[rows, :] + dn * scale * gml[...]).astype(bf16)
        co = cot[rows, :].astype(f32)
        weighted = co * gml[...]
        inner = jnp.mean(weighted * dn, axis=-1, keepdims=True)
        gd = scale * weighted - dn * scale**3 * inner
        gdall[pl.ds(pl.multiple_of(t * L + j * BL, BL), BL), :] = gd.astype(bf16)
        gsum[:, D:2 * D] += jnp.sum(co * dn * scale, axis=0, keepdims=True)

    loop(L // BL, output_rows)
    put_out = pltpu.make_async_copy(outb, out_h, loc.at[5, 1])
    put_out.start()
    ag(gdall, 2)

    def hidden_back(n):
        g_at, u_at = mul_of(n, NT), pl.ds(pl.multiple_of(fh + n * NT, NT), NT)
        acc[:, 0:NT] = dot_nt(gdall[...], wd[mul_of(n, NT), :])

        def rows_of(j):
            rows = mul_of(j, 64)
            g, u, gh = gu[rows, g_at], gu[rows, u_at], acc[rows, 0:NT]
            sig = jax.nn.sigmoid(g)
            gg2[rows, g_at] = (gh * u * sig * (1.0 + g * (1.0 - sig))).astype(bf16)
            gg2[rows, u_at] = (gh * (g * sig)).astype(bf16)

        loop(T // 64, rows_of)

    loop(fh // NT, hidden_back)

    def res_chunk(i):
        acc[...] = dot_nt(gg2[...], wgu[i * CW:(i + 1) * CW, :])

    rs(2, cbuf, res_chunk)

    def attn_grad_rows(j):
        rows = mul_of(j, BL)
        gr = cbuf[rows, :] + cot[rows, :].astype(f32)
        cbuf[rows, :] = gr
        a = abuf[rows, :]
        scale = lax.rsqrt(jnp.mean(a * a, axis=-1, keepdims=True) + eps_norm)
        weighted = gr * gat[...]
        inner = jnp.mean(weighted * a, axis=-1, keepdims=True)
        ga = scale * weighted - a * scale**3 * inner
        gaall[pl.ds(pl.multiple_of(t * L + j * BL, BL), BL), :] = ga.astype(bf16)
        gsum[:, 0:D] += jnp.sum(gr * a * scale, axis=0, keepdims=True)

    loop(L // BL, attn_grad_rows)
    ag(gaall, 3)

    acc[:, 0:ha] = dot_nt(gaall[...], wo[...])

    def attend_back(b):
        rows = blk(b)
        scale = columns(2, b)
        cos, sin = cos_v[...], sin_v[...]
        for h in range(heads):
            head = pl.ds(h * HD, HD)
            gm = acc[rows, head].astype(bf16)
            p = probs[b * heads + h]
            gqkv[rows, pl.ds(2 * ha + h * HD, HD)] = dot_tn(p.astype(bf16), gm).astype(bf16)
            gp = dot_nt(gm, vb[rows, head])
            gs = p * (gp - jnp.sum(p * gp, axis=-1, keepdims=True))
            gs = (gs * inv).astype(bf16)
            turned = (dot_nn(gs, qkrot[rows, pl.ds(ha + h * HD, HD)]), dot_tn(gs, qkrot[rows, head]))
            for which in range(2):
                at = pl.ds(which * ha + h * HD, HD)
                gn = turned[which] * cos - pltpu.roll(turned[which], HD // 2, 1) * sin
                field = qk[rows, at]
                spot = pl.ds(pl.multiple_of(2 * D + which * d.att + t * ha + h * HD, HD), HD)
                gsum[:, spot] += jnp.sum(gn * field * scale[which], axis=0, keepdims=True)
                gu[rows, at] = gn * gain_of(which, h)

    loop(TP, attend_back)

    def products(rows):
        return gu[rows, 0:2 * ha] * qk[rows, :]

    stat[3] = stat_sum(1, products) / d.att

    def qk_back(b):
        rows = blk(b)
        scale, inner = columns(2, b), columns(3, b)
        for which in range(2):
            at = pl.ds(which * ha, ha)
            sc = scale[which]
            gqkv[rows, at] = (sc * gu[rows, at] - qk[rows, at] * (sc**3 * inner[which])).astype(bf16)

    loop(TP, qk_back)

    def in_chunk(i):
        acc[...] = dot_nt(gqkv[...], wqkv[i * CW:(i + 1) * CW, :])

    rs(3, bbuf, in_chunk)

    def input_rows(j):
        rows = mul_of(j, BL)
        bbuf[rows, :] += cbuf[rows, :]

    loop(L // BL, input_rows)
    put_gin = pltpu.make_async_copy(bbuf, gin_h, loc.at[6, 0])
    put_gin.start()

    half_q = 3 * ha // 2

    def left_of(ref):
        return lambda row, n: ref[:, pl.ds(pl.multiple_of(row, n), n)]

    def by_cols(left, right, width):
        def make(row, n, core_):
            return dot_tn(left(row, n), right[:, mul_of(core_, width)])
        return make

    def by_rows(left, right, height):
        def make(row, n, core_):
            return dot_tn(left(core_ * height + row, n), right[...])
        return make

    sets = (
        (by_rows(left_of(hid), gdall, fh // 2), rc_d, rx_d, rh_d, fh // 2, 128),
        (by_cols(left_of(rall), gg2, fh), rc_gu, rx_gu, rh_gu, D, 256),
        (by_cols(left_of(xall), gqkv, half_q), rc_q, rx_q, rh_q, D, 256),
        (by_cols(left_of(mixed), gaall, D // 2), rc_o, rx_o, None, ha, 128),
    )
    top = hi // max(d.his // 2, 1)

    def tile_row(k, j):
        rows, n = sets[k][4], sets[k][5]
        tiles = rows // 2 // n
        if k == 3 or tiles < 2:
            return j * n
        return ((j + (1 - top) * (tiles // 2)) % tiles) * n

    def core_copy(k, row, slot):
        buf, n = sets[k][1], sets[k][5]
        dst = buf.at[pl.ds(pl.multiple_of(row, n), n)]
        return send(stage_view(k, slot), dst, stg_s.at[slot], c_r.at[k, row // n], dev_c)

    def stage_view(k, slot):
        buf, n = sets[k][1], sets[k][5]
        return stage.at[slot, 0:n, 0:buf.shape[1]]

    def order(k):
        rows, n = sets[k][4], sets[k][5]
        half = rows // 2
        tiles = half // n
        out = [(1 - s) * half + tile_row(k, j) for j in range(tiles)]
        return out + [s * half + tile_row(k, j) for j in range(tiles)]

    slots = stage.shape[0]
    used = [0]

    def give(k):
        for row in order(k):
            slot = used[0] % slots
            c = core_copy(k, row, slot)
            if used[0] >= slots:
                c_prev = pending[used[0] - slots]
                c_prev.wait_send()
            n = sets[k][5]
            w = sets[k][1].shape[1]
            stage[slot, 0:n, 0:w] = sets[k][0](row, n, 1 - core).astype(bf16)
            c.start()
            pending.append(c)
            used[0] += 1

    pending = []

    def x_copy(k, j):
        buf, far, n = sets[k][1], sets[k][2], sets[k][5]
        half = sets[k][4] // 2
        row = tile_row(k, j)
        src = buf.at[pl.ds(pl.multiple_of((1 - s) * half + row, n), n)]
        return send(src, far.at[pl.ds(pl.multiple_of(row, n), n)], x_s.at[k, j], x_r.at[k, j], dev_x)

    def own_tile(k, row):
        buf, n = sets[k][1], sets[k][5]
        rows = pl.ds(pl.multiple_of(row, n), n)
        core_copy(k, row, 0).wait_recv()
        buf[rows, :] = (sets[k][0](row, n, core) + buf[rows, :].astype(f32)).astype(bf16)

    def take(k):
        rows, n = sets[k][4], sets[k][5]
        half = rows // 2
        tiles = half // n
        for j in range(tiles):
            own_tile(k, (1 - s) * half + tile_row(k, j))
            x_copy(k, j).start()
        for j in range(tiles):
            own_tile(k, s * half + tile_row(k, j))

    def x_add(k, j):
        buf, far, n = sets[k][1], sets[k][2], sets[k][5]
        half = sets[k][4] // 2
        row = tile_row(k, j)
        rows = pl.ds(pl.multiple_of(s * half + row, n), n)
        x_copy(k, j).wait_recv()
        buf[rows, :] = (buf[rows, :].astype(f32) + far[pl.ds(pl.multiple_of(row, n), n), :].astype(f32)).astype(bf16)

    def hi_parts(k):
        half = sets[k][4] // 2
        parts = []
        base, size, at = 0, half, 0
        for level in range(d.levels):
            size //= 2
            weight = d.his >> (level + 1)
            bit = (hi // weight) % 2
            parts.append((level, base + (1 - bit) * size, base + bit * size, size, at, hi + weight * (1 - 2 * bit)))
            base = base + bit * size
            at += size
        return parts, base, size

    def hi_copy(k, part):
        level, far_row, _, size, at, other = part
        half = sets[k][4] // 2
        src = sets[k][1].at[pl.ds(pl.multiple_of(s * half + far_row, size), size)]
        return send(src, sets[k][3].at[pl.ds(at, size)], h_s.at[k, level], h_r.at[k, level], (s, rep(other, t, core)))

    def hi_add(k, part, final=None):
        level, _, row, size, at, _ = part
        half = sets[k][4] // 2
        hi_copy(k, part).wait_recv()
        n = min(size, 64)

        def step(j):
            rows = pl.ds(pl.multiple_of(s * half + row + j * n, n), n)
            total = sets[k][1][rows, :].astype(f32) + sets[k][3][pl.ds(pl.multiple_of(at + j * n, n), n), :].astype(f32)
            if final is None:
                sets[k][1][rows, :] = total.astype(bf16)
            else:
                final[mul_of(j, n), :] = total

        loop(size // n, step)

    def a2a_copies(k, p):
        half = sets[k][4] // 2
        _, base, size = hi_parts(k)
        src = sets[k][1].at[pl.ds(pl.multiple_of(s * half + base + p * d.own, d.own), d.own)]
        dst = (gu_h if k == 1 else qkv_h).at[t * CORES + core]
        return src, dst

    me = t * CORES + core

    def a2a_start(k):
        for p in range(TP * CORES):
            src, dst = a2a_copies(k, p)

            @pl.when(me != p)
            def _():
                send(src, dst, a_s.at[k - 1, p], a_r.at[k - 1, me], (s, rep(hi, p // CORES, p % CORES))).start()

            @pl.when(me == p)
            def _():
                pltpu.make_async_copy(src, dst, a_r.at[k - 1, me]).start()

    def a2a_wait(k):
        for p in range(TP * CORES):
            src, _ = a2a_copies(k, p)
            target = (gu_h if k == 1 else qkv_h).at[p]
            pltpu.make_async_copy(src, target, a_r.at[k - 1, p]).wait()

            @pl.when(me != p)
            def _():
                send(src, target, a_s.at[k - 1, p], a_r.at[k - 1, me], (s, rep(hi, p // CORES, p % CORES))).wait_send()

    for k in range(4):
        give(k)
    for k in range(4):
        take(k)
    for c in pending[-slots:]:
        c.wait_send()
    for k in range(4):
        for j in range(sets[k][4] // 2 // sets[k][5]):
            x_add(k, j)
    parts = [hi_parts(k)[0] for k in range(3)]
    for level in range(d.levels):
        for k in range(3):
            hi_copy(k, parts[k][level]).start()
        for k in range(3):
            last = k == 0 and level == d.levels - 1
            hi_add(k, parts[k][level], abuf if last else None)
    if not d.levels:
        abuf[0:d.unit, :] = rc_d[pl.ds(pl.multiple_of(s * d.unit, d.unit), d.unit), :].astype(f32)
    put_down = pltpu.make_async_copy(abuf.at[0:d.unit], down_h, loc.at[6, 1])
    put_down.start()
    a2a_start(1)
    a2a_start(2)

    for p in range(d.pieces):
        o_pc[p] = rc_o[pl.ds(pl.multiple_of(s * HD + p * d.own_o, d.own_o), d.own_o), :]
    o_slot = hi * CORES + core
    for p in range(d.pieces):
        goal = t * d.pieces + p

        @pl.when(goal != r)
        def _():
            send(o_pc.at[p], o_h.at[o_slot], o_s.at[p], o_r.at[o_slot], (s, goal)).start()

        @pl.when(goal == r)
        def _():
            pltpu.make_async_copy(o_pc.at[p], o_h.at[o_slot], o_r.at[o_slot]).start()

    partners = [dev_c, dev_x]
    for level in range(d.levels):
        weight = d.his >> (level + 1)
        bit = (hi // weight) % 2
        partners.append((s, rep(hi + weight * (1 - 2 * bit), t, core)))
    partners += [dev_y, dev_z]
    for n, dev in enumerate(partners):
        c = send(gsum, grecv.at[n], gn_s.at[n], gn_r.at[n], dev)
        c.start()
        c.wait_send()
        c.wait_recv()
        gsum[...] += grecv[n]
    gg_o[...] = gsum[...]

    a2a_wait(1)
    a2a_wait(2)
    for q in range(d.his * CORES):
        pltpu.make_async_copy(o_pc.at[0], o_h.at[q], o_r.at[q]).wait()
    for p in range(d.pieces):
        goal = t * d.pieces + p

        @pl.when(goal != r)
        def _():
            send(o_pc.at[p], o_h.at[o_slot], o_s.at[p], o_r.at[o_slot], (s, goal)).wait_send()

    far_gain.wait_send()
    for k in range(4):
        w_cross(k).wait_send()
        w_share(k).wait_send()
        for j in range(sets[k][4] // 2 // sets[k][5]):
            x_copy(k, j).wait_send()
    for k in range(3):
        for part in parts[k]:
            hi_copy(k, part).wait_send()
    put_out.wait()
    put_gin.wait()
    put_down.wait()


def body(shards, replicas, x_in, cotangent, w_query, w_key, w_value, w_out, w_gate, w_up, w_down,
         gain_query, gain_key, gain_attn, gain_mlp):
    seqs, length, width = x_in.shape
    assert seqs == 1
    d = Dims(length, width, w_query.shape[1], w_gate.shape[1], shards, replicas)
    r = lax.axis_index("replica")
    s = lax.axis_index("shard")
    t = (r // CORES) % TP

    def at(array, axis, index):
        return lax.dynamic_index_in_dim(array, index, axis, keepdims=False)

    def head_cols(w):
        return at(w.reshape(w.shape[0], d.S, TP, HD), 2, t).reshape(w.shape[0], d.ha)

    def hidden_cols(w):
        picked = at(w.reshape(w.shape[0], d.S, d.his, TP, CORES, d.unit), 3, t)
        return picked.transpose(0, 3, 1, 2, 4).reshape(w.shape[0], d.fh)

    wqkv = jnp.concatenate([head_cols(w_query), head_cols(w_key), head_cols(w_value)], axis=1)
    wo = at(w_out.reshape(TP, HD, width), 0, t)
    wgu = jnp.concatenate([hidden_cols(w_gate), hidden_cols(w_up)], axis=1)
    wd = at(w_down.reshape(d.his, TP, CORES, d.unit, width), 1, t).transpose(1, 0, 2, 3).reshape(-1, width)
    gain = jnp.concatenate([at(gain_query.reshape(TP, HD), 0, t), at(gain_key.reshape(TP, HD), 0, t),
                            gain_attn, gain_mlp]).astype(f32)[None]
    cos, sin = rope_tables(length, HD // 2)
    cos = jnp.concatenate([cos, cos], axis=1)
    sin = jnp.concatenate([-sin, sin], axis=1)

    L, D, T, ha, fh = d.L, d.D, d.T, d.ha, d.fh
    CW = D // CHUNKS
    vm = pltpu.VMEM
    dma = pltpu.SemaphoreType.DMA
    any_ = pl.BlockSpec(memory_space=pl.ANY)
    vmem = pl.BlockSpec(memory_space=pltpu.VMEM)
    hi_rows = lambda n: max(n - n // d.his, 16)
    steps = 4 + d.levels
    scratch = [
        vm((D, 3 * ha), bf16), vm((ha, D), bf16), vm((D, 2 * fh), bf16), vm((fh, D), bf16),
        vm((2, 1, d.gains), f32), vm((1, D), f32), vm((1, D), f32),
        vm((T, D), bf16), vm((T, D), bf16), vm((T, D), bf16), vm((T, D), bf16), vm((L, D), bf16),
        vm((T, 2 * ha), f32), vm((T, ha), bf16), vm((T, 2 * ha), bf16), vm((TP * ha // HD, L, L), f32),
        vm((T, ha), bf16), vm((T, 3 * ha), bf16), vm((4, 8, T), f32), vm((2, 3, 8, T), f32),
        vm((T, 2 * fh), f32), vm((T, fh), bf16), vm((T, 2 * fh), bf16),
        vm((L, D), f32), vm((L, D), f32), vm((L, D), f32), vm((L, D), bf16),
        vm((T, CW), f32), vm((CHUNKS, 4, L, CW // 2), bf16), vm((CHUNKS, 2, L, CW // 2), bf16),
        vm((CHUNKS, 4, L, CW // 2), bf16), vm((CHUNKS, 2, L, CW // 2), bf16), vm((CHUNKS, 2, L, CW // 2), f32),
        vm((2, 256, D), bf16),
        vm((D, fh), bf16), vm((fh // 2, D), bf16), vm((D, 3 * ha // 2), bf16), vm((ha, D // 2), bf16),
        vm((D // 2, fh), bf16), vm((fh // 4, D), bf16), vm((D // 2, 3 * ha // 2), bf16), vm((ha // 2, D // 2), bf16),
        vm((hi_rows(D // 2), fh), bf16), vm((hi_rows(fh // 4), D), bf16), vm((hi_rows(D // 2), 3 * ha // 2), bf16),
        vm((d.pieces, d.own_o, D // 2), bf16),
        vm((1, d.ggs), f32), vm((steps, 1, d.ggs), f32),
        dma((4, CHUNKS, 4)), dma((4, CHUNKS, 4)), dma((4, CHUNKS, 4)), dma((4, CHUNKS, 4)),
        dma((5,)), dma((5,)), dma((4,)), dma((4,)), dma((7, 2)), dma((2, 3)), dma((2, 3)),
        dma((2,)), dma((4,)), dma((4, 8)), dma((4, 4)), dma((4, 4)),
        dma((3, max(d.levels, 1))), dma((3, max(d.levels, 1))),
        dma((2, TP * CORES)), dma((2, TP * CORES)), dma((d.pieces,)), dma((d.his * CORES,)), dma((steps,)), dma((steps,)),
    ]
    struct = jax.ShapeDtypeStruct
    results = pl.pallas_call(
        functools.partial(kernel, d),
        out_shape=(
            struct((L, D), bf16), struct((L, D), f32), struct((TP * CORES, d.own, fh), bf16),
            struct((TP * CORES, d.own, 3 * ha // 2), bf16), struct((d.unit, D), f32),
            struct((d.his * CORES, d.own_o, D // 2), bf16), struct((1, d.ggs), f32),
        ),
        in_specs=[any_] * 6 + [vmem] * 3,
        out_specs=(any_,) * 6 + (vmem,),
        scratch_shapes=scratch,
        compiler_params=pltpu.CompilerParams(
            collective_id=0, has_side_effects=True, vmem_limit_bytes=67043328),
        name="layer",
    )(x_in[0], cotangent[0], wqkv, wo, wgu, wd, gain, cos, sin)
    out, gin, gu, qkv, down, o, gg = results

    def hidden_out(block):
        spread = block.reshape(TP, d.own, CORES, d.S, d.his, d.unit).transpose(1, 3, 4, 0, 2, 5)
        return spread.reshape(d.own, d.ff).astype(f32)

    gu = gu.reshape(TP, CORES, d.own, fh)
    qkv = qkv.reshape(TP, CORES, d.own, 3, HD).transpose(2, 1, 3, 0, 4).reshape(d.own, 3, d.S, TP, HD)

    def head_out(k):
        return qkv[:, k].reshape(d.own, d.att).astype(f32)

    o = o.reshape(d.his, CORES, d.own_o, D // 2).astype(f32).sum(0).transpose(1, 0, 2).reshape(d.own_o, D)
    gg = gg[0]
    here = s * d.R + r

    def share(vec):
        n = vec.shape[0] // (d.S * d.R)
        return lax.dynamic_slice_in_dim(vec, here * n, n)

    def head_gain(vec):
        return share(vec.reshape(TP, d.S, HD).transpose(1, 0, 2).reshape(-1))

    return (
        out[None], gin[None], head_out(0), head_out(1), head_out(2), o,
        hidden_out(gu[:, 0]), hidden_out(gu[:, 1]), down,
        head_gain(gg[2 * D:2 * D + d.att]), head_gain(gg[2 * D + d.att:]), share(gg[:D]), share(gg[D:2 * D]),
    )


def solution(mesh):
    both = ("shard", "replica")
    token = P(both, None, None)
    weight = P("shard", None)
    return jax.shard_map(
        functools.partial(body, mesh.shape["shard"], mesh.shape["replica"]),
        mesh=mesh,
        in_specs=(token, token) + (weight,) * 7 + (P("shard"),) * 4,
        out_specs=(token, token) + (P(both, None),) * 7 + (P(both),) * 4,
        check_vma=False,
    )
```

time: 1000 us -> 535 us (0.54)
  waiting for transfers between devices: 685 us -> 0 us
  Pallas kernels: 0 us -> 428 us
  matrix products: 73.1 us -> 0 us
  blocking collectives: 70.1 us -> 0 us
  other arithmetic: 35 us -> 9.15 us
  local copies, waits for them, and re-layouts: 107 us -> 89.7 us
  between operations: 15.2 us -> 1.39 us
    reduce_scatter x8 -> x0, waiting for transfers between devices: 444 us -> none  [the longest x4 127 us: scatter(): lax.psum_scatter(partial.astype(bf16), 't', scatter_dimension=0, tiled=True)]
    pallas_call x0 -> x1, Pallas kernels: none -> 428 us  [body(): pl.pallas_call(functools.partial(kernel, d), out_shape=(struct((L, D), bf...]
    all_gather x8 -> x0, waiting for transfers between devices: 241 us -> none  [the longest x4 115 us: whole(): return lax.all_gather(piece, ('shard', 'core'), axis=0, tiled=True)]
    dot_general x18 -> x0, matrix products: 73.1 us -> none  [the longest x4 23.8 us: matmul_nt(): lax.dot_general(left, right, (((1,), (1,)), ((), ())), preferred_element_...]
    unnamed x102 -> x26, local copies, waits for them, and re-layouts: 51.8 us -> 3.04 us
    unnamed x1 -> x0, blocking collectives: 46.3 us -> none
    reshape x19 -> x11, local copies, waits for them, and re-layouts: 22.7 us -> 46.5 us  [the longest x2 28.6 us: hidden_cols(): picked = at(w.reshape(w.shape[0], d.S, d.his, TP, CORES, d.unit), 3, t)]
    dynamic_slice x5 -> x8, local copies, waits for them, and re-layouts: 6.89 us -> 26.5 us  [at(): return lax.dynamic_index_in_dim(array, index, axis, keepdims=False)]
  transfers between devices with their start and end apart: 18 -> 0, of which waited for: 14 -> 0; matrix products, arithmetic and copies ran while one was open for 13% -> 0% of each run, Pallas kernels for 0% -> 0%
where the time goes in v2:
time: 535 us; the launch traced here: 528 us
  Pallas kernels  428 us (80%)
  local copies, waits for them, and re-layouts  89.7 us (17%)
  other arithmetic  9.15 us (2%)
    pallas_call x1, Pallas kernels, body(): pl.pallas_call(functools.partial(kernel, d), out_shape=(struct((L, D), bf...  428 us
    reshape x2, local copies, waits for them, and re-layouts, hidden_cols(): picked = at(w.reshape(w.shape[0], d.S, d.his, TP, CORES, d.unit), 3, t)  28.6 us
    dynamic_slice x8, local copies, waits for them, and re-layouts, at(): return lax.dynamic_index_in_dim(array, index, axis, keepdims=False)  26.5 us
    reshape x3, local copies, waits for them, and re-layouts, head_cols(): w.reshape(w.shape[0], d.S, TP, HD)  11.5 us

profile of v2, /device:TPU:0, one launch (start us, length us, event | category | flops | bytes accessed | tf_op | source)
XLA Modules:
  0.0 527.8 jit_solution(3899266431323323648)
XLA Ops:
  0.7 14.3 %reshape.194 = bf16[1024,2,2,4,2,128]{5,4,3,2,1,0:T(2,128)(2,1)} reshape(bf16[1024,4096]{1,0:T(8,128)(2,1)} %param.19) | data formatting | bytes 16777216 | tf_op jit(solution)/shard_map/reshape | solution.py:773
  15.0 14.3 %reshape.196 = bf16[1024,2,2,4,2,128]{5,4,3,2,1,0:T(2,128)(2,1)} reshape(bf16[1024,4096]{1,0:T(8,128)(2,1)} %param.20) | data formatting | bytes 16777216 | tf_op jit(solution)/shard_map/reshape | solution.py:773
  29.3 6.4 %constant_dynamic-slice_fusion.5 = (bf16[1024,2,2,1,2,128]{5,4,3,2,1,0:T(2,128)(2,1)}, bf16[1024,2,2,1,2,128]{5,4,3,2,1,0:T(2,128)(2,1)S(1)}) fusion(bf16[1024,2,2,4,2,128]{5,4,3,2,1,0:T(2,128)(2,1)} %reshape.196, s32[]{:T(128)S(6)} %select_n.37, bf16[1024,2,2,4,2,128]{5,4,3,2,1,0:T(2,128)(2,1)} %reshape.194), kind=kLoop, calls=%fused_computation.30 | loop fusion | bytes 8388612 | tf_op jit(solution)/shard_map/jit(dynamic_index_in_dim)/dynamic_slice | solution.py:767
  35.7 1.4 copy.103
  37.2 2.7 reshape.195
  39.9 3.0 copy.102
  42.9 2.8 reshape.197
  45.7 4.7 pad_maximum_fusion.wgu_h
  50.4 3.2 reshape.189
  53.6 4.6 reshape.191
  58.3 8.8 %dynamic-slice_reduce_fusion = (bf16[1024,2,128]{2,1,0:T(2,128)(2,1)S(1)}, bf16[1024,2,128]{2,1,0:T(2,128)(2,1)S(1)}) fusion(bf16[1024,2,4,128]{3,2,1,0:T(4,128)(2,1)} %reshape.191, s32[]{:T(128)S(6)} %select_n.37, bf16[1024,2,4,128]{3,2,1,0:T(4,128)(2,1)S(1)} %reshape.189), kind=kLoop, calls=%fused_computation.6 | loop fusion | bytes 2097156 | tf_op jit(solution)/shard_map/jit(dynamic_index_in_dim)/dynamic_slice | solution.py:767
  67.2 3.6 reshape.187
  70.9 3.6 dynamic-slice_reduce_fusion.2
  74.6 1.2 pad_maximum_fusion.1.wqkv_h
  75.8 1.7 constant_dynamic-slice_fusion.4
  77.6 1.5 copy.78
  79.1 0.6 maximum_convert_fusion.gain_v
  79.7 1.9 dynamic-slice_bitcast_fusion.wo_h
  81.9 0.8 pad_maximum_fusion.2
  82.7 427.5 %layer.1 = (bf16[128,2048]{1,0:T(8,128)(2,1)}, f32[128,2048]{1,0:T(8,128)}, bf16[8,64,1024]{2,1,0:T(8,128)(2,1)}, bf16[8,64,384]{2,1,0:T(8,128)(2,1)}, f32[128,2...) custom-call(bf16[128,2048]{1,0:T(8,128)(2,1)} %bitcast.89, bf16[128,2048]{1,0:T(8,128)(2,1)} %bitcast.90, ...), custom_call_target="tpu_custom_call" | custom-call | tf_op jit(solution)/shard_map/layer/pallas_call | solution.py:817
  510.2 1.4 slice_convert_fusion
  511.7 0.9 reshape.216
  513.1 1.8 reshape.214
  514.9 0.9 reshape.217
  516.4 1.8 reshape.215
  518.7 0.8 reshape.210
  519.7 0.8 reshape.211
  520.7 0.8 reshape.212
  521.5 0.7 copy.91
  524.6 0.8 copy.112
  525.4 1.0 copy.113
  526.4 1.0 copy.114
  (46 shorter events, 4.9 us)
Async XLA Ops:
  77.5 1.5 copy-start.8
  77.6 1.5 copy-start.9
  77.6 1.5 copy-start.6
  77.6 1.5 copy-start.7
  515.8 2.4 copy-start.3
  518.4 3.1 copy-start.4
  518.5 3.7 copy-start.5
  518.5 6.1 %copy-start.2 = (bf16[128,2048]{1,0:T(8,128)(2,1)S(1)}, bf16[128,2048]{1,0:T(8,128)(2,1)}, u32[]{:S(2)}) copy-start(bf16[128,2048]{1,0:T(8,128)(2,1)} %get-tuple-element.20) | copy-start | bytes 1572868
  519.5 5.9 %copy-start.1 = (f32[128,2048]{1,0:T(8,128)S(1)}, f32[128,2048]{1,0:T(8,128)}, u32[]{:S(2)}) copy-start(f32[128,2048]{1,0:T(8,128)} %get-tuple-element.21) | copy-start | bytes 3145732
  521.5 4.9 copy-start

commit v3 on v2

v3 whole, which is shorter than its diff:
```python
import functools
import math

import jax
import jax.numpy as jnp
import numpy as np
from jax import lax
from jax.experimental import pallas as pl
from jax.experimental.pallas import tpu as pltpu
from jax.sharding import PartitionSpec as P

HD = 128
TP = 4
CORES = 2
CHUNKS = 4

eps_norm = 1e-06
rope_theta = 500000.0

bf16 = jnp.bfloat16
f32 = jnp.float32


def rope_tables(length, half):
    position = np.arange(length).astype(np.float32)[:, None]
    exponent = np.arange(half).astype(np.float32) * np.float32(1.0 / half)
    angle = position * np.float32(rope_theta) ** (-exponent)
    return (np.cos(angle).astype(np.float32), np.sin(angle).astype(np.float32))


def dot_nn(left, right):
    return lax.dot_general(left, right, (((1,), (0,)), ((), ())), preferred_element_type=f32)


def dot_nt(left, right, precision=None):
    return lax.dot_general(
        left, right, (((1,), (1,)), ((), ())), preferred_element_type=f32, precision=precision)


def dot_tn(left, right):
    return lax.dot_general(left, right, (((0,), (0,)), ((), ())), preferred_element_type=f32)


def mul_of(index, step):
    return pl.ds(pl.multiple_of(index * step, step), step)


def loop(count, step, start=0):
    lax.fori_loop(start, count, lambda i, c: (step(i), c)[1], 0)


class Dims:
    def __init__(self, length, width, att, ff, shards, replicas):
        self.L, self.D, self.att, self.ff = length, width, att, ff
        self.S, self.R = shards, replicas
        self.his = replicas // (TP * CORES)
        self.T = TP * length
        self.ha = att // TP
        self.fh = ff // TP
        self.unit = ff // (shards * replicas)
        self.own = width // (shards * replicas)
        self.own_o = att // (shards * replicas)
        self.pieces = HD // self.own_o
        self.levels = self.his.bit_length() - 1
        self.gains = 2 * HD + width
        self.ggs = 2 * width + 2 * att
        self.direct = self.unit % 128 == 0
        assert shards == 2 and self.his == 1 << self.levels and self.levels > 0 and self.ha == shards * HD


def kernel(
    d,
    x_h, cot_h, wq_h, wk_h, wv_h, wo_h, wg_h, wu_h, wd_h, gain_v, cos_v, sin_v,
    out_h, gin_h, gu_h, qkv_h, down_h, o_h, gg_o,
    wqkv, wo, wgu, wd, gbuf, gat, gml,
    xall, rall, gdall, gaall, cot,
    qk, vb, qkrot, probs, mixed, gqkv, stat, statr,
    gu, hid, gg2,
    abuf, bbuf, cbuf, outb,
    acc, s1, s2, r1, r2, k2,
    stage_d, stage, rc_gu, rc_d, rc_q, rc_o, rx_gu, rx_d, rx_q, rx_o, rh_gu, rh_d, rh_q, o_pc,
    gsum, grecv,
    ag_s, ag_r, rs_s, rs_r, w_s, w_r, wf_s, wf_r, w_l, loc, st_s, st_r,
    stg_s, c_r, x_s, x_r, h0_s, h0_r, h_s, h_r, a_s, a_r, o_s, o_r, gn_s, gn_r,
):
    L, D, T, ha, fh, his, unit = d.L, d.D, d.T, d.ha, d.fh, d.his, d.unit
    CW = D // CHUNKS
    HW = CW // 2
    s = lax.axis_index("shard")
    r = lax.axis_index("replica")
    hi, t, core = r // (TP * CORES), (r // CORES) % TP, r % CORES
    tz, ty = t // 2, t % 2
    t_y, t_z, t_d = tz * 2 + 1 - ty, (1 - tz) * 2 + ty, (1 - tz) * 2 + 1 - ty

    def rep(hi_, t_, core_):
        return hi_ * (TP * CORES) + t_ * CORES + core_

    dev_y, dev_z, dev_d = ((s, rep(hi, q, core)) for q in (t_y, t_z, t_d))
    dev_x = (1 - s, r)
    dev_c = (s, rep(hi, t, 1 - core))

    def send(src, dst, ssem, rsem, dev):
        return pltpu.make_async_remote_copy(
            src_ref=src, dst_ref=dst, send_sem=ssem, recv_sem=rsem, device_id=dev,
            device_id_type=pl.DeviceIdType.MESH)

    def blk(q):
        return mul_of(q, L)

    def part(base, n):
        return pl.ds(pl.multiple_of(base, n), n)

    barrier = pltpu.get_barrier_semaphore()

    def greet(q):
        @pl.when(q != r)
        def _():
            pl.semaphore_signal(barrier, inc=1, device_id=(s, q), device_id_type=pl.DeviceIdType.MESH)

    loop(d.R, greet)
    pl.semaphore_signal(barrier, inc=1, device_id=dev_x, device_id_type=pl.DeviceIdType.MESH)
    pl.semaphore_wait(barrier, d.R)

    def ag_copies(buf, inst, i, src=None):
        own = buf.at[blk(t), mul_of(i, CW)]
        first = own if src is None else src.at[:, mul_of(i, CW)]
        ca, cb = mul_of(2 * i, HW), mul_of(2 * i + 1, HW)
        fy, fz = buf.at[blk(t_y), ca], buf.at[blk(t_z), cb]
        ends = ((first, own, dev_y), (first, own, dev_z), (fy, fy, dev_z), (fz, fz, dev_y))

        def copy(j):
            return send(ends[j][0], ends[j][1], ag_s.at[inst, i, j], ag_r.at[inst, i, j], ends[j][2])

        return copy

    def ag_start(buf, inst, i, src=None):
        c = ag_copies(buf, inst, i, src)
        c(0).start()
        c(1).start()

    def ag_fwd(buf, inst, i):
        c = ag_copies(buf, inst, i)
        c(0).wait_recv()
        c(2).start()
        c(1).wait_recv()
        c(3).start()

    def ag_done(buf, inst, i):
        c = ag_copies(buf, inst, i)
        c(2).wait_recv()
        c(3).wait_recv()

    def ag_drain(buf, inst):
        def wait(i):
            c = ag_copies(buf, inst, i)
            for j in range(4):
                c(j).wait_send()

        loop(CHUNKS, wait)

    def ag(buf, inst, src=None, between=lambda i: None):
        ag_start(buf, inst, 0, src)
        ag_start(buf, inst, 1, src)
        for i in range(CHUNKS):
            ag_fwd(buf, inst, i)
            if i + 2 < CHUNKS:
                ag_start(buf, inst, i + 2, src)
            between(i)
        for i in range(CHUNKS):
            ag_done(buf, inst, i)
        ag_drain(buf, inst)

    def rs_copies(inst, i):
        ends = ((s1.at[i, 0:2], r1.at[i, 0:2], dev_y), (s1.at[i, 2:4], r1.at[i, 2:4], dev_z),
                (s2.at[i, 0], r2.at[i, 0], dev_z), (s2.at[i, 1], r2.at[i, 1], dev_y))

        def copy(j):
            return send(ends[j][0], ends[j][1], rs_s.at[inst, i, j], rs_r.at[inst, i, j], ends[j][2])

        return copy

    def rs_send(inst, i, dest):
        c = rs_copies(inst, i)
        step = L // 4

        def rows_of(j):
            def rows(q):
                return part(q * L + j * step, step)

            here = mul_of(j, step)
            s1[i, 0, here] = acc[rows(t_y), 0:HW].astype(bf16)
            s1[i, 1, here] = acc[rows(t_d), 0:HW].astype(bf16)
            s1[i, 2, here] = acc[rows(t_z), HW:CW].astype(bf16)
            s1[i, 3, here] = acc[rows(t_d), HW:CW].astype(bf16)
            k2[i, 0, here] = acc[rows(t_z), 0:HW]
            k2[i, 1, here] = acc[rows(t_y), HW:CW]
            dest[here, mul_of(i, CW)] = acc[rows(t), :]

        loop(4, rows_of)
        c(0).start()
        c(1).start()

    def rs_fwd(inst, i, dest):
        c = rs_copies(inst, i)
        c(0).wait_recv()
        s2[i, 0] = (k2[i, 0] + r1[i, 1].astype(f32)).astype(bf16)
        c(2).start()
        c(1).wait_recv()
        s2[i, 1] = (k2[i, 1] + r1[i, 3].astype(f32)).astype(bf16)
        c(3).start()
        dest[:, mul_of(2 * i, HW)] += r1[i, 0].astype(f32)
        dest[:, mul_of(2 * i + 1, HW)] += r1[i, 2].astype(f32)

    def rs_done(inst, i, dest):
        c = rs_copies(inst, i)
        c(2).wait_recv()
        c(3).wait_recv()
        dest[:, mul_of(2 * i, HW)] += r2[i, 0].astype(f32)
        dest[:, mul_of(2 * i + 1, HW)] += r2[i, 1].astype(f32)

    def rs(inst, dest, compute, between=lambda i: None):
        def first(i):
            compute(i)
            rs_send(inst, i, dest)

        loop(CHUNKS, first)
        between(0)
        loop(CHUNKS // 2, lambda i: rs_fwd(inst, i, dest))
        between(1)
        loop(CHUNKS, lambda i: rs_fwd(inst, i, dest), CHUNKS // 2)
        between(2)
        loop(CHUNKS, lambda i: rs_done(inst, i, dest))

        def wait(i):
            c = rs_copies(inst, i)
            for j in range(4):
                c(j).wait_send()

        loop(CHUNKS, wait)

    def qkv_region(s_, piece):
        return wqkv.at[part(s_ * (D // 2) + piece * (D // 4), D // 4)]

    def qkv_parts(s_, piece):
        rows, to = part(piece * (D // 4), D // 4), part(s_ * (D // 2) + piece * (D // 4), D // 4)
        for which, src in enumerate((wq_h, wk_h, wv_h)):
            for h in range(d.S):
                yield src.at[rows, part((h * TP + t) * HD, HD)], wqkv.at[to, pl.ds(which * ha + h * HD, HD)]

    def o_region(s_, piece):
        return wo.at[part(s_ * HD + piece * (HD // 2), HD // 2)]

    def o_parts(s_, piece):
        yield wo_h.at[part(t * HD + piece * (HD // 2), HD // 2)], o_region(s_, piece)

    def gu_group(sub):
        n = D // 8

        def region(s_, piece):
            return wgu.at[part(s_ * (D // 2) + piece * (D // 4) + sub * n, n)]

        def parts(s_, piece):
            rows = part(piece * (D // 4) + sub * n, n)
            to = part(s_ * (D // 2) + piece * (D // 4) + sub * n, n)
            w = 2 * unit
            if not d.direct:
                yield wg_h.at[rows], wgu.at[to]
                return
            for m, src in enumerate((wg_h, wu_h)):
                for c in range(d.S * his):
                    yield src.at[rows, part((c * TP + t) * w, w)], wgu.at[to, pl.ds(m * fh + c * w, w)]

        return parts, region

    def d_region(s_, piece):
        n = fh // 4
        return wd.at[part(((s_ * 2 + piece) if d.direct else (piece * 2 + s_)) * n, n)]

    def d_parts(s_, piece):
        w = 2 * unit
        if not d.direct:
            yield wd_h.at[part(piece * (fh // 4), fh // 4)], d_region(s_, piece)
            return
        for e in range(his // 2):
            block = piece * (his // 2) + e
            yield wd_h.at[part((block * TP + t) * w, w)], wd.at[part((s_ * his + block) * w, w)]

    groups = ((qkv_parts, qkv_region), (o_parts, o_region), gu_group(0), gu_group(1), (d_parts, d_region))
    NG = len(groups)

    def local_start(k):
        for piece in range(2):
            for src, dst in groups[k][0](s, piece):
                pltpu.make_async_copy(src, dst, w_l.at[k, piece]).start()

    def local_wait(k):
        for piece in range(2):
            here = groups[k][1](s, piece)
            pltpu.make_async_copy(here, here, w_l.at[k, piece]).wait()

    def cross_start(k):
        for src, dst in groups[k][0](s, core):
            send(src, dst, w_s.at[k], w_r.at[k], dev_x).start()

    def cross(k):
        here = groups[k][1](s, core)
        return send(here, here, w_s.at[k], w_r.at[k], dev_x)

    def share(k):
        here = groups[k][1](1 - s, core)
        return send(here, here, wf_s.at[k], wf_r.at[k], dev_c)

    def w_forward(k):
        cross(k).wait_recv()
        share(k).start()

    def w_ready(k):
        local_wait(k)
        share(k).wait_recv()

    own_x = pltpu.make_async_copy(x_h, xall.at[blk(t)], loc.at[0])
    own_cot = pltpu.make_async_copy(cot_h, cot, loc.at[1])
    own_gain = pltpu.make_async_copy(gain_v, gbuf.at[s], loc.at[2])
    far_gain = send(gain_v, gbuf.at[s], w_s.at[NG], w_r.at[NG], dev_x)
    ag_start(xall, 0, 0, x_h)
    cross_start(0)
    ag_start(xall, 0, 1, x_h)
    own_x.start()
    far_gain.start()
    own_gain.start()
    local_start(0)
    for k in range(1, NG):
        cross_start(k)
    for k in range(1, NG):
        local_start(k)
    own_cot.start()

    for i in range(CHUNKS):
        ag_fwd(xall, 0, i)
        if i + 2 < CHUNKS:
            ag_start(xall, 0, i + 2, x_h)
    w_forward(0)
    own_x.wait()
    own_gain.wait()
    far_gain.wait_recv()
    for q in range(2):
        gat[:, q * (D // 2):(q + 1) * (D // 2)] = gbuf[q, :, 2 * HD:2 * HD + D // 2]
        gml[:, q * (D // 2):(q + 1) * (D // 2)] = gbuf[q, :, 2 * HD + D // 2:]
    gsum[...] = jnp.zeros_like(gsum)
    for i in range(CHUNKS):
        ag_done(xall, 0, i)
    ag_drain(xall, 0)
    w_ready(0)

    qk[:, 0:ha] = dot_nn(xall[...], wqkv[:, 0:ha])
    qk[:, ha:2 * ha] = dot_nn(xall[...], wqkv[:, ha:2 * ha])
    vb[...] = dot_nn(xall[...], wqkv[:, 2 * ha:]).astype(bf16)
    w_forward(1)

    row8 = lax.broadcasted_iota(jnp.int32, (8, 2 * ha), 0)
    col8 = lax.broadcasted_iota(jnp.int32, (8, 2 * ha), 1)
    pick = jnp.where((row8 < 4) == (col8 < ha), 1.0, 0.0).astype(f32)
    HIGH = lax.Precision.HIGHEST

    def stat_sum(k, values, between=lambda: None):
        def sequence(b):
            stat[k, :, blk(b)] = dot_nt(pick, values(blk(b)), HIGH)

        loop(TP, sequence)
        copies = [send(stat.at[k], statr.at[k, j], st_s.at[k, j], st_r.at[k, j], dev)
                  for j, dev in enumerate((dev_y, dev_z, dev_d))]
        for c in copies:
            c.start()
        between()
        for c in copies:
            c.wait_recv()
        for c in copies:
            c.wait_send()
        return stat[k] + statr[k, 0] + statr[k, 1] + statr[k, 2]

    def squares(rows):
        v = qk[rows, :]
        return v * v

    stat[2] = lax.rsqrt(stat_sum(0, squares) / d.att + eps_norm)

    def columns(k, b):
        flat = stat[k, :, blk(b)]
        wide = jnp.concatenate([flat] * (L // 8), axis=0).T
        return wide[:, 0:1], wide[:, 4:5]

    def gain_of(which, h):
        return gbuf[h, :, which * HD:(which + 1) * HD]

    inv = 1.0 / math.sqrt(HD)
    heads = ha // HD

    def attend(b):
        rows = blk(b)
        scale = columns(2, b)
        cos, sin = cos_v[...], sin_v[...]
        above = lax.broadcasted_iota(jnp.int32, (L, L), 0) < lax.broadcasted_iota(jnp.int32, (L, L), 1)
        for h in range(heads):
            rot = []
            for which in range(2):
                at = pl.ds(which * ha + h * HD, HD)
                normed = qk[rows, at] * scale[which] * gain_of(which, h)
                turned = (normed * cos + pltpu.roll(normed, HD // 2, 1) * sin).astype(bf16)
                qkrot[rows, at] = turned
                rot.append(turned)
            scores = jnp.where(above, -jnp.inf, dot_nt(rot[0], rot[1]) * inv)
            peak = jnp.max(scores, axis=-1, keepdims=True)
            log_total = peak + jnp.log(jnp.sum(jnp.exp(scores - peak), axis=-1, keepdims=True))
            p = jnp.exp(scores - log_total)
            probs[b * heads + h] = p
            head = pl.ds(h * HD, HD)
            mixed[rows, head] = dot_nn(p.astype(bf16), vb[rows, head]).astype(bf16)

    loop(TP, attend)
    w_ready(1)

    def attn_chunk(i):
        acc[...] = dot_nn(mixed[...], wo[:, mul_of(i, CW)])

    rs(0, abuf, attn_chunk)

    BL = 16

    def residual_rows(j):
        rows = mul_of(j, BL)
        a = abuf[rows, :]
        scale = lax.rsqrt(jnp.mean(a * a, axis=-1, keepdims=True) + eps_norm)
        mine = part(t * L + j * BL, BL)
        res = xall[mine, :].astype(f32) + a * scale * gat[...]
        cbuf[rows, :] = res
        rall[mine, :] = res.astype(bf16)

    loop(L // BL, residual_rows)
    w_forward(2)
    ag(rall, 1)
    w_forward(3)
    w_ready(2)
    w_ready(3)

    NT = 256

    def gate_up(n):
        g_at, u_at = mul_of(n, NT), part(fh + n * NT, NT)
        gu[:, g_at] = dot_nn(rall[...], wgu[:, g_at])
        gu[:, u_at] = dot_nn(rall[...], wgu[:, u_at])

        def rows_of(j):
            rows = mul_of(j, 64)
            g, u = gu[rows, g_at], gu[rows, u_at]
            hid[rows, g_at] = (g * jax.nn.sigmoid(g) * u).astype(bf16)

        loop(T // 64, rows_of)

    loop(fh // NT, gate_up)
    w_forward(4)
    w_ready(4)

    def down_chunk(i):
        acc[...] = dot_nn(hid[...], wd[:, mul_of(i, CW)])

    rs(1, bbuf, down_chunk)
    own_cot.wait()

    def output_rows(j):
        rows = mul_of(j, BL)
        dn = bbuf[rows, :]
        scale = lax.rsqrt(jnp.mean(dn * dn, axis=-1, keepdims=True) + eps_norm)
        outb[rows, :] = (cbuf[rows, :] + dn * scale * gml[...]).astype(bf16)
        co = cot[rows, :].astype(f32)
        weighted = co * gml[...]
        inner = jnp.mean(weighted * dn, axis=-1, keepdims=True)
        gd = scale * weighted - dn * scale**3 * inner
        gdall[part(t * L + j * BL, BL), :] = gd.astype(bf16)
        gsum[:, D:2 * D] += jnp.sum(co * dn * scale, axis=0, keepdims=True)

    loop(L // BL, output_rows)
    put_out = pltpu.make_async_copy(outb, out_h, loc.at[3])
    put_out.start()
    ag(gdall, 2)

    half_q = 3 * ha // 2

    def by_cols(left, right, width):
        def make(row, n, core_):
            return dot_tn(left[:, part(row, n)], right[:, mul_of(core_, width)])
        return make

    def down_grad(row, n, core_):
        start = (row // unit) * 2 * unit + core_ * unit if d.direct else core_ * (fh // 2) + row
        return dot_tn(hid[:, part(start, n)], gdall[...])

    ND, NG2, NQ, NO = range(4)
    sets = (
        (down_grad, rc_d, rx_d, rh_d, fh // 2, 128, stage_d),
        (by_cols(rall, gg2, fh), rc_gu, rx_gu, rh_gu, D, 256, stage),
        (by_cols(xall, gqkv, half_q), rc_q, rx_q, rh_q, D, 256, stage),
        (by_cols(mixed, gaall, D // 2), rc_o, rx_o, None, ha, 128, stage),
    )
    top = hi // (his // 2)

    def tiles_of(k):
        return sets[k][4] // 2 // sets[k][5]

    def tile_row(k, j):
        tiles, n = tiles_of(k), sets[k][5]
        if tiles < 2:
            return j * n
        return ((j + (1 - top) * (tiles // 2)) % tiles) * n

    def whole_row(k, j):
        tiles = tiles_of(k)
        late = j // tiles
        return (late * s + (1 - late) * (1 - s)) * (sets[k][4] // 2) + tile_row(k, j % tiles)

    def core_copy(k, j, slot):
        _, buf, _, _, _, n, st = sets[k]
        row = whole_row(k, j)
        view = st.at[slot, :, 0:buf.shape[1]] if st.shape[1] == n else st.at[slot, 0:n, 0:buf.shape[1]]
        return send(view, buf.at[part(row, n)], stg_s.at[0 if k == ND else 1, slot], c_r.at[k, row // n], dev_c)

    def give(k):
        make, buf, _, _, _, n, st = sets[k]
        slots, w, count = st.shape[0], buf.shape[1], 2 * tiles_of(k)

        def tile(j):
            slot = j % slots

            @pl.when(j >= slots)
            def _():
                core_copy(k, j, slot).wait_send()

            st[slot, 0:n, 0:w] = make(whole_row(k, j), n, 1 - core).astype(bf16)
            core_copy(k, j, slot).start()

        loop(count, tile)
        for slot in range(min(slots, count)):
            core_copy(k, 0, slot).wait_send()

    def x_copy(k, j):
        _, buf, far, _, rows, n, _ = sets[k]
        row = tile_row(k, j)
        return send(buf.at[part((1 - s) * (rows // 2) + row, n)], far.at[part(row, n)], x_s.at[k, j], x_r.at[k, j], dev_x)

    def take(k, late):
        make, buf, _, _, _, n, _ = sets[k]
        tiles = tiles_of(k)

        def tile(j):
            row = whole_row(k, j)
            core_copy(k, j, 0).wait_recv()
            buf[part(row, n), :] = (make(row, n, core) + buf[part(row, n), :].astype(f32)).astype(bf16)
            if not late:
                x_copy(k, j).start()

        loop(2 * tiles if late else tiles, tile, tiles if late else 0)

    def hi_first(k, j):
        _, buf, _, back, rows, n, _ = sets[k]
        other = hi + (his // 2) * (1 - 2 * top)
        return send(buf.at[part(s * (rows // 2) + tile_row(k, j), n)], back.at[mul_of(j, n)],
                    h0_s.at[k, j], h0_r.at[k, j], (s, rep(other, t, core)))

    def add_rows(buf, row, far, far_row, n, final=None):
        step = min(n, 64)

        def rows_of(j):
            rows = part(row + j * step, step)
            total = buf[rows, :].astype(f32) + far[part(far_row + j * step, step), :].astype(f32)
            if final is None:
                buf[rows, :] = total.astype(bf16)
            else:
                final[mul_of(j, step), :] = total

        loop(n // step, rows_of)

    def x_add(k, j0, j1):
        _, buf, far, _, rows, n, _ = sets[k]
        tiles = tiles_of(k)

        def tile(j):
            row = tile_row(k, j)
            x_copy(k, j).wait_recv()
            add_rows(buf, s * (rows // 2) + row, far, row, n)
            if k != NO:
                @pl.when(j < tiles // 2)
                def _():
                    hi_first(k, j).start()

        loop(j1, tile, j0)

    def hi_later(k):
        half = sets[k][4] // 2
        base, size, at, out = top * (half // 2), half // 2, half // 2, []
        for level in range(1, d.levels):
            size //= 2
            weight = his >> (level + 1)
            bit = (hi // weight) % 2
            out.append((level - 1, base + (1 - bit) * size, base + bit * size, size, at, hi + weight * (1 - 2 * bit)))
            base = base + bit * size
            at += size
        return out, base, size

    def hi_copy(k, step):
        level, far_row, _, size, at, other = step
        half = sets[k][4] // 2
        return send(sets[k][1].at[part(s * half + far_row, size)], sets[k][3].at[pl.ds(at, size)],
                    h_s.at[k, level], h_r.at[k, level], (s, rep(other, t, core)))

    def hi_finish(k, final=None):
        _, buf, _, back, rows, n, _ = sets[k]
        tiles, half = tiles_of(k), rows // 2
        last = final if d.levels == 1 else None

        def tile(j):
            hi_first(k, j).wait_recv()
            add_rows(buf, s * half + tile_row(k, j + tiles // 2), back, j * n, n, last)

        loop(tiles // 2, tile)
        later = hi_later(k)[0]
        for step in later:
            hi_copy(k, step).start()
            hi_copy(k, step).wait_recv()
            add_rows(buf, s * half + step[2], back, step[4], step[3], final if step is later[-1] else None)

    me = t * CORES + core

    def keep_parts(k, p, slot_t, slot_core):
        half = sets[k][4] // 2
        _, base, _ = hi_later(k)
        rows = part(s * half + base + p * d.own, d.own)
        if k == NQ:
            for c in range(3):
                e = slot_core * 3 + c
                yield (rc_q.at[rows, pl.ds(c * HD, HD)],
                       qkv_h.at[e // 2, :, part(((e % 2) * TP + slot_t) * HD, HD)])
        elif d.direct:
            w = 2 * unit
            for c in range(d.S * his):
                yield rc_gu.at[rows, pl.ds(c * w, w)], gu_h.at[slot_core, :, part((c * TP + slot_t) * w, w)]
        else:
            yield rc_gu.at[rows], gu_h.at[slot_t * CORES + slot_core]

    def keep_start(k):
        def piece(p):
            @pl.when(me != p)
            def _():
                for src, dst in keep_parts(k, p, t, core):
                    send(src, dst, a_s.at[k - 1, p], a_r.at[k - 1, me], (s, rep(hi, p // CORES, p % CORES))).start()

            @pl.when(me == p)
            def _():
                for src, dst in keep_parts(k, p, t, core):
                    pltpu.make_async_copy(src, dst, a_r.at[k - 1, me]).start()

        loop(TP * CORES, piece)

    def keep_wait(k):
        def piece(p):
            whole = sets[k][1].at[pl.ds(0, d.own)]
            pltpu.make_async_copy(whole, whole, a_r.at[k - 1, p]).wait()

            @pl.when(me != p)
            def _():
                send(whole, whole, a_s.at[k - 1, p], a_r.at[k - 1, me], (s, rep(hi, p // CORES, p % CORES))).wait_send()

        loop(TP * CORES, piece)

    partners = [dev_c, dev_x]
    for level in range(d.levels):
        weight = his >> (level + 1)
        bit = (hi // weight) % 2
        partners.append((s, rep(hi + weight * (1 - 2 * bit), t, core)))
    partners += [dev_y, dev_z]

    def gain_copy(n):
        return send(gsum, grecv.at[n], gn_s.at[n], gn_r.at[n], partners[n])

    def gain_step(n):
        if n:
            gain_copy(n - 1).wait_send()
            gain_copy(n - 1).wait_recv()
            gsum[...] += grecv[n - 1]
        if n < len(partners):
            gain_copy(n).start()

    give(ND)

    def hidden_back(n):
        g_at, u_at = mul_of(n, NT), part(fh + n * NT, NT)
        acc[:, 0:NT] = dot_nt(gdall[...], wd[mul_of(n, NT), :])

        def rows_of(j):
            rows = mul_of(j, 64)
            g, u, gh = gu[rows, g_at], gu[rows, u_at], acc[rows, 0:NT]
            sig = jax.nn.sigmoid(g)
            gg2[rows, g_at] = (gh * u * sig * (1.0 + g * (1.0 - sig))).astype(bf16)
            gg2[rows, u_at] = (gh * (g * sig)).astype(bf16)

        loop(T // 64, rows_of)

    loop(fh // NT, hidden_back)
    take(ND, False)

    def res_chunk(i):
        acc[...] = dot_nt(gg2[...], wgu[mul_of(i, CW), :])

    def res_between(i):
        if i == 0:
            give(NG2)
        elif i == 1:
            take(NG2, False)
        else:
            take(ND, True)
            take(NG2, True)

    rs(2, cbuf, res_chunk, res_between)

    def attn_grad_rows(j):
        rows = mul_of(j, BL)
        gr = cbuf[rows, :] + cot[rows, :].astype(f32)
        cbuf[rows, :] = gr
        a = abuf[rows, :]
        scale = lax.rsqrt(jnp.mean(a * a, axis=-1, keepdims=True) + eps_norm)
        weighted = gr * gat[...]
        inner = jnp.mean(weighted * a, axis=-1, keepdims=True)
        ga = scale * weighted - a * scale**3 * inner
        gaall[part(t * L + j * BL, BL), :] = ga.astype(bf16)
        gsum[:, 0:D] += jnp.sum(gr * a * scale, axis=0, keepdims=True)

    loop(L // BL, attn_grad_rows)

    def ga_between(i):
        if i == 1:
            x_add(ND, 0, 1)
        if i == 3:
            x_add(ND, 1, 2)

    ag(gaall, 3, None, ga_between)

    give(NO)
    acc[:, 0:ha] = dot_nt(gaall[...], wo[...])
    x_add(NG2, 0, 1)

    def attend_back(b):
        rows = blk(b)
        scale = columns(2, b)
        cos, sin = cos_v[...], sin_v[...]
        for h in range(heads):
            head = pl.ds(h * HD, HD)
            gm = acc[rows, head].astype(bf16)
            p = probs[b * heads + h]
            gqkv[rows, pl.ds(2 * ha + h * HD, HD)] = dot_tn(p.astype(bf16), gm).astype(bf16)
            gp = dot_nt(gm, vb[rows, head])
            gs = p * (gp - jnp.sum(p * gp, axis=-1, keepdims=True))
            gs = (gs * inv).astype(bf16)
            turned = (dot_nn(gs, qkrot[rows, pl.ds(ha + h * HD, HD)]), dot_tn(gs, qkrot[rows, head]))
            for which in range(2):
                at = pl.ds(which * ha + h * HD, HD)
                gn = turned[which] * cos - pltpu.roll(turned[which], HD // 2, 1) * sin
                field = qk[rows, at]
                spot = part(2 * D + which * d.att + t * ha + h * HD, HD)
                gsum[:, spot] += jnp.sum(gn * field * scale[which], axis=0, keepdims=True)
                gu[rows, at] = gn * gain_of(which, h)

    loop(TP, attend_back)

    def products(rows):
        return gu[rows, 0:2 * ha] * qk[rows, :]

    stat[3] = stat_sum(1, products, lambda: take(NO, False)) / d.att
    gain_step(0)

    def qk_back(b):
        rows = blk(b)
        scale, inner = columns(2, b), columns(3, b)
        for which in range(2):
            at = pl.ds(which * ha, ha)
            sc = scale[which]
            gqkv[rows, at] = (sc * gu[rows, at] - qk[rows, at] * (sc**3 * inner[which])).astype(bf16)

    loop(TP, qk_back)
    give(NQ)
    gain_step(1)

    def in_chunk(i):
        acc[...] = dot_nt(gqkv[...], wqkv[mul_of(i, CW), :])

    def in_between(i):
        if i == 0:
            take(NQ, False)
            x_add(NG2, 1, 2)
            gain_step(2)
        elif i == 1:
            take(NQ, True)
            take(NO, True)
        else:
            hi_finish(ND, abuf)
            pltpu.make_async_copy(abuf.at[0:unit], down_h, loc.at[4]).start()
            gain_step(3)

    rs(3, bbuf, in_chunk, in_between)

    def input_rows(j):
        rows = mul_of(j, BL)
        bbuf[rows, :] += cbuf[rows, :]

    loop(L // BL, input_rows)
    put_gin = pltpu.make_async_copy(bbuf, gin_h, loc.at[5])
    put_gin.start()

    gain_step(4)
    x_add(NG2, 2, 4)
    for n in range(5, len(partners) + 1):
        gain_step(n)
    gg_o[...] = gsum[...]
    x_add(NO, 0, 1)

    for p in range(d.pieces):
        o_pc[p] = rc_o[part(s * HD + p * d.own_o, d.own_o), :]
    o_slot = hi * CORES + core

    def o_start(p):
        goal = t * d.pieces + p

        @pl.when(goal != r)
        def _():
            send(o_pc.at[p], o_h.at[o_slot], o_s.at[p], o_r.at[o_slot], (s, goal)).start()

        @pl.when(goal == r)
        def _():
            pltpu.make_async_copy(o_pc.at[p], o_h.at[o_slot], o_r.at[o_slot]).start()

    loop(d.pieces, o_start)
    x_add(NQ, 0, 4)
    hi_finish(NG2)
    keep_start(NG2)
    hi_finish(NQ)
    keep_start(NQ)

    keep_wait(NG2)
    keep_wait(NQ)

    def o_wait(q):
        pltpu.make_async_copy(o_pc.at[0], o_pc.at[0], o_r.at[q]).wait()

    loop(his * CORES, o_wait)

    def o_sent(p):
        goal = t * d.pieces + p

        @pl.when(goal != r)
        def _():
            send(o_pc.at[p], o_h.at[o_slot], o_s.at[p], o_r.at[o_slot], (s, goal)).wait_send()

    loop(d.pieces, o_sent)
    far_gain.wait_send()
    for k in range(NG):
        cross(k).wait_send()
        share(k).wait_send()
    for k in range(4):
        loop(tiles_of(k), lambda j: x_copy(k, j).wait_send())
    for k in range(3):
        loop(tiles_of(k) // 2, lambda j: hi_first(k, j).wait_send())
        for step in hi_later(k)[0]:
            hi_copy(k, step).wait_send()
    put_out.wait()
    put_gin.wait()
    pltpu.make_async_copy(abuf.at[0:unit], down_h, loc.at[4]).wait()


def body(shards, replicas, x_in, cotangent, w_query, w_key, w_value, w_out, w_gate, w_up, w_down,
         gain_query, gain_key, gain_attn, gain_mlp):
    seqs, length, width = x_in.shape
    assert seqs == 1
    d = Dims(length, width, w_query.shape[1], w_gate.shape[1], shards, replicas)
    r = lax.axis_index("replica")
    s = lax.axis_index("shard")
    t = (r // CORES) % TP

    def at(array, axis, index):
        return lax.dynamic_index_in_dim(array, index, axis, keepdims=False)

    def hidden_cols(w):
        picked = at(w.reshape(w.shape[0], d.S, d.his, TP, CORES, d.unit), 3, t)
        return picked.transpose(0, 3, 1, 2, 4).reshape(w.shape[0], d.fh)

    if not d.direct:
        w_gate = jnp.concatenate([hidden_cols(w_gate), hidden_cols(w_up)], axis=1)
        w_down = at(w_down.reshape(d.his, TP, CORES, d.unit, width), 1, t).transpose(1, 0, 2, 3).reshape(-1, width)
    gain = jnp.concatenate([at(gain_query.reshape(TP, HD), 0, t), at(gain_key.reshape(TP, HD), 0, t),
                            gain_attn, gain_mlp]).astype(f32)[None]
    cos, sin = rope_tables(length, HD // 2)
    cos = np.concatenate([cos, cos], axis=1)
    sin = np.concatenate([-sin, sin], axis=1)

    L, D, T, ha, fh = d.L, d.D, d.T, d.ha, d.fh
    CW = D // CHUNKS
    vm = pltpu.VMEM
    dma = pltpu.SemaphoreType.DMA
    any_ = pl.BlockSpec(memory_space=pl.ANY)
    vmem = pl.BlockSpec(memory_space=pltpu.VMEM)
    hi_rows = lambda n: max(n - n // d.his, 16)
    steps = 4 + d.levels
    later = max(d.levels - 1, 1)
    scratch = [
        vm((D, 3 * ha), bf16), vm((ha, D), bf16), vm((D, 2 * fh), bf16), vm((fh, D), bf16),
        vm((2, 1, d.gains), f32), vm((1, D), f32), vm((1, D), f32),
        vm((T, D), bf16), vm((T, D), bf16), vm((T, D), bf16), vm((T, D), bf16), vm((L, D), bf16),
        vm((T, 2 * ha), f32), vm((T, ha), bf16), vm((T, 2 * ha), bf16), vm((TP * ha // HD, L, L), f32),
        vm((T, ha), bf16), vm((T, 3 * ha), bf16), vm((4, 8, T), f32), vm((2, 3, 8, T), f32),
        vm((T, 2 * fh), f32), vm((T, fh), bf16), vm((T, 2 * fh), bf16),
        vm((L, D), f32), vm((L, D), f32), vm((L, D), f32), vm((L, D), bf16),
        vm((T, CW), f32), vm((CHUNKS, 4, L, CW // 2), bf16), vm((CHUNKS, 2, L, CW // 2), bf16),
        vm((CHUNKS, 4, L, CW // 2), bf16), vm((CHUNKS, 2, L, CW // 2), bf16), vm((CHUNKS, 2, L, CW // 2), f32),
        vm((2, 128, D), bf16), vm((2, 256, fh), bf16),
        vm((D, fh), bf16), vm((fh // 2, D), bf16), vm((D, 3 * ha // 2), bf16), vm((ha, D // 2), bf16),
        vm((D // 2, fh), bf16), vm((fh // 4, D), bf16), vm((D // 2, 3 * ha // 2), bf16), vm((ha // 2, D // 2), bf16),
        vm((hi_rows(D // 2), fh), bf16), vm((hi_rows(fh // 4), D), bf16), vm((hi_rows(D // 2), 3 * ha // 2), bf16),
        vm((d.pieces, d.own_o, D // 2), bf16),
        vm((1, d.ggs), f32), vm((steps, 1, d.ggs), f32),
        dma((4, CHUNKS, 4)), dma((4, CHUNKS, 4)), dma((4, CHUNKS, 4)), dma((4, CHUNKS, 4)),
        dma((6,)), dma((6,)), dma((5,)), dma((5,)), dma((5, 2)), dma((6,)), dma((2, 3)), dma((2, 3)),
        dma((2, 2)), dma((4, 8)), dma((4, 4)), dma((4, 4)), dma((3, 4)), dma((3, 4)),
        dma((3, later)), dma((3, later)),
        dma((2, TP * CORES)), dma((2, TP * CORES)), dma((d.pieces,)), dma((d.his * CORES,)), dma((steps,)), dma((steps,)),
    ]
    struct = jax.ShapeDtypeStruct
    gu_shape = (2, d.own, d.ff) if d.direct else (TP * CORES, d.own, fh)
    results = pl.pallas_call(
        functools.partial(kernel, d),
        out_shape=(
            struct((L, D), bf16), struct((L, D), f32), struct(gu_shape, bf16), struct((3, d.own, d.att), bf16),
            struct((d.unit, D), f32), struct((d.his * CORES, d.own_o, D // 2), bf16), struct((1, d.ggs), f32),
        ),
        in_specs=[any_] * 9 + [vmem] * 3,
        out_specs=(any_,) * 6 + (vmem,),
        scratch_shapes=scratch,
        compiler_params=pltpu.CompilerParams(
            collective_id=0, has_side_effects=True, vmem_limit_bytes=67043328),
        name="layer",
    )(x_in[0], cotangent[0], w_query, w_key, w_value, w_out, w_gate, w_up, w_down, gain, cos, sin)
    out, gin, gu, qkv, down, o, gg = results

    def hidden_out(k):
        if d.direct:
            return gu[k].astype(f32)
        block = gu.reshape(TP, CORES, d.own, fh)[:, k]
        spread = block.reshape(TP, d.own, CORES, d.S, d.his, d.unit).transpose(1, 3, 4, 0, 2, 5)
        return spread.reshape(d.own, d.ff).astype(f32)

    o = o.reshape(d.his, CORES, d.own_o, D // 2).astype(f32).sum(0).transpose(1, 0, 2).reshape(d.own_o, D)
    gg = gg[0]
    here = s * d.R + r

    def share(vec):
        n = vec.shape[0] // (d.S * d.R)
        return lax.dynamic_slice_in_dim(vec, here * n, n)

    def head_gain(vec):
        return share(vec.reshape(TP, d.S, HD).transpose(1, 0, 2).reshape(-1))

    return (
        out[None], gin[None], qkv[0].astype(f32), qkv[1].astype(f32), qkv[2].astype(f32), o,
        hidden_out(0), hidden_out(1), down,
        head_gain(gg[2 * D:2 * D + d.att]), head_gain(gg[2 * D + d.att:]), share(gg[:D]), share(gg[D:2 * D]),
    )


def solution(mesh):
    both = ("shard", "replica")
    token = P(both, None, None)
    weight = P("shard", None)
    return jax.shard_map(
        functools.partial(body, mesh.shape["shard"], mesh.shape["replica"]),
        mesh=mesh,
        in_specs=(token, token) + (weight,) * 7 + (P("shard"),) * 4,
        out_specs=(token, token) + (P(both, None),) * 7 + (P(both),) * 4,
        check_vma=False,
    )
```

time: 535 us -> 305 us (0.57); the launches traced: 528 us -> 304 us
  Pallas kernels: 428 us -> 291 us
  local copies, waits for them, and re-layouts: 89.7 us -> 7.9 us
    pallas_call x1, Pallas kernels: 428 us -> 291 us  [body(): pl.pallas_call(functools.partial(kernel, d), out_shape=(struct((L, D), bf...]
    reshape x8 -> x0, local copies, waits for them, and re-layouts: 45.7 us -> none  [the longest x2 28.6 us: hidden_cols(): picked = at(w.reshape(w.shape[0], d.S, d.his, TP, CORES, d.unit), 3, t)]
    dynamic_slice x8 -> x1, local copies, waits for them, and re-layouts: 26.5 us -> 0.71 us  [at(): return lax.dynamic_index_in_dim(array, index, axis, keepdims=False)]
    convert_element_type x12 -> x0, local copies, waits for them, and re-layouts: 9.45 us -> none  [the longest x6 6.51 us: hidden_out(): return spread.reshape(d.own, d.ff).astype(f32)]
    concatenate x3 -> x0, other arithmetic: 6.68 us -> none  [the longest x1 4.68 us: body(): wgu = jnp.concatenate([hidden_cols(w_gate), hidden_cols(w_up)], axis=1)]
where the time goes in v3:
time: 305 us; the launch traced here: 304 us
  Pallas kernels  291 us (95%)
  local copies, waits for them, and re-layouts  7.9 us (3%)
  other arithmetic  4.36 us (1%)
    pallas_call x1, Pallas kernels, body(): pl.pallas_call(functools.partial(kernel, d), out_shape=(struct((L, D), bf...  291 us

profile of v3, /device:TPU:0, one launch (start us, length us, event | category | flops | bytes accessed | tf_op | source)
XLA Modules:
  0.0 303.6 jit_solution(9611481876183621675)
XLA Ops:
  0.7 0.7 constant_dynamic-slice_fusion.2
  1.4 0.7 concatenate.14
  2.1 0.7 concatenate.15
  2.8 0.6 maximum_convert_fusion.gain_v
  3.4 290.6 %layer.1 = (bf16[128,2048]{1,0:T(8,128)(2,1)}, f32[128,2048]{1,0:T(8,128)}, bf16[2,64,4096]{2,1,0:T(8,128)(2,1)}, bf16[3,64,1024]{2,1,0:T(8,128)(2,1)}, f32[128,...) custom-call(bf16[128,2048]{1,0:T(8,128)(2,1)} %bitcast.40, bf16[128,2048]{1,0:T(8,128)(2,1)} %bitcast.41, ...), custom_call_target="tpu_custom_call" | custom-call | tf_op jit(solution)/shard_map/layer/pallas_call | solution.py:934
  294.0 0.0 copy-start.3
  294.0 0.0 copy-start.4
  294.0 0.0 copy-start.5
  294.0 0.0 copy-start.2
  294.0 2.8 bitcast_convert_fusion
  296.8 0.0 copy-start.1
  296.8 0.0 copy-done.3
  296.8 0.9 bitcast_convert_fusion.2
  297.7 0.0 copy-done.4
  297.7 0.0 copy-start
  297.8 0.7 copy.35
  298.5 0.0 copy-done.5
  298.5 0.6 fusion
  299.1 0.6 fusion.1
  299.7 0.6 dynamic_slice.25
  300.3 0.6 dynamic_slice.26
  300.8 0.0 copy-done.2
  300.8 0.8 copy.39
  301.6 0.0 copy-done.1
  301.6 1.0 copy.40
  302.6 0.0 copy-done
  302.6 1.0 copy.41
  (5 shorter events, 0.0 us)
Async XLA Ops:
  294.0 2.9 copy-start.3
  294.0 3.8 %copy-start.4 = (bf16[4,32,1024]{2,1,0:T(8,128)(2,1)S(1)}, bf16[4,32,1024]{2,1,0:T(8,128)(2,1)}, u32[]{:S(2)}) copy-start(bf16[4,32,1024]{2,1,0:T(8,128)(2,1)} %get-tuple-element.23) | copy-start | bytes 786436
  294.0 4.5 %copy-start.5 = (f32[1,6144]{1,0:T(1,128)S(1)}, f32[1,6144]{1,0:T(1,128)}, u32[]{:S(2)}) copy-start(f32[1,6144]{1,0:T(1,128)} %get-tuple-element.26) | copy-start | bytes 73732
  294.0 6.8 %copy-start.2 = (bf16[128,2048]{1,0:T(8,128)(2,1)S(1)}, bf16[128,2048]{1,0:T(8,128)(2,1)}, u32[]{:S(2)}) copy-start(bf16[128,2048]{1,0:T(8,128)(2,1)} %get-tuple-element.20) | copy-start | bytes 1572868
  296.8 4.8 %copy-start.1 = (f32[128,2048]{1,0:T(8,128)S(1)}, f32[128,2048]{1,0:T(8,128)}, u32[]{:S(2)}) copy-start(f32[128,2048]{1,0:T(8,128)} %get-tuple-element.21) | copy-start | bytes 3145732
  297.7 4.9 %copy-start = (f32[128,2048]{1,0:T(8,128)S(1)}, f32[128,2048]{1,0:T(8,128)}, u32[]{:S(2)}) copy-start(f32[128,2048]{1,0:T(8,128)} %get-tuple-element.59) | copy-start | bytes 3145732

commit v4 on v3

--- a/solution.py
+++ b/solution.py
@@ -13,6 +13,8 @@
 TP = 4
 CORES = 2
 CHUNKS = 4
+Z_AG = (256, 256, 256, 0)
+Z_RS = (256, 256, 256, 128)
 
 eps_norm = 1e-06
 rope_theta = 500000.0
@@ -66,12 +68,13 @@
         self.ggs = 2 * width + 2 * att
         self.direct = self.unit % 128 == 0
         assert shards == 2 and self.his == 1 << self.levels and self.levels > 0 and self.ha == shards * HD
+        assert self.fh == 2 * (width // CHUNKS)
 
 
 def kernel(
     d,
     x_h, cot_h, wq_h, wk_h, wv_h, wo_h, wg_h, wu_h, wd_h, gain_v, cos_v, sin_v,
-    out_h, gin_h, gu_h, qkv_h, down_h, o_h, gg_o,
+    out_h, gin_h, gu_h, qkv_h, down_h, o_h, relay_d, relay_gu, relay_q, gg_o,
     wqkv, wo, wgu, wd, gbuf, gat, gml,
     xall, rall, gdall, gaall, cot,
     qk, vb, qkrot, probs, mixed, gqkv, stat, statr,
@@ -81,7 +84,7 @@
     stage_d, stage, rc_gu, rc_d, rc_q, rc_o, rx_gu, rx_d, rx_q, rx_o, rh_gu, rh_d, rh_q, o_pc,
     gsum, grecv,
     ag_s, ag_r, rs_s, rs_r, w_s, w_r, wf_s, wf_r, w_l, loc, st_s, st_r,
-    stg_s, c_r, x_s, x_r, h0_s, h0_r, h_s, h_r, a_s, a_r, o_s, o_r, gn_s, gn_r,
+    stg_s, c_r, x_s, x_r, h0_s, h0_r, rl_s, rl_r, rf_s, h_s, h_r, a_s, a_r, ko, o_s, o_r, gn_s, gn_r,
 ):
     L, D, T, ha, fh, his, unit = d.L, d.D, d.T, d.ha, d.fh, d.his, d.unit
     CW = D // CHUNKS
@@ -110,22 +113,12 @@
     def part(base, n):
         return pl.ds(pl.multiple_of(base, n), n)
 
-    barrier = pltpu.get_barrier_semaphore()
-
-    def greet(q):
-        @pl.when(q != r)
-        def _():
-            pl.semaphore_signal(barrier, inc=1, device_id=(s, q), device_id_type=pl.DeviceIdType.MESH)
-
-    loop(d.R, greet)
-    pl.semaphore_signal(barrier, inc=1, device_id=dev_x, device_id_type=pl.DeviceIdType.MESH)
-    pl.semaphore_wait(barrier, d.R)
-
     def ag_copies(buf, inst, i, src=None):
         own = buf.at[blk(t), mul_of(i, CW)]
         first = own if src is None else src.at[:, mul_of(i, CW)]
-        ca, cb = mul_of(2 * i, HW), mul_of(2 * i + 1, HW)
-        fy, fz = buf.at[blk(t_y), ca], buf.at[blk(t_z), cb]
+        wz = Z_AG[inst]
+        fy = buf.at[blk(t_y), pl.ds(pl.multiple_of(i * CW + CW - wz, 128), wz)] if wz else None
+        fz = buf.at[blk(t_z), pl.ds(pl.multiple_of(i * CW, 128), CW - wz)]
         ends = ((first, own, dev_y), (first, own, dev_z), (fy, fy, dev_z), (fz, fz, dev_y))
 
         def copy(j):
@@ -140,21 +133,24 @@
 
     def ag_fwd(buf, inst, i):
         c = ag_copies(buf, inst, i)
-        c(0).wait_recv()
-        c(2).start()
         c(1).wait_recv()
         c(3).start()
+        c(0).wait_recv()
+        if Z_AG[inst]:
+            c(2).start()
 
     def ag_done(buf, inst, i):
         c = ag_copies(buf, inst, i)
-        c(2).wait_recv()
+        if Z_AG[inst]:
+            c(2).wait_recv()
         c(3).wait_recv()
 
     def ag_drain(buf, inst):
         def wait(i):
             c = ag_copies(buf, inst, i)
             for j in range(4):
-                c(j).wait_send()
+                if j != 2 or Z_AG[inst]:
+                    c(j).wait_send()
 
         loop(CHUNKS, wait)
 
@@ -171,16 +167,25 @@
         ag_drain(buf, inst)
 
     def rs_copies(inst, i):
-        ends = ((s1.at[i, 0:2], r1.at[i, 0:2], dev_y), (s1.at[i, 2:4], r1.at[i, 2:4], dev_z),
-                (s2.at[i, 0], r2.at[i, 0], dev_z), (s2.at[i, 1], r2.at[i, 1], dev_y))
+        wa = CW - Z_RS[inst]
+        ya, zb = pl.ds(0, wa), pl.ds(wa, CW - wa)
 
         def copy(j):
-            return send(ends[j][0], ends[j][1], rs_s.at[inst, i, j], rs_r.at[inst, i, j], ends[j][2])
+            if j == 0:
+                a, b, dev = s1.at[i, :, :, ya], r1.at[i, :, :, ya], dev_y
+            elif j == 1:
+                a, b, dev = s1.at[i, :, :, zb], r1.at[i, :, :, zb], dev_z
+            elif j == 2:
+                a, b, dev = s2.at[i, :, ya], r2.at[i, :, ya], dev_z
+            else:
+                a, b, dev = s2.at[i, :, zb], r2.at[i, :, zb], dev_y
+            return send(a, b, rs_s.at[inst, i, j], rs_r.at[inst, i, j], dev)
 
         return copy
 
     def rs_send(inst, i, dest):
         c = rs_copies(inst, i)
+        wa = CW - Z_RS[inst]
         step = L // 4
 
         def rows_of(j):
@@ -188,53 +193,61 @@
                 return part(q * L + j * step, step)
 
             here = mul_of(j, step)
-            s1[i, 0, here] = acc[rows(t_y), 0:HW].astype(bf16)
-            s1[i, 1, here] = acc[rows(t_d), 0:HW].astype(bf16)
-            s1[i, 2, here] = acc[rows(t_z), HW:CW].astype(bf16)
-            s1[i, 3, here] = acc[rows(t_d), HW:CW].astype(bf16)
-            k2[i, 0, here] = acc[rows(t_z), 0:HW]
-            k2[i, 1, here] = acc[rows(t_y), HW:CW]
+            s1[i, 0, here, 0:wa] = acc[rows(t_y), 0:wa].astype(bf16)
+            k2[i, here, 0:wa] = acc[rows(t_z), 0:wa]
+            if wa < CW:
+                s1[i, 0, here, wa:CW] = acc[rows(t_z), wa:CW].astype(bf16)
+                k2[i, here, wa:CW] = acc[rows(t_y), wa:CW]
+            s1[i, 1, here] = acc[rows(t_d), :].astype(bf16)
             dest[here, mul_of(i, CW)] = acc[rows(t), :]
 
         loop(4, rows_of)
         c(0).start()
-        c(1).start()
+        if wa < CW:
+            c(1).start()
 
     def rs_fwd(inst, i, dest):
         c = rs_copies(inst, i)
+        wa = CW - Z_RS[inst]
         c(0).wait_recv()
-        s2[i, 0] = (k2[i, 0] + r1[i, 1].astype(f32)).astype(bf16)
+        s2[i, :, 0:wa] = (k2[i, :, 0:wa] + r1[i, 1, :, 0:wa].astype(f32)).astype(bf16)
         c(2).start()
-        c(1).wait_recv()
-        s2[i, 1] = (k2[i, 1] + r1[i, 3].astype(f32)).astype(bf16)
-        c(3).start()
-        dest[:, mul_of(2 * i, HW)] += r1[i, 0].astype(f32)
-        dest[:, mul_of(2 * i + 1, HW)] += r1[i, 2].astype(f32)
+        if wa < CW:
+            c(1).wait_recv()
+            s2[i, :, wa:CW] = (k2[i, :, wa:CW] + r1[i, 1, :, wa:CW].astype(f32)).astype(bf16)
+            c(3).start()
+        dest[:, mul_of(i, CW)] += r1[i, 0].astype(f32)
 
     def rs_done(inst, i, dest):
         c = rs_copies(inst, i)
         c(2).wait_recv()
-        c(3).wait_recv()
-        dest[:, mul_of(2 * i, HW)] += r2[i, 0].astype(f32)
-        dest[:, mul_of(2 * i + 1, HW)] += r2[i, 1].astype(f32)
-
-    def rs(inst, dest, compute, between=lambda i: None):
+        if Z_RS[inst]:
+            c(3).wait_recv()
+        dest[:, mul_of(i, CW)] += r2[i].astype(f32)
+
+    def rs(inst, dest, compute, between=lambda i: None, extra=lambda i: None):
         def first(i):
             compute(i)
             rs_send(inst, i, dest)
+            extra(i)
+
+            @pl.when(i >= 2)
+            def _():
+                rs_fwd(inst, i - 2, dest)
 
         loop(CHUNKS, first)
         between(0)
-        loop(CHUNKS // 2, lambda i: rs_fwd(inst, i, dest))
+        rs_fwd(inst, CHUNKS - 2, dest)
         between(1)
-        loop(CHUNKS, lambda i: rs_fwd(inst, i, dest), CHUNKS // 2)
+        rs_fwd(inst, CHUNKS - 1, dest)
         between(2)
         loop(CHUNKS, lambda i: rs_done(inst, i, dest))
 
         def wait(i):
             c = rs_copies(inst, i)
             for j in range(4):
-                c(j).wait_send()
+                if j % 2 == 0 or Z_RS[inst]:
+                    c(j).wait_send()
 
         loop(CHUNKS, wait)
 
@@ -253,8 +266,10 @@
     def o_parts(s_, piece):
         yield wo_h.at[part(t * HD + piece * (HD // 2), HD // 2)], o_region(s_, piece)
 
+    SUBS = 4
+
     def gu_group(sub):
-        n = D // 8
+        n = D // 4 // SUBS
 
         def region(s_, piece):
             return wgu.at[part(s_ * (D // 2) + piece * (D // 4) + sub * n, n)]
@@ -272,42 +287,54 @@
 
         return parts, region
 
-    def d_region(s_, piece):
+    def d_group(sub):
+        at = mul_of(sub, CW)
         n = fh // 4
-        return wd.at[part(((s_ * 2 + piece) if d.direct else (piece * 2 + s_)) * n, n)]
-
-    def d_parts(s_, piece):
-        w = 2 * unit
-        if not d.direct:
-            yield wd_h.at[part(piece * (fh // 4), fh // 4)], d_region(s_, piece)
-            return
-        for e in range(his // 2):
-            block = piece * (his // 2) + e
-            yield wd_h.at[part((block * TP + t) * w, w)], wd.at[part((s_ * his + block) * w, w)]
-
-    groups = ((qkv_parts, qkv_region), (o_parts, o_region), gu_group(0), gu_group(1), (d_parts, d_region))
-    NG = len(groups)
+
+        def region(s_, piece):
+            return wd.at[part(((s_ * 2 + piece) if d.direct else (piece * 2 + s_)) * n, n), at]
+
+        def parts(s_, piece):
+            w = 2 * unit
+            if not d.direct:
+                yield wd_h.at[part(piece * n, n), at], region(s_, piece)
+                return
+            step = min(w, n)
+            for e in range(n // step):
+                first = piece * n + e * step
+                src = (first // w) * (TP * w) + t * w + first % w
+                yield wd_h.at[part(src, step), at], wd.at[part(s_ * (fh // 2) + first, step), at]
+
+        return parts, region
+
+    GU0, DN0 = 2, 2 + SUBS
+    NG = DN0 + CHUNKS
+
+    def group_of(k):
+        if isinstance(k, int) and k < DN0:
+            return ((qkv_parts, qkv_region), (o_parts, o_region))[k] if k < GU0 else gu_group(k - GU0)
+        return d_group(k - DN0)
 
     def local_start(k):
         for piece in range(2):
-            for src, dst in groups[k][0](s, piece):
+            for src, dst in group_of(k)[0](s, piece):
                 pltpu.make_async_copy(src, dst, w_l.at[k, piece]).start()
 
     def local_wait(k):
         for piece in range(2):
-            here = groups[k][1](s, piece)
+            here = group_of(k)[1](s, piece)
             pltpu.make_async_copy(here, here, w_l.at[k, piece]).wait()
 
     def cross_start(k):
-        for src, dst in groups[k][0](s, core):
+        for src, dst in group_of(k)[0](s, core):
             send(src, dst, w_s.at[k], w_r.at[k], dev_x).start()
 
     def cross(k):
-        here = groups[k][1](s, core)
+        here = group_of(k)[1](s, core)
         return send(here, here, w_s.at[k], w_r.at[k], dev_x)
 
     def share(k):
-        here = groups[k][1](1 - s, core)
+        here = group_of(k)[1](1 - s, core)
         return send(here, here, wf_s.at[k], wf_r.at[k], dev_c)
 
     def w_forward(k):
@@ -322,18 +349,30 @@
     own_cot = pltpu.make_async_copy(cot_h, cot, loc.at[1])
     own_gain = pltpu.make_async_copy(gain_v, gbuf.at[s], loc.at[2])
     far_gain = send(gain_v, gbuf.at[s], w_s.at[NG], w_r.at[NG], dev_x)
+    own_x.start()
+    local_start(0)
+    own_gain.start()
+    own_cot.start()
+
+    barrier = pltpu.get_barrier_semaphore()
+
+    def greet(q):
+        @pl.when(q != r)
+        def _():
+            pl.semaphore_signal(barrier, inc=1, device_id=(s, q), device_id_type=pl.DeviceIdType.MESH)
+
+    loop(d.R, greet)
+    pl.semaphore_signal(barrier, inc=1, device_id=dev_x, device_id_type=pl.DeviceIdType.MESH)
+    pl.semaphore_wait(barrier, d.R)
+
     ag_start(xall, 0, 0, x_h)
     cross_start(0)
     ag_start(xall, 0, 1, x_h)
-    own_x.start()
     far_gain.start()
-    own_gain.start()
-    local_start(0)
     for k in range(1, NG):
         cross_start(k)
     for k in range(1, NG):
         local_start(k)
-    own_cot.start()
 
     for i in range(CHUNKS):
         ag_fwd(xall, 0, i)
@@ -355,7 +394,6 @@
     qk[:, 0:ha] = dot_nn(xall[...], wqkv[:, 0:ha])
     qk[:, ha:2 * ha] = dot_nn(xall[...], wqkv[:, ha:2 * ha])
     vb[...] = dot_nn(xall[...], wqkv[:, 2 * ha:]).astype(bf16)
-    w_forward(1)
 
     row8 = lax.broadcasted_iota(jnp.int32, (8, 2 * ha), 0)
     col8 = lax.broadcasted_iota(jnp.int32, (8, 2 * ha), 1)
@@ -417,12 +455,17 @@
             mixed[rows, head] = dot_nn(p.astype(bf16), vb[rows, head]).astype(bf16)
 
     loop(TP, attend)
+    w_forward(1)
     w_ready(1)
 
     def attn_chunk(i):
         acc[...] = dot_nn(mixed[...], wo[:, mul_of(i, CW)])
 
-    rs(0, abuf, attn_chunk)
+    def attn_between(i):
+        if i == 2:
+            w_forward(GU0)
+
+    rs(0, abuf, attn_chunk, attn_between)
 
     BL = 16
 
@@ -436,18 +479,48 @@
         rall[mine, :] = res.astype(bf16)
 
     loop(L // BL, residual_rows)
-    w_forward(2)
-    ag(rall, 1)
-    w_forward(3)
-    w_ready(2)
-    w_ready(3)
-
     NT = 256
 
-    def gate_up(n):
+    def turn(i):
+        return ((i // 2 + s) % 2) * 2 + i % 2
+
+    def gate_up(i):
+        chunk = mul_of(turn(i), CW)
+
+        def tile(n):
+            at = mul_of(n, NT)
+            value = dot_nn(rall[:, chunk], wgu[chunk, at])
+            gu[:, at] = value if i == 0 else gu[:, at] + value
+
+        loop(2 * fh // NT, tile)
+
+    ag_start(rall, 1, turn(0))
+    ag_start(rall, 1, turn(1))
+    w_forward(GU0 + 1)
+    ag_fwd(rall, 1, turn(0))
+    ag_start(rall, 1, turn(2))
+    ag_fwd(rall, 1, turn(1))
+    ag_start(rall, 1, turn(3))
+    for k in range(GU0, DN0):
+        local_wait(k)
+    ag_done(rall, 1, turn(0))
+    w_forward(GU0 + 2)
+    gate_up(0)
+    ag_fwd(rall, 1, turn(2))
+    ag_done(rall, 1, turn(1))
+    ag_fwd(rall, 1, turn(3))
+    gate_up(1)
+    ag_done(rall, 1, turn(2))
+    w_forward(GU0 + 3)
+    for k in range(GU0, DN0):
+        share(k).wait_recv()
+    gate_up(2)
+    ag_done(rall, 1, turn(3))
+    gate_up(3)
+    ag_drain(rall, 1)
+
+    def hidden(n):
         g_at, u_at = mul_of(n, NT), part(fh + n * NT, NT)
-        gu[:, g_at] = dot_nn(rall[...], wgu[:, g_at])
-        gu[:, u_at] = dot_nn(rall[...], wgu[:, u_at])
 
         def rows_of(j):
             rows = mul_of(j, 64)
@@ -456,11 +529,10 @@
 
         loop(T // 64, rows_of)
 
-    loop(fh // NT, gate_up)
-    w_forward(4)
-    w_ready(4)
-
+    loop(fh // NT, hidden)
     def down_chunk(i):
+        w_forward(DN0 + i)
+        w_ready(DN0 + i)
         acc[...] = dot_nn(hid[...], wd[:, mul_of(i, CW)])
 
     rs(1, bbuf, down_chunk)
@@ -481,120 +553,183 @@
     loop(L // BL, output_rows)
     put_out = pltpu.make_async_copy(outb, out_h, loc.at[3])
     put_out.start()
-    ag(gdall, 2)
-
     half_q = 3 * ha // 2
 
     def by_cols(left, right, width):
-        def make(row, n, core_):
+        def make(row, n, core_, i):
             return dot_tn(left[:, part(row, n)], right[:, mul_of(core_, width)])
         return make
 
-    def down_grad(row, n, core_):
+    def down_grad(row, n, core_, i):
         start = (row // unit) * 2 * unit + core_ * unit if d.direct else core_ * (fh // 2) + row
-        return dot_tn(hid[:, part(start, n)], gdall[...])
+        return dot_tn(hid[:, part(start, n)], gdall[:, mul_of(i, CW)])
 
     ND, NG2, NQ, NO = range(4)
     sets = (
-        (down_grad, rc_d, rx_d, rh_d, fh // 2, 128, stage_d),
-        (by_cols(rall, gg2, fh), rc_gu, rx_gu, rh_gu, D, 256, stage),
-        (by_cols(xall, gqkv, half_q), rc_q, rx_q, rh_q, D, 256, stage),
-        (by_cols(mixed, gaall, D // 2), rc_o, rx_o, None, ha, 128, stage),
+        (down_grad, rc_d, rx_d, rh_d, fh // 2, 128, 128, CHUNKS, stage_d),
+        (by_cols(rall, gg2, fh), rc_gu, rx_gu, rh_gu, D, 256, 128, 1, stage),
+        (by_cols(xall, gqkv, half_q), rc_q, rx_q, rh_q, D, 256, 256, 1, stage),
+        (by_cols(mixed, gaall, D // 2), rc_o, rx_o, None, ha, 128, 128, 1, stage),
     )
     top = hi // (his // 2)
 
+    def half_of(k):
+        return sets[k][4] // 2
+
     def tiles_of(k):
-        return sets[k][4] // 2 // sets[k][5]
-
-    def tile_row(k, j):
-        tiles, n = tiles_of(k), sets[k][5]
-        if tiles < 2:
+        return half_of(k) // sets[k][5]
+
+    def moves_of(k):
+        return half_of(k) // sets[k][6]
+
+    def place(k, j, n):
+        count = half_of(k) // n
+        if count < 2:
             return j * n
-        return ((j + (1 - top) * (tiles // 2)) % tiles) * n
+        return ((j + (1 - top) * (count // 2)) % count) * n
 
     def whole_row(k, j):
         tiles = tiles_of(k)
         late = j // tiles
-        return (late * s + (1 - late) * (1 - s)) * (sets[k][4] // 2) + tile_row(k, j % tiles)
-
-    def core_copy(k, j, slot):
-        _, buf, _, _, _, n, st = sets[k]
+        return (late * s + (1 - late) * (1 - s)) * half_of(k) + place(k, j % tiles, sets[k][5])
+
+    def cols(k, i):
+        return mul_of(i, CW) if sets[k][7] > 1 else pl.ds(0, sets[k][1].shape[1])
+
+    def core_copy(k, j, i, slot):
+        buf, n, st = sets[k][1], sets[k][5], sets[k][8]
         row = whole_row(k, j)
-        view = st.at[slot, :, 0:buf.shape[1]] if st.shape[1] == n else st.at[slot, 0:n, 0:buf.shape[1]]
-        return send(view, buf.at[part(row, n)], stg_s.at[0 if k == ND else 1, slot], c_r.at[k, row // n], dev_c)
-
-    def give(k):
-        make, buf, _, _, _, n, st = sets[k]
-        slots, w, count = st.shape[0], buf.shape[1], 2 * tiles_of(k)
-
+        w = CW if sets[k][7] > 1 else buf.shape[1]
+        return send(st.at[slot, 0:n, 0:w], buf.at[part(row, n), cols(k, i)], stg_s.at[0 if k == ND else 1, slot],
+                    c_r.at[k, (row // n) * sets[k][7] + i], dev_c)
+
+    def give_down(late, i):
         def tile(j):
-            slot = j % slots
-
-            @pl.when(j >= slots)
+            slot = 4 * (i % 2) + j
+            if i >= 2:
+                core_copy(ND, j, i - 2, slot).wait_send()
+            stage_d[slot] = down_grad(whole_row(ND, j), 128, 1 - core, i).astype(bf16)
+            core_copy(ND, j, i, slot).start()
+
+        n = tiles_of(ND)
+        loop(n * (late + 1), tile, n * late)
+
+    before = {NG2: None, NO: NG2, NQ: NO}
+
+    def give(k, j):
+        make, buf, n = sets[k][0], sets[k][1], sets[k][5]
+        slot = j % 2
+        if before[k] is not None:
+            @pl.when(j < 2)
             def _():
-                core_copy(k, j, slot).wait_send()
-
-            st[slot, 0:n, 0:w] = make(whole_row(k, j), n, 1 - core).astype(bf16)
-            core_copy(k, j, slot).start()
-
-        loop(count, tile)
-        for slot in range(min(slots, count)):
-            core_copy(k, 0, slot).wait_send()
-
-    def x_copy(k, j):
-        _, buf, far, _, rows, n, _ = sets[k]
-        row = tile_row(k, j)
-        return send(buf.at[part((1 - s) * (rows // 2) + row, n)], far.at[part(row, n)], x_s.at[k, j], x_r.at[k, j], dev_x)
-
-    def take(k, late):
-        make, buf, _, _, _, n, _ = sets[k]
-        tiles = tiles_of(k)
-
-        def tile(j):
-            row = whole_row(k, j)
-            core_copy(k, j, 0).wait_recv()
-            buf[part(row, n), :] = (make(row, n, core) + buf[part(row, n), :].astype(f32)).astype(bf16)
-            if not late:
-                x_copy(k, j).start()
-
-        loop(2 * tiles if late else tiles, tile, tiles if late else 0)
-
-    def hi_first(k, j):
-        _, buf, _, back, rows, n, _ = sets[k]
+                core_copy(before[k], j, 0, slot).wait_send()
+
+        if 2 * tiles_of(k) > 2:
+            @pl.when(j >= 2)
+            def _():
+                core_copy(k, j, 0, slot).wait_send()
+
+        stage[slot, 0:n, 0:buf.shape[1]] = make(whole_row(k, j), n, 1 - core, 0).astype(bf16)
+        core_copy(k, j, 0, slot).start()
+
+    def x_copy(k, q):
+        _, buf, far, _, _, _, m, _, _ = sets[k]
+        i, j = q // moves_of(k), q % moves_of(k)
+        row = place(k, j, m)
+        return send(buf.at[part((1 - s) * half_of(k) + row, m), cols(k, i)], far.at[part(row, m), cols(k, i)],
+                    x_s.at[k, q], x_r.at[k, q], dev_x)
+
+    def take(k, j, i=0):
+        make, buf, n, m = sets[k][0], sets[k][1], sets[k][5], sets[k][6]
+        rows, at = part(whole_row(k, j), n), cols(k, i)
+        core_copy(k, j, i, 0).wait_recv()
+        buf[rows, at] = (make(whole_row(k, j), n, core, i) + buf[rows, at].astype(f32)).astype(bf16)
+
+        @pl.when(j < tiles_of(k))
+        def _():
+            for e in range(n // m):
+                x_copy(k, i * moves_of(k) + j * (n // m) + e).start()
+
+    def takes(k, j0, j1, i=0):
+        loop(j1, lambda j: take(k, j, i), j0)
+
+    def gives(k, j0, j1):
+        loop(j1, lambda j: give(k, j), j0)
+
+    def hi_first(k, q):
+        _, buf, _, back, _, _, m, _, _ = sets[k]
+        per = moves_of(k) // 2
+        i, j = q // per, q % per
         other = hi + (his // 2) * (1 - 2 * top)
-        return send(buf.at[part(s * (rows // 2) + tile_row(k, j), n)], back.at[mul_of(j, n)],
-                    h0_s.at[k, j], h0_r.at[k, j], (s, rep(other, t, core)))
-
-    def add_rows(buf, row, far, far_row, n, final=None):
+        return send(buf.at[part(s * half_of(k) + place(k, j, m), m), cols(k, i)], back.at[mul_of(j, m), cols(k, i)],
+                    h0_s.at[k, q], h0_r.at[k, q], (s, rep(other, t, core)))
+
+    edge = tz == top
+    relays = (relay_d, relay_gu, relay_q)
+
+    def relay_in(k, q):
+        _, buf, _, _, _, _, m, _, _ = sets[k]
+        per = moves_of(k) // 2
+        i, j = q // per, q % per
+        return send(buf.at[part(s * half_of(k) + place(k, j, m), m), cols(k, i)], relays[k].at[mul_of(j, m), cols(k, i)],
+                    rl_s.at[k, q], rl_r.at[k, q], dev_z)
+
+    def relay_out(k, q):
+        _, _, _, back, _, _, m, _, _ = sets[k]
+        per = moves_of(k) // 2
+        i, j = q // per, q % per
+        other = hi + (his // 2) * (1 - 2 * top)
+        at = (mul_of(j, m), cols(k, i))
+        return send(relays[k].at[at], back.at[at], rf_s.at[k, q], h0_r.at[k, q], (s, rep(other, t_z, core)))
+
+    def hi_send(k, q):
+        @pl.when(edge)
+        def _():
+            relay_in(k, q).start()
+
+        @pl.when(jnp.logical_not(edge))
+        def _():
+            hi_first(k, q).start()
+
+    def relay(k, q0, q1):
+        @pl.when(jnp.logical_not(edge))
+        def _():
+            def piece(q):
+                relay_in(k, q).wait_recv()
+                relay_out(k, q).start()
+
+            loop(q1, piece, q0)
+
+    def add_rows(buf, row, far, far_row, n, at, final=None):
         step = min(n, 64)
 
         def rows_of(j):
             rows = part(row + j * step, step)
-            total = buf[rows, :].astype(f32) + far[part(far_row + j * step, step), :].astype(f32)
+            ours, theirs_ = buf[rows, at], far[part(far_row + j * step, step), at]
             if final is None:
-                buf[rows, :] = total.astype(bf16)
+                buf[rows, at] = ours + theirs_
             else:
-                final[mul_of(j, step), :] = total
+                final[mul_of(j, step), at] = ours.astype(f32) + theirs_.astype(f32)
 
         loop(n // step, rows_of)
 
-    def x_add(k, j0, j1):
-        _, buf, far, _, rows, n, _ = sets[k]
-        tiles = tiles_of(k)
-
-        def tile(j):
-            row = tile_row(k, j)
-            x_copy(k, j).wait_recv()
-            add_rows(buf, s * (rows // 2) + row, far, row, n)
+    def x_add(k, q0, q1):
+        _, buf, far, _, _, _, m, _, _ = sets[k]
+
+        def piece(q):
+            i, j = q // moves_of(k), q % moves_of(k)
+            row = place(k, j, m)
+            x_copy(k, q).wait_recv()
+            add_rows(buf, s * half_of(k) + row, far, row, m, cols(k, i))
             if k != NO:
-                @pl.when(j < tiles // 2)
+                @pl.when(j < moves_of(k) // 2)
                 def _():
-                    hi_first(k, j).start()
-
-        loop(j1, tile, j0)
+                    hi_send(k, i * (moves_of(k) // 2) + j)
+
+        loop(q1, piece, q0)
 
     def hi_later(k):
-        half = sets[k][4] // 2
+        half = half_of(k)
         base, size, at, out = top * (half // 2), half // 2, half // 2, []
         for level in range(1, d.levels):
             size //= 2
@@ -607,66 +742,78 @@
 
     def hi_copy(k, step):
         level, far_row, _, size, at, other = step
-        half = sets[k][4] // 2
-        return send(sets[k][1].at[part(s * half + far_row, size)], sets[k][3].at[pl.ds(at, size)],
+        return send(sets[k][1].at[part(s * half_of(k) + far_row, size)], sets[k][3].at[pl.ds(at, size)],
                     h_s.at[k, level], h_r.at[k, level], (s, rep(other, t, core)))
 
     def hi_finish(k, final=None):
-        _, buf, _, back, rows, n, _ = sets[k]
-        tiles, half = tiles_of(k), rows // 2
+        _, buf, _, back, _, _, m, chunks, _ = sets[k]
+        per = moves_of(k) // 2
         last = final if d.levels == 1 else None
 
-        def tile(j):
-            hi_first(k, j).wait_recv()
-            add_rows(buf, s * half + tile_row(k, j + tiles // 2), back, j * n, n, last)
-
-        loop(tiles // 2, tile)
+        def piece(q):
+            i, j = q // per, q % per
+            hi_first(k, q).wait_recv()
+            add_rows(buf, s * half_of(k) + place(k, j + per, m), back, j * m, m, cols(k, i), last)
+
+        assert last is None or per == 1
+        loop(per * chunks, piece)
         later = hi_later(k)[0]
         for step in later:
             hi_copy(k, step).start()
             hi_copy(k, step).wait_recv()
-            add_rows(buf, s * half + step[2], back, step[4], step[3], final if step is later[-1] else None)
+            add_rows(buf, s * half_of(k) + step[2], back, step[4], step[3], pl.ds(0, buf.shape[1]),
+                     final if step is later[-1] else None)
 
     me = t * CORES + core
 
-    def keep_parts(k, p, slot_t, slot_core):
-        half = sets[k][4] // 2
-        _, base, _ = hi_later(k)
-        rows = part(s * half + base + p * d.own, d.own)
+    def kept(k, slot):
+        return gg2.at[part(slot * d.own, d.own), pl.ds(0, fh) if k == NG2 else pl.ds(fh, half_q)]
+
+    def keep_start(k):
+        base = hi_later(k)[1]
+
+        def piece(p):
+            src = sets[k][1].at[part(s * half_of(k) + base + p * d.own, d.own)]
+
+            @pl.when(me != p)
+            def _():
+                send(src, kept(k, me), a_s.at[k - 1, p], a_r.at[k - 1, me], (s, rep(hi, p // CORES, p % CORES))).start()
+
+            @pl.when(me == p)
+            def _():
+                pltpu.make_async_copy(src, kept(k, me), a_r.at[k - 1, me]).start()
+
+        loop(TP * CORES, piece)
+
+    def keep_out(k, p):
+        rows = part(p * d.own, d.own)
         if k == NQ:
             for c in range(3):
-                e = slot_core * 3 + c
-                yield (rc_q.at[rows, pl.ds(c * HD, HD)],
-                       qkv_h.at[e // 2, :, part(((e % 2) * TP + slot_t) * HD, HD)])
+                e = (p % CORES) * 3 + c
+                yield (gg2.at[rows, pl.ds(fh + c * HD, HD)],
+                       qkv_h.at[e // 2, :, part(((e % 2) * TP + p // CORES) * HD, HD)])
         elif d.direct:
             w = 2 * unit
             for c in range(d.S * his):
-                yield rc_gu.at[rows, pl.ds(c * w, w)], gu_h.at[slot_core, :, part((c * TP + slot_t) * w, w)]
+                yield gg2.at[rows, pl.ds(c * w, w)], gu_h.at[p % CORES, :, part((c * TP + p // CORES) * w, w)]
         else:
-            yield rc_gu.at[rows], gu_h.at[slot_t * CORES + slot_core]
-
-    def keep_start(k):
+            yield gg2.at[rows, pl.ds(0, fh)], gu_h.at[p]
+
+    def keep_wait(k):
         def piece(p):
+            pltpu.make_async_copy(kept(k, p), kept(k, p), a_r.at[k - 1, p]).wait()
+            for src, dst in keep_out(k, p):
+                pltpu.make_async_copy(src, dst, ko.at[k - 1, p]).start()
+
+        loop(TP * CORES, piece)
+
+    def keep_end(k):
+        def piece(p):
+            pltpu.make_async_copy(kept(k, p), kept(k, p), ko.at[k - 1, p]).wait()
+
             @pl.when(me != p)
             def _():
-                for src, dst in keep_parts(k, p, t, core):
-                    send(src, dst, a_s.at[k - 1, p], a_r.at[k - 1, me], (s, rep(hi, p // CORES, p % CORES))).start()
-
-            @pl.when(me == p)
-            def _():
-                for src, dst in keep_parts(k, p, t, core):
-                    pltpu.make_async_copy(src, dst, a_r.at[k - 1, me]).start()
-
-        loop(TP * CORES, piece)
-
-    def keep_wait(k):
-        def piece(p):
-            whole = sets[k][1].at[pl.ds(0, d.own)]
-            pltpu.make_async_copy(whole, whole, a_r.at[k - 1, p]).wait()
-
-            @pl.when(me != p)
-            def _():
-                send(whole, whole, a_s.at[k - 1, p], a_r.at[k - 1, me], (s, rep(hi, p // CORES, p % CORES))).wait_send()
+                send(kept(k, p), kept(k, p), a_s.at[k - 1, p], a_r.at[k - 1, me], (s, rep(hi, p // CORES, p % CORES))).wait_send()
 
         loop(TP * CORES, piece)
 
@@ -688,37 +835,82 @@
         if n < len(partners):
             gain_copy(n).start()
 
-    give(ND)
-
-    def hidden_back(n):
-        g_at, u_at = mul_of(n, NT), part(fh + n * NT, NT)
-        acc[:, 0:NT] = dot_nt(gdall[...], wd[mul_of(n, NT), :])
-
-        def rows_of(j):
-            rows = mul_of(j, 64)
-            g, u, gh = gu[rows, g_at], gu[rows, u_at], acc[rows, 0:NT]
-            sig = jax.nn.sigmoid(g)
-            gg2[rows, g_at] = (gh * u * sig * (1.0 + g * (1.0 - sig))).astype(bf16)
-            gg2[rows, u_at] = (gh * (g * sig)).astype(bf16)
-
-        loop(T // 64, rows_of)
-
-    loop(fh // NT, hidden_back)
-    take(ND, False)
+    ag_start(gdall, 2, 0)
+    ag_start(gdall, 2, 1)
+    ag_fwd(gdall, 2, 0)
+    ag_start(gdall, 2, 2)
+    ag_fwd(gdall, 2, 1)
+    ag_start(gdall, 2, 3)
+    def grad_hidden(i):
+        chunk = pl.ds(i * CW, CW)
+
+        def tile(n):
+            at = mul_of(n, NT)
+            value = dot_nt(gdall[:, chunk], wd[at, chunk])
+            acc[:, at] = value if i == 0 else acc[:, at] + value
+            value = dot_nt(gdall[:, chunk], wd[part(CW + n * NT, NT), chunk]).reshape(TP, L, NT)
+            k2[:, :, at] = value if i == 0 else k2[:, :, at] + value
+
+        loop(CW // NT, tile)
+
+    for i in range(CHUNKS):
+        ag_done(gdall, 2, i)
+        if i + 2 < CHUNKS:
+            ag_fwd(gdall, 2, i + 2)
+        give_down(0, i)
+        grad_hidden(i)
+        if i:
+            takes(ND, 0, 2, i - 1)
+    ag_drain(gdall, 2)
+
+    def hidden_back(half):
+        step = L // 2
+
+        def tile(n):
+            at = mul_of(n, NT)
+            g_at, u_at = part(half * CW + n * NT, NT), part(fh + half * CW + n * NT, NT)
+
+            def rows_of(j):
+                rows = mul_of(j, step)
+                g, u = gu[rows, g_at], gu[rows, u_at]
+                gh = k2[j // 2, mul_of(j % 2, step), at] if half else acc[rows, at]
+                sig = jax.nn.sigmoid(g)
+                gg2[rows, g_at] = (gh * u * sig * (1.0 + g * (1.0 - sig))).astype(bf16)
+                gg2[rows, u_at] = (gh * (g * sig)).astype(bf16)
+
+            loop(T // step, rows_of)
+
+        loop(CW // NT, tile)
+
+    hidden_back(0)
+    hidden_back(1)
+    takes(ND, 0, 2, CHUNKS - 1)
 
     def res_chunk(i):
         acc[...] = dot_nt(gg2[...], wgu[mul_of(i, CW), :])
 
+    def res_extra(i):
+        give(NG2, i)
+
+        @pl.when(i > 0)
+        def _():
+            take(NG2, i - 1)
+
     def res_between(i):
         if i == 0:
-            give(NG2)
+            take(NG2, 3)
+            give_down(1, 0)
+            give_down(1, 1)
         elif i == 1:
-            take(NG2, False)
+            give_down(1, 2)
+            give_down(1, 3)
         else:
-            take(ND, True)
-            take(NG2, True)
-
-    rs(2, cbuf, res_chunk, res_between)
+            for c in range(CHUNKS):
+                takes(ND, 2, 4, c)
+            x_add(ND, 0, 4)
+            gives(NG2, 4, 8)
+
+    rs(2, cbuf, res_chunk, res_between, res_extra)
 
     def attn_grad_rows(j):
         rows = mul_of(j, BL)
@@ -734,20 +926,9 @@
 
     loop(L // BL, attn_grad_rows)
 
-    def ga_between(i):
-        if i == 1:
-            x_add(ND, 0, 1)
-        if i == 3:
-            x_add(ND, 1, 2)
-
-    ag(gaall, 3, None, ga_between)
-
-    give(NO)
-    acc[:, 0:ha] = dot_nt(gaall[...], wo[...])
-    x_add(NG2, 0, 1)
-
     def attend_back(b):
         rows = blk(b)
+        acc[rows, 0:ha] = dot_nt(gaall[rows, :], wo[...])
         scale = columns(2, b)
         cos, sin = cos_v[...], sin_v[...]
         for h in range(heads):
@@ -767,12 +948,34 @@
                 gsum[:, spot] += jnp.sum(gn * field * scale[which], axis=0, keepdims=True)
                 gu[rows, at] = gn * gain_of(which, h)
 
-    loop(TP, attend_back)
+    for i in range(CHUNKS):
+        ag_start(gaall, 3, i)
+    attend_back(t)
+    ag_fwd(gaall, 3, 0)
+    takes(NG2, 4, 6)
+    ag_fwd(gaall, 3, 1)
+    takes(NG2, 6, 8)
+    ag_fwd(gaall, 3, 2)
+    ag_fwd(gaall, 3, 3)
+    x_add(ND, 4, 8)
+    relay(ND, 0, 2)
+    x_add(NG2, 0, 1)
+    loop(2, lambda j: attend_back(t_y + j * (t_z - t_y)))
+    for i in range(CHUNKS):
+        ag_done(gaall, 3, i)
+    attend_back(t_d)
+    gives(NO, 0, 2)
+    relay(ND, 2, 4)
+    ag_drain(gaall, 3)
 
     def products(rows):
         return gu[rows, 0:2 * ha] * qk[rows, :]
 
-    stat[3] = stat_sum(1, products, lambda: take(NO, False)) / d.att
+    def in_stat():
+        takes(NO, 0, 2)
+        x_add(NG2, 1, 2)
+
+    stat[3] = stat_sum(1, products, in_stat) / d.att
     gain_step(0)
 
     def qk_back(b):
@@ -784,26 +987,40 @@
             gqkv[rows, at] = (sc * gu[rows, at] - qk[rows, at] * (sc**3 * inner[which])).astype(bf16)
 
     loop(TP, qk_back)
-    give(NQ)
     gain_step(1)
 
     def in_chunk(i):
         acc[...] = dot_nt(gqkv[...], wqkv[mul_of(i, CW), :])
 
+    def in_extra(i):
+        give(NQ, i)
+
+        @pl.when(i == 2)
+        def _():
+            x_add(NG2, 2, 3)
+
+        @pl.when(i > 0)
+        def _():
+            take(NQ, i - 1)
+
     def in_between(i):
         if i == 0:
-            take(NQ, False)
-            x_add(NG2, 1, 2)
+            take(NQ, 3)
+            relay(NG2, 0, 2)
+            gives(NQ, 4, 8)
             gain_step(2)
         elif i == 1:
-            take(NQ, True)
-            take(NO, True)
+            takes(NQ, 4, 8)
+            gain_step(3)
         else:
+            x_add(NG2, 3, 8)
+            x_add(NQ, 0, 2)
+            relay(NG2, 2, 3)
             hi_finish(ND, abuf)
             pltpu.make_async_copy(abuf.at[0:unit], down_h, loc.at[4]).start()
-            gain_step(3)
-
-    rs(3, bbuf, in_chunk, in_between)
+            gain_step(4)
+
+    rs(3, bbuf, in_chunk, in_between, in_extra)
 
     def input_rows(j):
         rows = mul_of(j, BL)
@@ -813,37 +1030,39 @@
     put_gin = pltpu.make_async_copy(bbuf, gin_h, loc.at[5])
     put_gin.start()
 
-    gain_step(4)
-    x_add(NG2, 2, 4)
+    relay(NG2, 3, 4)
+    x_add(NQ, 2, 4)
+    relay(NQ, 0, 2)
+    x_add(NO, 0, 1)
+    hi_finish(NG2)
+    keep_start(NG2)
+
+    for p in range(d.pieces):
+        o_pc[p] = rc_o[part(s * HD + p * d.own_o, d.own_o), :]
+    o_slot = hi * CORES + core
+
+    def o_start(p):
+        goal = t * d.pieces + p
+
+        @pl.when(goal != r)
+        def _():
+            send(o_pc.at[p], o_h.at[o_slot], o_s.at[p], o_r.at[o_slot], (s, goal)).start()
+
+        @pl.when(goal == r)
+        def _():
+            pltpu.make_async_copy(o_pc.at[p], o_h.at[o_slot], o_r.at[o_slot]).start()
+
+    loop(d.pieces, o_start)
+    hi_finish(NQ)
+    keep_start(NQ)
     for n in range(5, len(partners) + 1):
         gain_step(n)
     gg_o[...] = gsum[...]
-    x_add(NO, 0, 1)
-
-    for p in range(d.pieces):
-        o_pc[p] = rc_o[part(s * HD + p * d.own_o, d.own_o), :]
-    o_slot = hi * CORES + core
-
-    def o_start(p):
-        goal = t * d.pieces + p
-
-        @pl.when(goal != r)
-        def _():
-            send(o_pc.at[p], o_h.at[o_slot], o_s.at[p], o_r.at[o_slot], (s, goal)).start()
-
-        @pl.when(goal == r)
-        def _():
-            pltpu.make_async_copy(o_pc.at[p], o_h.at[o_slot], o_r.at[o_slot]).start()
-
-    loop(d.pieces, o_start)
-    x_add(NQ, 0, 4)
-    hi_finish(NG2)
-    keep_start(NG2)
-    hi_finish(NQ)
-    keep_start(NQ)
 
     keep_wait(NG2)
     keep_wait(NQ)
+    keep_end(NG2)
+    keep_end(NQ)
 
     def o_wait(q):
         pltpu.make_async_copy(o_pc.at[0], o_pc.at[0], o_r.at[q]).wait()
@@ -862,10 +1081,21 @@
     for k in range(NG):
         cross(k).wait_send()
         share(k).wait_send()
+    for i in range(CHUNKS - 2, CHUNKS):
+        loop(2 * tiles_of(ND), lambda j: core_copy(ND, j, i, 4 * (i % 2) + j).wait_send())
+    for slot in range(2):
+        core_copy(NQ, slot, 0, slot).wait_send()
     for k in range(4):
-        loop(tiles_of(k), lambda j: x_copy(k, j).wait_send())
+        loop(moves_of(k) * sets[k][7], lambda q: x_copy(k, q).wait_send())
     for k in range(3):
-        loop(tiles_of(k) // 2, lambda j: hi_first(k, j).wait_send())
+        @pl.when(edge)
+        def _():
+            loop(moves_of(k) // 2 * sets[k][7], lambda q: relay_in(k, q).wait_send())
+
+        @pl.when(jnp.logical_not(edge))
+        def _():
+            loop(moves_of(k) // 2 * sets[k][7], lambda q: (hi_first(k, q).wait_send(), relay_out(k, q).wait_send()))
+
         for step in hi_later(k)[0]:
             hi_copy(k, step).wait_send()
     put_out.wait()
@@ -915,19 +1145,19 @@
         vm((T, ha), bf16), vm((T, 3 * ha), bf16), vm((4, 8, T), f32), vm((2, 3, 8, T), f32),
         vm((T, 2 * fh), f32), vm((T, fh), bf16), vm((T, 2 * fh), bf16),
         vm((L, D), f32), vm((L, D), f32), vm((L, D), f32), vm((L, D), bf16),
-        vm((T, CW), f32), vm((CHUNKS, 4, L, CW // 2), bf16), vm((CHUNKS, 2, L, CW // 2), bf16),
-        vm((CHUNKS, 4, L, CW // 2), bf16), vm((CHUNKS, 2, L, CW // 2), bf16), vm((CHUNKS, 2, L, CW // 2), f32),
-        vm((2, 128, D), bf16), vm((2, 256, fh), bf16),
+        vm((T, CW), f32), vm((CHUNKS, 2, L, CW), bf16), vm((CHUNKS, L, CW), bf16),
+        vm((CHUNKS, 2, L, CW), bf16), vm((CHUNKS, L, CW), bf16), vm((CHUNKS, L, CW), f32),
+        vm((8, 128, CW), bf16), vm((2, 256, fh), bf16),
         vm((D, fh), bf16), vm((fh // 2, D), bf16), vm((D, 3 * ha // 2), bf16), vm((ha, D // 2), bf16),
         vm((D // 2, fh), bf16), vm((fh // 4, D), bf16), vm((D // 2, 3 * ha // 2), bf16), vm((ha // 2, D // 2), bf16),
         vm((hi_rows(D // 2), fh), bf16), vm((hi_rows(fh // 4), D), bf16), vm((hi_rows(D // 2), 3 * ha // 2), bf16),
         vm((d.pieces, d.own_o, D // 2), bf16),
         vm((1, d.ggs), f32), vm((steps, 1, d.ggs), f32),
         dma((4, CHUNKS, 4)), dma((4, CHUNKS, 4)), dma((4, CHUNKS, 4)), dma((4, CHUNKS, 4)),
-        dma((6,)), dma((6,)), dma((5,)), dma((5,)), dma((5, 2)), dma((6,)), dma((2, 3)), dma((2, 3)),
-        dma((2, 2)), dma((4, 8)), dma((4, 4)), dma((4, 4)), dma((3, 4)), dma((3, 4)),
+        dma((11,)), dma((11,)), dma((10,)), dma((10,)), dma((10, 2)), dma((6,)), dma((2, 3)), dma((2, 3)),
+        dma((2, 8)), dma((4, 16)), dma((4, 8)), dma((4, 8)), dma((3, 4)), dma((3, 4)), dma((3, 4)), dma((3, 4)), dma((3, 4)),
         dma((3, later)), dma((3, later)),
-        dma((2, TP * CORES)), dma((2, TP * CORES)), dma((d.pieces,)), dma((d.his * CORES,)), dma((steps,)), dma((steps,)),
+        dma((2, TP * CORES)), dma((2, TP * CORES)), dma((2, TP * CORES)), dma((d.pieces,)), dma((d.his * CORES,)), dma((steps,)), dma((steps,)),
     ]
     struct = jax.ShapeDtypeStruct
     gu_shape = (2, d.own, d.ff) if d.direct else (TP * CORES, d.own, fh)
@@ -935,16 +1165,19 @@
         functools.partial(kernel, d),
         out_shape=(
             struct((L, D), bf16), struct((L, D), f32), struct(gu_shape, bf16), struct((3, d.own, d.att), bf16),
-            struct((d.unit, D), f32), struct((d.his * CORES, d.own_o, D // 2), bf16), struct((1, d.ggs), f32),
+            struct((d.unit, D), f32), struct((d.his * CORES, d.own_o, D // 2), bf16),
+            struct((fh // 8, D), bf16), struct((D // 4, fh), bf16), struct((D // 4, 3 * ha // 2), bf16),
+            struct((1, d.ggs), f32),
         ),
         in_specs=[any_] * 9 + [vmem] * 3,
-        out_specs=(any_,) * 6 + (vmem,),
+        out_specs=(any_,) * 9 + (vmem,),
         scratch_shapes=scratch,
         compiler_params=pltpu.CompilerParams(
             collective_id=0, has_side_effects=True, vmem_limit_bytes=67043328),
         name="layer",
     )(x_in[0], cotangent[0], w_query, w_key, w_value, w_out, w_gate, w_up, w_down, gain, cos, sin)
-    out, gin, gu, qkv, down, o, gg = results
+    out, gin, gu, qkv, down, o = results[:6]
+    gg = results[-1]
 
     def hidden_out(k):
         if d.direct:

time: 305 us -> 284 us (0.931)
  Pallas kernels: 291 us -> 271 us
    pallas_call x1, Pallas kernels: 291 us -> 271 us  [body(): pl.pallas_call(functools.partial(kernel, d), out_shape=(struct((L, D), bf...]
where the time goes in v4:
time: 284 us
  Pallas kernels  271 us (95%)
  local copies, waits for them, and re-layouts  7.9 us (3%)
  other arithmetic  4.36 us (2%)
    pallas_call x1, Pallas kernels, body(): pl.pallas_call(functools.partial(kernel, d), out_shape=(struct((L, D), bf...  271 us

profile of v4, /device:TPU:0, one launch (start us, length us, event | category | flops | bytes accessed | tf_op | source)
XLA Modules:
  0.0 283.9 jit_solution(10703863696762079494)
XLA Ops:
  0.7 0.7 constant_dynamic-slice_fusion.2
  1.4 0.7 concatenate.14
  2.1 0.7 concatenate.15
  2.8 0.6 maximum_convert_fusion.gain_v
  3.4 271.0 %layer.1 = (bf16[128,2048]{1,0:T(8,128)(2,1)}, f32[128,2048]{1,0:T(8,128)}, bf16[2,64,4096]{2,1,0:T(8,128)(2,1)}, bf16[3,64,1024]{2,1,0:T(8,128)(2,1)}, f32[128,...) custom-call(bf16[128,2048]{1,0:T(8,128)(2,1)} %bitcast.40, ...), custom_call_target="tpu_custom_call" | custom-call | tf_op jit(solution)/shard_map/layer/pallas_call | solution.py:1164
  274.3 0.0 copy-start.3
  274.3 0.0 copy-start.4
  274.3 0.0 copy-start.5
  274.4 0.0 copy-start.2
  274.4 2.8 bitcast_convert_fusion
  277.2 0.0 copy-start.1
  277.2 0.0 copy-done.3
  277.2 0.9 bitcast_convert_fusion.2
  278.1 0.0 copy-done.4
  278.1 0.0 copy-start
  278.1 0.7 copy.35
  278.8 0.0 copy-done.5
  278.9 0.6 fusion
  279.4 0.6 fusion.1
  280.0 0.6 dynamic_slice.25
  280.6 0.6 dynamic_slice.26
  281.2 0.0 copy-done.2
  281.2 0.8 copy.39
  282.0 0.0 copy-done.1
  282.0 1.0 copy.40
  283.0 0.0 copy-done
  283.0 1.0 copy.41
  (5 shorter events, 0.0 us)
Async XLA Ops:
  274.3 2.9 %copy-start.3 = (bf16[3,64,1024]{2,1,0:T(8,128)(2,1)S(1)}, bf16[3,64,1024]{2,1,0:T(8,128)(2,1)}, u32[]{:S(2)}) copy-start(bf16[3,64,1024]{2,1,0:T(8,128)(2,1)} %get-tuple-element.22) | copy-start | bytes 1179652
  274.3 3.8 %copy-start.4 = (bf16[4,32,1024]{2,1,0:T(8,128)(2,1)S(1)}, bf16[4,32,1024]{2,1,0:T(8,128)(2,1)}, u32[]{:S(2)}) copy-start(bf16[4,32,1024]{2,1,0:T(8,128)(2,1)} %get-tuple-element.23) | copy-start | bytes 786436
  274.3 4.5 %copy-start.5 = (f32[1,6144]{1,0:T(1,128)S(1)}, f32[1,6144]{1,0:T(1,128)}, u32[]{:S(2)}) copy-start(f32[1,6144]{1,0:T(1,128)} %get-tuple-element.26) | copy-start | bytes 73732
  274.4 6.8 %copy-start.2 = (bf16[128,2048]{1,0:T(8,128)(2,1)S(1)}, bf16[128,2048]{1,0:T(8,128)(2,1)}, u32[]{:S(2)}) copy-start(bf16[128,2048]{1,0:T(8,128)(2,1)} %get-tuple-element.20) | copy-start | bytes 1572868
  277.2 4.8 %copy-start.1 = (f32[128,2048]{1,0:T(8,128)S(1)}, f32[128,2048]{1,0:T(8,128)}, u32[]{:S(2)}) copy-start(f32[128,2048]{1,0:T(8,128)} %get-tuple-element.21) | copy-start | bytes 3145732
  278.1 4.9 %copy-start = (f32[128,2048]{1,0:T(8,128)S(1)}, f32[128,2048]{1,0:T(8,128)}, u32[]{:S(2)}) copy-start(f32[128,2048]{1,0:T(8,128)} %get-tuple-element.59) | copy-start | bytes 3145732

commit v5 on v4

--- a/solution.py
+++ b/solution.py
@@ -745,7 +745,7 @@
         return send(sets[k][1].at[part(s * half_of(k) + far_row, size)], sets[k][3].at[pl.ds(at, size)],
                     h_s.at[k, level], h_r.at[k, level], (s, rep(other, t, core)))
 
-    def hi_finish(k, final=None):
+    def hi_finish(k, final=None, then=None):
         _, buf, _, back, _, _, m, chunks, _ = sets[k]
         per = moves_of(k) // 2
         last = final if d.levels == 1 else None
@@ -754,6 +754,8 @@
             i, j = q // per, q % per
             hi_first(k, q).wait_recv()
             add_rows(buf, s * half_of(k) + place(k, j + per, m), back, j * m, m, cols(k, i), last)
+            if then is not None and d.levels == 1:
+                loop(m // d.own, lambda e: then(k, q * (m // d.own) + e))
 
         assert last is None or per == 1
         loop(per * chunks, piece)
@@ -769,21 +771,20 @@
     def kept(k, slot):
         return gg2.at[part(slot * d.own, d.own), pl.ds(0, fh) if k == NG2 else pl.ds(fh, half_q)]
 
+    def keep_piece(k, p):
+        base = hi_later(k)[1]
+        src = sets[k][1].at[part(s * half_of(k) + base + p * d.own, d.own)]
+
+        @pl.when(me != p)
+        def _():
+            send(src, kept(k, me), a_s.at[k - 1, p], a_r.at[k - 1, me], (s, rep(hi, p // CORES, p % CORES))).start()
+
+        @pl.when(me == p)
+        def _():
+            pltpu.make_async_copy(src, kept(k, me), a_r.at[k - 1, me]).start()
+
     def keep_start(k):
-        base = hi_later(k)[1]
-
-        def piece(p):
-            src = sets[k][1].at[part(s * half_of(k) + base + p * d.own, d.own)]
-
-            @pl.when(me != p)
-            def _():
-                send(src, kept(k, me), a_s.at[k - 1, p], a_r.at[k - 1, me], (s, rep(hi, p // CORES, p % CORES))).start()
-
-            @pl.when(me == p)
-            def _():
-                pltpu.make_async_copy(src, kept(k, me), a_r.at[k - 1, me]).start()
-
-        loop(TP * CORES, piece)
+        loop(TP * CORES, lambda p: keep_piece(k, p))
 
     def keep_out(k, p):
         rows = part(p * d.own, d.own)
@@ -817,12 +818,11 @@
 
         loop(TP * CORES, piece)
 
-    partners = [dev_c, dev_x]
+    partners = [dev_y, dev_z, dev_c, dev_x]
     for level in range(d.levels):
         weight = his >> (level + 1)
         bit = (hi // weight) % 2
         partners.append((s, rep(hi + weight * (1 - 2 * bit), t, core)))
-    partners += [dev_y, dev_z]
 
     def gain_copy(n):
         return send(gsum, grecv.at[n], gn_s.at[n], gn_r.at[n], partners[n])
@@ -964,6 +964,7 @@
     for i in range(CHUNKS):
         ag_done(gaall, 3, i)
     attend_back(t_d)
+    gain_step(0)
     gives(NO, 0, 2)
     relay(ND, 2, 4)
     ag_drain(gaall, 3)
@@ -973,10 +974,10 @@
 
     def in_stat():
         takes(NO, 0, 2)
-        x_add(NG2, 1, 2)
 
     stat[3] = stat_sum(1, products, in_stat) / d.att
-    gain_step(0)
+    gain_step(1)
+    x_add(NG2, 1, 3)
 
     def qk_back(b):
         rows = blk(b)
@@ -987,7 +988,7 @@
             gqkv[rows, at] = (sc * gu[rows, at] - qk[rows, at] * (sc**3 * inner[which])).astype(bf16)
 
     loop(TP, qk_back)
-    gain_step(1)
+    gain_step(2)
 
     def in_chunk(i):
         acc[...] = dot_nt(gqkv[...], wqkv[mul_of(i, CW), :])
@@ -997,7 +998,7 @@
 
         @pl.when(i == 2)
         def _():
-            x_add(NG2, 2, 3)
+            x_add(NG2, 3, 4)
 
         @pl.when(i > 0)
         def _():
@@ -1008,17 +1009,17 @@
             take(NQ, 3)
             relay(NG2, 0, 2)
             gives(NQ, 4, 8)
-            gain_step(2)
+            gain_step(3)
         elif i == 1:
             takes(NQ, 4, 8)
-            gain_step(3)
+            relay(NG2, 2, 3)
         else:
-            x_add(NG2, 3, 8)
             x_add(NQ, 0, 2)
-            relay(NG2, 2, 3)
+            gain_step(4)
+            relay(NG2, 3, 4)
+            x_add(NG2, 4, 8)
             hi_finish(ND, abuf)
             pltpu.make_async_copy(abuf.at[0:unit], down_h, loc.at[4]).start()
-            gain_step(4)
 
     rs(3, bbuf, in_chunk, in_between, in_extra)
 
@@ -1030,12 +1031,12 @@
     put_gin = pltpu.make_async_copy(bbuf, gin_h, loc.at[5])
     put_gin.start()
 
-    relay(NG2, 3, 4)
     x_add(NQ, 2, 4)
     relay(NQ, 0, 2)
     x_add(NO, 0, 1)
-    hi_finish(NG2)
-    keep_start(NG2)
+    hi_finish(NG2, None, keep_piece)
+    if d.levels > 1:
+        keep_start(NG2)
 
     for p in range(d.pieces):
         o_pc[p] = rc_o[part(s * HD + p * d.own_o, d.own_o), :]

time: 284 us -> 280 us (0.986)
  Pallas kernels: 271 us -> 267 us
    pallas_call x1, Pallas kernels: 271 us -> 267 us  [body(): pl.pallas_call(functools.partial(kernel, d), out_shape=(struct((L, D), bf...]
where the time goes in v5:
time: 280 us
  Pallas kernels  267 us (95%)
  local copies, waits for them, and re-layouts  7.9 us (3%)
  other arithmetic  4.36 us (2%)
    pallas_call x1, Pallas kernels, body(): pl.pallas_call(functools.partial(kernel, d), out_shape=(struct((L, D), bf...  267 us

profile of v5, /device:TPU:0, one launch (start us, length us, event | category | flops | bytes accessed | tf_op | source)
XLA Modules:
  0.0 279.8 jit_solution(2629367537494027303)
XLA Ops:
  0.7 0.7 constant_dynamic-slice_fusion.2
  1.4 0.7 concatenate.14
  2.1 0.7 concatenate.15
  2.8 0.6 maximum_convert_fusion.gain_v
  3.4 266.8 %layer.1 = (bf16[128,2048]{1,0:T(8,128)(2,1)}, f32[128,2048]{1,0:T(8,128)}, bf16[2,64,4096]{2,1,0:T(8,128)(2,1)}, bf16[3,64,1024]{2,1,0:T(8,128)(2,1)}, f32[128,...) custom-call(bf16[128,2048]{1,0:T(8,128)(2,1)} %bitcast.40, ...), custom_call_target="tpu_custom_call" | custom-call | tf_op jit(solution)/shard_map/layer/pallas_call | solution.py:1165
  270.1 0.0 copy-start.3
  270.2 0.0 copy-start.4
  270.2 0.0 copy-start.5
  270.2 0.0 copy-start.2
  270.2 2.8 %bitcast_convert_fusion = (f32[64,4096]{1,0:T(8,128)}, f32[64,4096]{1,0:T(8,128)}) fusion(bf16[2,64,4096]{2,1,0:T(8,128)(2,1)} %get-tuple-element.24), kind=kLoop, calls=%fused_computation | loop fusion | flops 524288 | bytes 3145728 | tf_op jit(solution)/shard_map/convert_element_type | solution.py:1185
  273.0 0.0 copy-start.1
  273.0 0.0 copy-done.3
  273.0 0.9 bitcast_convert_fusion.2
  273.9 0.0 copy-done.4
  273.9 0.0 copy-start
  273.9 0.7 copy.35
  274.7 0.0 copy-done.5
  274.7 0.6 fusion
  275.3 0.6 fusion.1
  275.8 0.6 dynamic_slice.25
  276.4 0.6 dynamic_slice.26
  277.0 0.0 copy-done.2
  277.0 0.8 copy.39
  277.8 0.0 copy-done.1
  277.8 1.0 copy.40
  278.8 0.0 copy-done
  278.8 1.0 copy.41
  (5 shorter events, 0.0 us)
Async XLA Ops:
  270.1 2.9 %copy-start.3 = (bf16[3,64,1024]{2,1,0:T(8,128)(2,1)S(1)}, bf16[3,64,1024]{2,1,0:T(8,128)(2,1)}, u32[]{:S(2)}) copy-start(bf16[3,64,1024]{2,1,0:T(8,128)(2,1)} %get-tuple-element.22) | copy-start | bytes 1179652
  270.2 3.8 %copy-start.4 = (bf16[4,32,1024]{2,1,0:T(8,128)(2,1)S(1)}, bf16[4,32,1024]{2,1,0:T(8,128)(2,1)}, u32[]{:S(2)}) copy-start(bf16[4,32,1024]{2,1,0:T(8,128)(2,1)} %get-tuple-element.23) | copy-start | bytes 786436
  270.2 4.5 %copy-start.5 = (f32[1,6144]{1,0:T(1,128)S(1)}, f32[1,6144]{1,0:T(1,128)}, u32[]{:S(2)}) copy-start(f32[1,6144]{1,0:T(1,128)} %get-tuple-element.26) | copy-start | bytes 73732
  270.2 6.8 %copy-start.2 = (bf16[128,2048]{1,0:T(8,128)(2,1)S(1)}, bf16[128,2048]{1,0:T(8,128)(2,1)}, u32[]{:S(2)}) copy-start(bf16[128,2048]{1,0:T(8,128)(2,1)} %get-tuple-element.20) | copy-start | bytes 1572868
  273.0 4.8 %copy-start.1 = (f32[128,2048]{1,0:T(8,128)S(1)}, f32[128,2048]{1,0:T(8,128)}, u32[]{:S(2)}) copy-start(f32[128,2048]{1,0:T(8,128)} %get-tuple-element.21) | copy-start | bytes 3145732
  273.9 4.9 %copy-start = (f32[128,2048]{1,0:T(8,128)S(1)}, f32[128,2048]{1,0:T(8,128)}, u32[]{:S(2)}) copy-start(f32[128,2048]{1,0:T(8,128)} %get-tuple-element.59) | copy-start | bytes 3145732

commit v6 on v5

--- a/solution.py
+++ b/solution.py
@@ -496,11 +496,11 @@
 
     ag_start(rall, 1, turn(0))
     ag_start(rall, 1, turn(1))
+    ag_start(rall, 1, turn(2))
     w_forward(GU0 + 1)
     ag_fwd(rall, 1, turn(0))
-    ag_start(rall, 1, turn(2))
+    ag_start(rall, 1, turn(3))
     ag_fwd(rall, 1, turn(1))
-    ag_start(rall, 1, turn(3))
     for k in range(GU0, DN0):
         local_wait(k)
     ag_done(rall, 1, turn(0))
@@ -837,10 +837,10 @@
 
     ag_start(gdall, 2, 0)
     ag_start(gdall, 2, 1)
+    ag_start(gdall, 2, 2)
     ag_fwd(gdall, 2, 0)
-    ag_start(gdall, 2, 2)
+    ag_start(gdall, 2, 3)
     ag_fwd(gdall, 2, 1)
-    ag_start(gdall, 2, 3)
     def grad_hidden(i):
         chunk = pl.ds(i * CW, CW)
 

time: 280 us -> 280 us (level)
  no operation moved by 1% of the time
where the time goes in v6:
time: 280 us
  Pallas kernels  267 us (95%)
  local copies, waits for them, and re-layouts  7.9 us (3%)
  other arithmetic  4.36 us (2%)
    pallas_call x1, Pallas kernels, body(): pl.pallas_call(functools.partial(kernel, d), out_shape=(struct((L, D), bf...  267 us

profile of v6, /device:TPU:0, one launch (start us, length us, event | category | flops | bytes accessed | tf_op | source)
XLA Modules:
  0.0 279.8 jit_solution(5939800533483910397)
XLA Ops:
  0.7 0.7 constant_dynamic-slice_fusion.2
  1.4 0.7 concatenate.14
  2.1 0.7 concatenate.15
  2.8 0.6 maximum_convert_fusion.gain_v
  3.4 266.8 %layer.1 = (bf16[128,2048]{1,0:T(8,128)(2,1)}, f32[128,2048]{1,0:T(8,128)}, bf16[2,64,4096]{2,1,0:T(8,128)(2,1)}, bf16[3,64,1024]{2,1,0:T(8,128)(2,1)}, f32[128,...) custom-call(bf16[128,2048]{1,0:T(8,128)(2,1)} %bitcast.40, ...), custom_call_target="tpu_custom_call" | custom-call | tf_op jit(solution)/shard_map/layer/pallas_call | solution.py:1165
  270.2 0.0 copy-start.3
  270.2 0.0 copy-start.4
  270.2 0.0 copy-start.5
  270.2 0.0 copy-start.2
  270.2 2.8 %bitcast_convert_fusion = (f32[64,4096]{1,0:T(8,128)}, f32[64,4096]{1,0:T(8,128)}) fusion(bf16[2,64,4096]{2,1,0:T(8,128)(2,1)} %get-tuple-element.24), kind=kLoop, calls=%fused_computation | loop fusion | flops 524288 | bytes 3145728 | tf_op jit(solution)/shard_map/convert_element_type | solution.py:1185
  273.0 0.0 copy-start.1
  273.0 0.0 copy-done.3
  273.0 0.9 bitcast_convert_fusion.2
  273.9 0.0 copy-done.4
  273.9 0.0 copy-start
  274.0 0.7 copy.35
  274.7 0.0 copy-done.5
  274.7 0.6 fusion
  275.3 0.6 fusion.1
  275.9 0.6 dynamic_slice.25
  276.5 0.6 dynamic_slice.26
  277.1 0.0 copy-done.2
  277.1 0.8 copy.39
  277.8 0.0 copy-done.1
  277.8 1.0 copy.40
  278.8 0.0 copy-done
  278.8 1.0 copy.41
  (5 shorter events, 0.0 us)
Async XLA Ops:
  270.2 2.9 %copy-start.3 = (bf16[3,64,1024]{2,1,0:T(8,128)(2,1)S(1)}, bf16[3,64,1024]{2,1,0:T(8,128)(2,1)}, u32[]{:S(2)}) copy-start(bf16[3,64,1024]{2,1,0:T(8,128)(2,1)} %get-tuple-element.22) | copy-start | bytes 1179652
  270.2 3.8 %copy-start.4 = (bf16[4,32,1024]{2,1,0:T(8,128)(2,1)S(1)}, bf16[4,32,1024]{2,1,0:T(8,128)(2,1)}, u32[]{:S(2)}) copy-start(bf16[4,32,1024]{2,1,0:T(8,128)(2,1)} %get-tuple-element.23) | copy-start | bytes 786436
  270.2 4.5 %copy-start.5 = (f32[1,6144]{1,0:T(1,128)S(1)}, f32[1,6144]{1,0:T(1,128)}, u32[]{:S(2)}) copy-start(f32[1,6144]{1,0:T(1,128)} %get-tuple-element.26) | copy-start | bytes 73732
  270.2 6.8 %copy-start.2 = (bf16[128,2048]{1,0:T(8,128)(2,1)S(1)}, bf16[128,2048]{1,0:T(8,128)(2,1)}, u32[]{:S(2)}) copy-start(bf16[128,2048]{1,0:T(8,128)(2,1)} %get-tuple-element.20) | copy-start | bytes 1572868
  273.0 4.8 %copy-start.1 = (f32[128,2048]{1,0:T(8,128)S(1)}, f32[128,2048]{1,0:T(8,128)}, u32[]{:S(2)}) copy-start(f32[128,2048]{1,0:T(8,128)} %get-tuple-element.21) | copy-start | bytes 3145732
  273.9 4.9 %copy-start = (f32[128,2048]{1,0:T(8,128)S(1)}, f32[128,2048]{1,0:T(8,128)}, u32[]{:S(2)}) copy-start(f32[128,2048]{1,0:T(8,128)} %get-tuple-element.59) | copy-start | bytes 3145732

commit v7 on v5

--- a/solution.py
+++ b/solution.py
@@ -1034,26 +1034,26 @@
     x_add(NQ, 2, 4)
     relay(NQ, 0, 2)
     x_add(NO, 0, 1)
+
+    for p in range(d.pieces):
+        o_pc[p] = rc_o[part(s * HD + p * d.own_o, d.own_o), :]
+    o_slot = hi * CORES + core
+
+    def o_start(p):
+        goal = t * d.pieces + p
+
+        @pl.when(goal != r)
+        def _():
+            send(o_pc.at[p], o_h.at[o_slot], o_s.at[p], o_r.at[o_slot], (s, goal)).start()
+
+        @pl.when(goal == r)
+        def _():
+            pltpu.make_async_copy(o_pc.at[p], o_h.at[o_slot], o_r.at[o_slot]).start()
+
+    loop(d.pieces, o_start)
     hi_finish(NG2, None, keep_piece)
     if d.levels > 1:
         keep_start(NG2)
-
-    for p in range(d.pieces):
-        o_pc[p] = rc_o[part(s * HD + p * d.own_o, d.own_o), :]
-    o_slot = hi * CORES + core
-
-    def o_start(p):
-        goal = t * d.pieces + p
-
-        @pl.when(goal != r)
-        def _():
-            send(o_pc.at[p], o_h.at[o_slot], o_s.at[p], o_r.at[o_slot], (s, goal)).start()
-
-        @pl.when(goal == r)
-        def _():
-            pltpu.make_async_copy(o_pc.at[p], o_h.at[o_slot], o_r.at[o_slot]).start()
-
-    loop(d.pieces, o_start)
     hi_finish(NQ)
     keep_start(NQ)
     for n in range(5, len(partners) + 1):

time: 280 us -> 280 us (level)
  no operation moved by 1% of the time
where the time goes in v7:
time: 280 us
  Pallas kernels  267 us (95%)
  local copies, waits for them, and re-layouts  7.9 us (3%)
  other arithmetic  4.36 us (2%)
    pallas_call x1, Pallas kernels, body(): pl.pallas_call(functools.partial(kernel, d), out_shape=(struct((L, D), bf...  267 us

profile of v7, /device:TPU:0, one launch (start us, length us, event | category | flops | bytes accessed | tf_op | source)
XLA Modules:
  0.0 279.8 jit_solution(12305429664440883869)
XLA Ops:
  0.7 0.7 constant_dynamic-slice_fusion.2
  1.4 0.7 concatenate.14
  2.1 0.7 concatenate.15
  2.8 0.6 maximum_convert_fusion.gain_v
  3.4 266.8 %layer.1 = (bf16[128,2048]{1,0:T(8,128)(2,1)}, f32[128,2048]{1,0:T(8,128)}, bf16[2,64,4096]{2,1,0:T(8,128)(2,1)}, bf16[3,64,1024]{2,1,0:T(8,128)(2,1)}, f32[128,...) custom-call(bf16[128,2048]{1,0:T(8,128)(2,1)} %bitcast.40, ...), custom_call_target="tpu_custom_call" | custom-call | tf_op jit(solution)/shard_map/layer/pallas_call | solution.py:1165
  270.1 0.0 copy-start.3
  270.2 0.0 copy-start.4
  270.2 0.0 copy-start.5
  270.2 0.0 copy-start.2
  270.2 2.8 %bitcast_convert_fusion = (f32[64,4096]{1,0:T(8,128)}, f32[64,4096]{1,0:T(8,128)}) fusion(bf16[2,64,4096]{2,1,0:T(8,128)(2,1)} %get-tuple-element.24), kind=kLoop, calls=%fused_computation | loop fusion | flops 524288 | bytes 3145728 | tf_op jit(solution)/shard_map/convert_element_type | solution.py:1185
  273.0 0.0 copy-start.1
  273.0 0.0 copy-done.3
  273.0 0.9 bitcast_convert_fusion.2
  273.9 0.0 copy-done.4
  273.9 0.0 copy-start
  273.9 0.7 copy.35
  274.7 0.0 copy-done.5
  274.7 0.6 fusion
  275.3 0.6 fusion.1
  275.8 0.6 dynamic_slice.25
  276.4 0.6 dynamic_slice.26
  277.0 0.0 copy-done.2
  277.0 0.8 copy.39
  277.8 0.0 copy-done.1
  277.8 1.0 copy.40
  278.8 0.0 copy-done
  278.8 1.0 copy.41
  (5 shorter events, 0.0 us)
Async XLA Ops:
  270.1 2.9 %copy-start.3 = (bf16[3,64,1024]{2,1,0:T(8,128)(2,1)S(1)}, bf16[3,64,1024]{2,1,0:T(8,128)(2,1)}, u32[]{:S(2)}) copy-start(bf16[3,64,1024]{2,1,0:T(8,128)(2,1)} %get-tuple-element.22) | copy-start | bytes 1179652
  270.2 3.8 %copy-start.4 = (bf16[4,32,1024]{2,1,0:T(8,128)(2,1)S(1)}, bf16[4,32,1024]{2,1,0:T(8,128)(2,1)}, u32[]{:S(2)}) copy-start(bf16[4,32,1024]{2,1,0:T(8,128)(2,1)} %get-tuple-element.23) | copy-start | bytes 786436
  270.2 4.5 %copy-start.5 = (f32[1,6144]{1,0:T(1,128)S(1)}, f32[1,6144]{1,0:T(1,128)}, u32[]{:S(2)}) copy-start(f32[1,6144]{1,0:T(1,128)} %get-tuple-element.26) | copy-start | bytes 73732
  270.2 6.8 %copy-start.2 = (bf16[128,2048]{1,0:T(8,128)(2,1)S(1)}, bf16[128,2048]{1,0:T(8,128)(2,1)}, u32[]{:S(2)}) copy-start(bf16[128,2048]{1,0:T(8,128)(2,1)} %get-tuple-element.20) | copy-start | bytes 1572868
  273.0 4.8 %copy-start.1 = (f32[128,2048]{1,0:T(8,128)S(1)}, f32[128,2048]{1,0:T(8,128)}, u32[]{:S(2)}) copy-start(f32[128,2048]{1,0:T(8,128)} %get-tuple-element.21) | copy-start | bytes 3145732
  273.9 4.9 %copy-start = (f32[128,2048]{1,0:T(8,128)S(1)}, f32[128,2048]{1,0:T(8,128)}, u32[]{:S(2)}) copy-start(f32[128,2048]{1,0:T(8,128)} %get-tuple-element.59) | copy-start | bytes 3145732
